TPU v7x, 128 devices: a whole 4x4x4 slice. The times are simulated.
128 devices in a mesh: gx: 2 (over core), gy: 32 (over z, y, x_hi), gz: 2 (over x_lo).
Axes of the slice: x: 4 (x_hi: 2, x_lo: 2; x = x_hi * 2 + x_lo), y: 4, z: 4, core: 2. Of those that a mesh axis runs over, the one named last changes fastest.
Arguments:
- number_densities: float32 [64, 8, 128, 256], P(None, 'gx', 'gy', 'gz'), may hold values from 0.0125 to 24, as said below
- kinetic_kelvin: float32 [8, 128, 256], P('gx', 'gy', 'gz'), may hold values from 0.5 to 3
- flow_vector: float32 [3, 8, 128, 256], P(None, 'gx', 'gy', 'gz'), may hold values from -1 to 1
- opacity_area: float32 [128, 64], replicated, may hold values from 0.0078125 to 0.078125
- illumination: float32 [6], replicated, may hold values from 0.2 to 1
- arrhenius_coefficient: float32 [128], replicated, may hold values from 0.1 to 1
- arrhenius_barrier: float32 [128], replicated, may hold values from 0.5 to 5
- exothermic_energy: float32 [256], replicated, may hold values from 0.002 to 0.02
- emission_loss: float32 [64], replicated, may hold values from 0.01 to 0.1
- participant_indices: int32 [4, 256], replicated, may hold values from 0 to 63
- demanding_patches: int32 [2, 32, 2, 4], P('gx', 'gy', 'gz'), may hold values from 0 to 16, as said below
Outputs:
- ending_populations: float32 [64, 8, 128, 256], P(None, 'gx', 'gy', 'gz')
- ending_warmth: float32 [8, 128, 256], P('gx', 'gy', 'gz')
Inputs may be any that keep to these rules, and one draw needn't show every extreme that they name: `participant_indices`: stoichiometry names species. `number_densities`: densities are positive. `demanding_patches`: each brick's row holds distinct tile numbers first and 16 in its remaining slots; a brick lists at most 4 tiles and some brick lists exactly 4; the 2 bricks that share their first two brick indices together list exactly 4 tiles.
All inputs are finite; a program needn't handle non-finite values.
Results may differ from a plain program's by a relative error of at most 0.0003.
Values sent between devices are 32-bit elements; how exact they have to be, the bound alone decides.
No kernel may reach another device: no remote copies, remote signals or barrier semaphores. Data moves between devices by JAX's collectives and lax.ppermute only.
A program may use at most 64 MiB of HBM per device.

v0:
```python
import functools

import jax
import jax.numpy as jnp
from jax import lax
from jax.experimental import pallas as pl
from jax.experimental.pallas import tpu as pltpu
from jax.sharding import PartitionSpec as P

KINDS = 64
PHOTON = 128
NSUB = 8
TILES = 16
LANES = 128
MAXD = 4
LOG2E = 1.4426950408889634

F32 = jnp.float32
BF16 = jnp.bfloat16


def split(x):
    hi = x.astype(BF16)
    lo = (x - hi.astype(F32)).astype(BF16)
    return hi, lo


def dot(a, b):
    return jnp.dot(a, b, preferred_element_type=F32)


def totals_kernel(n_ref, v_ref, n2_ref, ty_ref, xpay_ref, zpay_ref):
    tiles = []
    for t in range(TILES):
        a = n_ref[pl.ds(t, KINDS, stride=TILES), :]
        n2_ref[t] = a
        tiles.append(a)
    for q in range(4):
        ty_ref[pl.ds(q * KINDS, KINDS), :] = (tiles[4 * q] + tiles[4 * q + 1]) + (
            tiles[4 * q + 2] + tiles[4 * q + 3]
        )
        xpay_ref[pl.ds(q * KINDS, KINDS), :] = (tiles[q] + tiles[q + 4]) + (
            tiles[q + 8] + tiles[q + 12]
        )
    lane = lax.broadcasted_iota(jnp.int32, (KINDS, LANES), 1)
    tz = jnp.zeros((KINDS, LANES), F32)
    for t in range(TILES):
        tz = jnp.where(lane == t, jnp.sum(tiles[t], axis=1, keepdims=True), tz)
    zpay_ref[pl.ds(0, KINDS), :] = tz
    xpay_ref[pl.ds(256, TILES), :] = v_ref[pl.ds(0, TILES), :]
    zpay_ref[pl.ds(KINDS, TILES), :] = v_ref[pl.ds(2 * TILES, TILES), :]


def chem(n, temp, photo, thermal, loss_light, g2, pg, lt, emission, h):
    hi, lo = split(n)
    gat = dot(g2, jnp.concatenate([hi, lo], axis=0))
    na, nb = gat[128:256], gat[256:384]
    kb = thermal * nb
    ka = thermal * na
    rate = jnp.concatenate([photo * gat[:128], kb * na], axis=0)
    rem = jnp.concatenate([kb, ka], axis=0)
    made = dot(pg, jnp.concatenate(split(rate), axis=0))
    lost = dot(lt, jnp.concatenate(split(rem), axis=0)) + loss_light
    heat = made[64:65] + made[65:66]
    cool = jnp.sum(emission * n, axis=0, keepdims=True)
    new_n = (n + h * made[:64]) / (1.0 + h * lost)
    new_t = (temp + h * heat) / (1.0 + h * cool)
    return new_n, new_t


def thermal_rates(temp, coef, barrier):
    return coef * jnp.exp2(barrier * (1.0 / temp))


def wide(parts):
    return jnp.concatenate(parts, axis=1)


def chemistry_kernel(
    where_ref, light_ref, listed_ref,
    n2_ref, temp_ref, v_ref, xown_ref, xpay_ref, yb_ref, yt_ref, zown_ref, zpay_ref,
    ost_ref, uu_ref, g2_ref, pg_ref, lt_ref, lp_ref, cols_ref, em_ref,
    n_out, temp_out, up_out, dn_out, z_out,
    cz_ref, ph_ref, ll_ref, cur_ref, curt_ref,
):
    gx, gz = where_ref[0], where_ref[1]
    for c in range(4):
        blk = n2_ref[pl.ds(c * 4, 4)].reshape(256, LANES)
        cz_ref[pl.ds(c * 256, 256), :] = dot(wide(split(blk)), uu_ref[...])
    ost = ost_ref[...]
    zsum = zown_ref[pl.ds(0, KINDS), :] + zpay_ref[pl.ds(0, KINDS), :]
    zlow = gz * zpay_ref[pl.ds(0, KINDS), :]
    runx = [gx * xpay_ref[pl.ds(q * KINDS, KINDS), :] for q in range(4)]
    for i in range(4):
        runy = yb_ref[pl.ds(i * KINDS, KINDS), :]
        ysum = yt_ref[pl.ds(i * KINDS, KINDS), :]
        for j in range(4):
            t = i * 4 + j
            n = n2_ref[t]
            half = 0.5 * n
            xl = runx[j] + half
            runx[j] = runx[j] + n
            yl = runy + half
            runy = runy + n
            zl = cz_ref[pl.ds(t * KINDS, KINDS), :] + zlow[:, t : t + 1]
            xsum = xown_ref[pl.ds(j * KINDS, KINDS), :] + xpay_ref[pl.ds(j * KINDS, KINDS), :]
            six = wide([xl, xsum - xl, yl, ysum - yl, zl, zsum[:, t : t + 1] - zl])
            hi, lo = split(six)
            tau = dot(ost, jnp.concatenate([hi, lo, hi], axis=0))
            ph = None
            for d in range(6):
                size = (8.0, 128.0, 256.0)[d // 2]
                part = light_ref[d] * jnp.exp2(tau[:, d * 128 : (d + 1) * 128] * (-LOG2E / size))
                ph = part if d == 0 else ph + part
            ph_ref[t] = ph

    g2, pg, lt, lp = g2_ref[...], pg_ref[...], lt_ref[...], lp_ref[...]
    coef = cols_ref[:, 0:1]
    barrier = cols_ref[:, 1:2]
    em = em_ref[:, 0:1]

    def quiet(c, carry):
        base = c * 4
        for p in range(2):
            a = base + 2 * p
            n = wide([n2_ref[a], n2_ref[a + 1]])
            temp = wide([temp_ref[pl.ds(a, 1), :], temp_ref[pl.ds(a + 1, 1), :]])
            ph = wide([ph_ref[a], ph_ref[a + 1]])
            ll = dot(lp, jnp.concatenate(split(ph), axis=0))
            ll_ref[a] = ll[:, :LANES]
            ll_ref[a + 1] = ll[:, LANES:]
            th = thermal_rates(temp, coef, barrier)
            nn, tt = chem(n, temp, ph, th, ll, g2, pg, lt, em, 1.0)
            n_out[a] = nn[:, :LANES]
            n_out[a + 1] = nn[:, LANES:]
            temp_out[pl.ds(a, 1), :] = tt[:, :LANES]
            temp_out[pl.ds(a + 1, 1), :] = tt[:, LANES:]
        return carry

    lax.fori_loop(0, 4, quiet, 0)

    pick = [jnp.minimum(listed_ref[m], TILES - 1) for m in range(MAXD)]
    for m in range(MAXD):
        cur_ref[m] = n2_ref[pick[m]]
        curt_ref[pl.ds(m, 1), :] = temp_ref[pl.ds(pick[m], 1), :]

    def substep(s, carry):
        for p in range(2):
            a, b = 2 * p, 2 * p + 1
            n = wide([cur_ref[a], cur_ref[b]])
            temp = wide([curt_ref[a : a + 1, :], curt_ref[b : b + 1, :]])
            ph = wide([ph_ref[pick[a]], ph_ref[pick[b]]])
            ll = wide([ll_ref[pick[a]], ll_ref[pick[b]]])
            th = thermal_rates(temp, coef, barrier)
            nn, tt = chem(n, temp, ph, th, ll, g2, pg, lt, em, 1.0 / NSUB)
            cur_ref[a] = nn[:, :LANES]
            cur_ref[b] = nn[:, LANES:]
            curt_ref[a : a + 1, :] = tt[:, :LANES]
            curt_ref[b : b + 1, :] = tt[:, LANES:]
        return carry

    lax.fori_loop(0, NSUB, substep, 0)

    for m in range(MAXD):

        @pl.when(listed_ref[m] < TILES)
        def _():
            n_out[pick[m]] = cur_ref[m]
            temp_out[pl.ds(pick[m], 1), :] = curt_ref[m : m + 1, :]

    lane = lax.broadcasted_iota(jnp.int32, (KINDS, LANES), 1)
    zp = jnp.zeros((KINDS, LANES), F32)
    up_out[pl.ds(512, 8), :] = jnp.zeros((8, LANES), F32)
    dn_out[pl.ds(512, 8), :] = jnp.zeros((8, LANES), F32)
    for i in range(4):
        for j in range(4):
            t = i * 4 + j
            u = n_out[t]
            zp = jnp.where(lane // 4 == t, pltpu.roll(u, 4 * t + 2, 1), zp)
            if j < 2:
                dn_out[pl.ds((j * 4 + i) * KINDS, KINDS), :] = u
            else:
                up_out[pl.ds(((j - 2) * 4 + i) * KINDS, KINDS), :] = u
        up_out[pl.ds(512 + i, 1), :] = v_ref[pl.ds(TILES + i * 4 + 3, 1), :]
        dn_out[pl.ds(512 + i, 1), :] = v_ref[pl.ds(TILES + i * 4, 1), :]
    z_out[...] = zp


def transport_kernel(n_ref, v_ref, hx_ref, xpay_ref, lo_ref, hi_ref, hz_ref, zpay_ref, out_ref):
    lane = lax.broadcasted_iota(jnp.int32, (KINDS, LANES), 1)
    lane1 = lax.broadcasted_iota(jnp.int32, (1, LANES), 1)

    def flux(face, um1, u, up1, up2):
        state = jnp.where(face > 0, 1.5 * u - 0.5 * um1, 1.5 * up1 - 0.5 * up2)
        return face * state

    def x_u(i, j):
        if 0 <= i < 4:
            return n_ref[i * 4 + j]
        return hx_ref[(i % 4) * 4 + j]

    def x_v(i, j):
        if 0 <= i < 4:
            return v_ref[i * 4 + j : i * 4 + j + 1, :]
        r = 256 + (i % 4) * 4 + j
        return xpay_ref[r : r + 1, :]

    def y_u(i, j):
        if j < 0:
            return lo_ref[pl.ds(((j + 2) * 4 + i) * KINDS, KINDS), :]
        if j > 3:
            return hi_ref[pl.ds(((j - 4) * 4 + i) * KINDS, KINDS), :]
        return n_ref[i * 4 + j]

    def y_v(i, j):
        if j < 0:
            return lo_ref[512 + i : 513 + i, :]
        if j > 3:
            return hi_ref[512 + i : 513 + i, :]
        return v_ref[16 + i * 4 + j : 17 + i * 4 + j, :]

    def x_flux(i, j):
        face = 0.5 * (x_v(i, j) + x_v(i + 1, j))
        return flux(face, x_u(i - 1, j), x_u(i, j), x_u(i + 1, j), x_u(i + 2, j))

    def y_flux(i, j):
        face = 0.5 * (y_v(i, j) + y_v(i, j + 1))
        return flux(face, y_u(i, j - 1), y_u(i, j), y_u(i, j + 1), y_u(i, j + 2))

    hz = hz_ref[...]
    xf = [x_flux(-1, j) for j in range(4)]
    for i in range(4):
        yf = y_flux(i, -1)
        for j in range(4):
            t = i * 4 + j
            u = n_ref[t]
            top = x_flux(i, j)
            change = top - xf[j]
            xf[j] = top
            top = y_flux(i, j)
            change = change + (top - yf)
            yf = top
            r = pltpu.roll(hz, (LANES - (4 * t + 2)) % LANES, 1)
            vz = v_ref[32 + t : 33 + t, :]
            pz = zpay_ref[64 + t : 65 + t, :]
            vup = pltpu.roll(jnp.where(lane1 == 0, pz, vz), LANES - 1, 1)
            face = 0.5 * (vz + vup)
            facelow = 0.5 * (pz + pltpu.roll(vz, LANES - 1, 1))
            r1, l1, l2 = (
                pltpu.roll(u, 1, 1), pltpu.roll(u, LANES - 1, 1), pltpu.roll(u, LANES - 2, 1),
            )
            q1, p1, p2 = (
                pltpu.roll(r, 1, 1), pltpu.roll(r, LANES - 1, 1), pltpu.roll(r, LANES - 2, 1),
            )
            fz = flux(
                face,
                jnp.where(lane == 0, q1, r1),
                u,
                jnp.where(lane == LANES - 1, p1, l1),
                jnp.where(lane >= LANES - 2, p2, l2),
            )
            flow = flux(facelow, q1, r, l1, l2)
            below = pltpu.roll(jnp.where(lane == LANES - 1, flow, fz), 1, 1)
            change = change + (fz - below)
            out_ref[pl.ds(t, KINDS, stride=TILES), :] = u - 0.25 * change


def sds(*shape):
    return jax.ShapeDtypeStruct(shape, F32)


VM = pl.BlockSpec(memory_space=pltpu.VMEM)
SM = pl.BlockSpec(memory_space=pltpu.SMEM)


def shards(
    number_densities, kinetic_kelvin, flow_vector, opacity_area, illumination,
    arrhenius_coefficient, arrhenius_barrier, exothermic_energy, emission_loss,
    participant_indices, demanding_patches,
):
    n = number_densities.reshape(KINDS * TILES, LANES)
    v = flow_vector.reshape(3 * TILES, LANES)
    temp = kinetic_kelvin.reshape(TILES, LANES)
    n2, ty, xown, zown = pl.pallas_call(
        totals_kernel,
        out_shape=(sds(TILES, KINDS, LANES), sds(256, LANES), sds(272, LANES), sds(80, LANES)),
        in_specs=[VM, VM],
        out_specs=(VM, VM, VM, VM),
        name="totals",
    )(n, v)

    gx, gy, gz = lax.axis_index("gx"), lax.axis_index("gy"), lax.axis_index("gz")
    size = lax.axis_size("gy")
    gx_size, gz_size = lax.axis_size("gx"), lax.axis_size("gz")
    around = lambda count, by: [(a, (a + by) % count) for a in range(count)]

    first = lax.ppermute(ty, "gy", [(a, a ^ 1) for a in range(size)])
    xpay = lax.ppermute(xown, "gx", around(gx_size, 1))
    zpay = lax.ppermute(zown, "gz", around(gz_size, 1))
    beneath = jnp.where(gy % 2 == 1, first, 0.0)
    total = ty + first
    row = (gy // 2) % 4
    got = [
        lax.ppermute(
            total, "gy", [(a, (a // 8) * 8 + ((a // 2 + k) % 4) * 2 + a % 2) for a in range(size)]
        )
        for k in (1, 2, 3)
    ]
    for k in (1, 2, 3):
        beneath = beneath + jnp.where(row >= k, got[k - 1], 0.0)
        total = total + got[k - 1]
    plane = gy // 8
    got = [lax.ppermute(total, "gy", around(size, 8 * k)) for k in (1, 2, 3)]
    for k in (1, 2, 3):
        beneath = beneath + jnp.where(plane >= k, got[k - 1], 0.0)
        total = total + got[k - 1]

    species = jnp.arange(LANES, dtype=jnp.int32) % KINDS
    taken = jnp.concatenate([participant_indices[0], participant_indices[1, PHOTON:]])
    g2 = (taken[:, None] == species[None, :]).astype(BF16)
    rows = jnp.arange(80, dtype=jnp.int32)[:, None]
    made = (participant_indices[2][None, :] == rows).astype(F32) + (
        participant_indices[3][None, :] == rows
    ).astype(F32)
    exo_hi = lax.reduce_precision(exothermic_energy, 8, 7)
    exo_lo = exothermic_energy - exo_hi
    pg = jnp.where(rows == 64, exo_hi[None, :], jnp.where(rows == 65, exo_lo[None, :], made))
    pg = jnp.concatenate([pg, pg], axis=1).astype(BF16)
    rows = rows[:KINDS]
    lt = jnp.concatenate(
        [participant_indices[0, PHOTON:], participant_indices[1, PHOTON:]]
    )[None, :] == rows
    lt = jnp.concatenate([lt, lt], axis=1).astype(BF16)
    lp = participant_indices[0, :PHOTON][None, :] == rows
    lp = jnp.concatenate([lp, lp], axis=1).astype(BF16)
    op_hi = lax.reduce_precision(opacity_area, 8, 7)
    ost = jnp.concatenate([op_hi, op_hi, opacity_area - op_hi], axis=1).astype(BF16)
    k_in = (jnp.arange(2 * LANES, dtype=jnp.int32) % LANES)[:, None]
    k_out = jnp.arange(LANES, dtype=jnp.int32)[None, :]
    uu = jnp.where(k_in < k_out, 1.0, jnp.where(k_in == k_out, 0.5, 0.0)).astype(BF16)
    cols = jnp.stack([arrhenius_coefficient, arrhenius_barrier * (-LOG2E)], axis=1)

    n_new, temp_new, up, dn, zs = pl.pallas_call(
        chemistry_kernel,
        out_shape=(
            sds(TILES, KINDS, LANES), sds(TILES, LANES), sds(520, LANES), sds(520, LANES),
            sds(KINDS, LANES),
        ),
        in_specs=[SM, SM, SM] + [VM] * 17,
        out_specs=(VM,) * 5,
        scratch_shapes=[
            pltpu.VMEM((TILES * KINDS, LANES), F32),
            pltpu.VMEM((TILES, PHOTON, LANES), F32),
            pltpu.VMEM((TILES, KINDS, LANES), F32),
            pltpu.VMEM((MAXD, KINDS, LANES), F32),
            pltpu.VMEM((8, LANES), F32),
        ],
        name="chemistry",
    )(
        jnp.stack([gx, gz]).astype(F32), illumination, demanding_patches.reshape(MAXD),
        n2, temp, v, xown, xpay, beneath, total, zown, zpay,
        ost, uu, g2, pg, lt, lp, cols, emission_loss[:, None],
    )

    low = lax.ppermute(up, "gy", around(size, 1))
    high = lax.ppermute(dn, "gy", around(size, -1))
    hx = lax.ppermute(n_new, "gx", around(gx_size, 1))
    hz = lax.ppermute(zs, "gz", around(gz_size, 1))

    out = pl.pallas_call(
        transport_kernel,
        out_shape=sds(KINDS * TILES, LANES),
        in_specs=[VM] * 8,
        out_specs=VM,
        name="transport",
    )(n_new, v, hx, xpay, low, high, hz, zpay)
    return out.reshape(KINDS, 4, 4, LANES), temp_new.reshape(4, 4, LANES)


def solution(mesh):
    field = P(None, "gx", "gy", "gz")
    return jax.shard_map(
        shards,
        mesh=mesh,
        in_specs=(field, P("gx", "gy", "gz"), field) + (P(),) * 7 + (P("gx", "gy", "gz", None),),
        out_specs=(field, P("gx", "gy", "gz")),
        check_vma=False,
    )
```

profile of v0, /device:TPU:2, one launch (start us, length us, event | category | flops | bytes accessed | tf_op | source)
XLA Modules:
  0.0 73.4 jit_solution(1813328205359883889)
XLA Ops:
  0.6 2.1 %totals.1 = (f32[16,64,128]{2,1,0:T(8,128)}, f32[256,128]{1,0:T(8,128)}, f32[272,128]{1,0:T(8,128)}, f32[80,128]{1,0:T(8,128)}) custom-call(f32[1024,128]{1,0:T(8,128)} %bitcast.23, f32[48,128]{1,0:T(8,128)} %bitcast.25), custom_call_target="tpu_custom_call" | custom-call | tf_op jit(solution)/shard_map/totals/pallas_call | solution.py:284
  3.2 2.5 %collective-permute-start.1 = (f32[256,128]{1,0:T(8,128)}, f32[256,128]{1,0:T(8,128)S(1)}, u32[]{:S(2)}, u32[]{:S(2)}) collective-permute-start(f32[256,128]{1,0:T(8,128)} %get-tuple-element.13), channel_id=1, source_target_pairs={{0,2},{2,0},{4,6},{6,4},{8,10},{10,8},{12,14},{14,12},{16,18},{18,... | collective-permute-start | bytes 393224 | tf_op jit(solution)/shard_map/ppermute | solution.py:297
  6.5 0.7 copy-done.9
  7.4 0.7 select_convert_fusion.uu_ref
  8.2 0.8 %compare_convert_fusion.g2_ref = bf16[384,128]{1,0:T(8,128)(2,1)} fusion(s32[128]{0:T(128)S(1)} %and_select_fusion, s32[384]{0:T(512)S(1)} %pad_add_fusion), kind=kLoop, calls=%fused_computation.2 | loop fusion | flops 98304 | bytes 100352 | tf_op jit(solution)/shard_map/convert_element_type | solution.py:320
  9.1 0.6 add_convert_fusion.1.lp_ref
  9.7 0.6 add_convert_fusion.lt_ref
  10.3 3.2 %collective-permute-start.4 = (f32[256,128]{1,0:T(8,128)S(1)}, f32[256,128]{1,0:T(8,128)S(1)}, u32[]{:S(2)}, u32[]{:S(2)}) collective-permute-start(f32[256,128]{1,0:T(8,128)S(1)} %add.73), channel_id=1, source_target_pairs={{0,12},{2,14},{4,0},{6,2},{8,4},{10,6},{12,8},{14,10},{16,28},{18,... | collective-permute-start | bytes 393224 | tf_op jit(solution)/shard_map/ppermute | solution.py:304
  13.5 0.6 collective-permute-start.3
  14.2 1.0 %collective-permute-start.2 = (f32[256,128]{1,0:T(8,128)S(1)}, f32[256,128]{1,0:T(8,128)S(1)}, u32[]{:S(2)}, u32[]{:S(2)}) collective-permute-start(f32[256,128]{1,0:T(8,128)S(1)} %add.73), channel_id=1, source_target_pairs={{0,4},{2,6},{4,8},{6,10},{8,12},{10,14},{12,0},{14,2},{16,20},{18,... | collective-permute-start | bytes 393224 | tf_op jit(solution)/shard_map/ppermute | solution.py:304
  15.2 0.7 pad_maximum_fusion.1.ost_ref
  15.9 3.8 %collective-permute-done.4 = f32[256,128]{1,0:T(8,128)S(1)} collective-permute-done((f32[256,128]{1,0:T(8,128)S(1)}, f32[256,128]{1,0:T(8,128)S(1)}, u32[]{:S(2)}, u32[]{:S(2)}) %collective-permute-start.4) | collective-permute-done | bytes 131104 | tf_op jit(solution)/shard_map/ppermute | solution.py:304
  19.6 1.8 %collective-permute-done.3 = f32[256,128]{1,0:T(8,128)S(1)} collective-permute-done((f32[256,128]{1,0:T(8,128)S(1)}, f32[256,128]{1,0:T(8,128)S(1)}, u32[]{:S(2)}, u32[]{:S(2)}) %collective-permute-start.3) | collective-permute-done | bytes 131104 | tf_op jit(solution)/shard_map/ppermute | solution.py:304
  21.5 1.9 %collective-permute-done.2 = f32[256,128]{1,0:T(8,128)S(1)} collective-permute-done((f32[256,128]{1,0:T(8,128)S(1)}, f32[256,128]{1,0:T(8,128)S(1)}, u32[]{:S(2)}, u32[]{:S(2)}) %collective-permute-start.2) | collective-permute-done | bytes 131104 | tf_op jit(solution)/shard_map/ppermute | solution.py:304
  23.4 4.1 %collective-permute-start.7 = (f32[256,128]{1,0:T(8,128)S(1)}, f32[256,128]{1,0:T(8,128)S(1)}, u32[]{:S(2)}, u32[]{:S(2)}) collective-permute-start(f32[256,128]{1,0:T(8,128)S(1)} %add_add_fusion.1), channel_id=1, source_target_pairs={{0,48},{2,50},{4,52},{6,54},{8,56},{10,58},{12,60},{14,62},{16,0},... | collective-permute-start | bytes 393224 | tf_op jit(solution)/shard_map/ppermute | solution.py:313
  27.5 1.3 %collective-permute-start.5 = (f32[256,128]{1,0:T(8,128)S(1)}, f32[256,128]{1,0:T(8,128)S(1)}, u32[]{:S(2)}, u32[]{:S(2)}) collective-permute-start(f32[256,128]{1,0:T(8,128)S(1)} %add_add_fusion.1), channel_id=1, source_target_pairs={{0,16},{2,18},{4,20},{6,22},{8,24},{10,26},{12,28},{14,30},{16,32}... | collective-permute-start | bytes 393224 | tf_op jit(solution)/shard_map/ppermute | solution.py:313
  29.3 0.7 copy-done.10
  29.9 0.7 copy.26.em_ref
  30.6 0.7 copy.25.cols_ref
  31.4 0.6 pad_maximum_fusion.pg_ref
  32.0 1.2 %collective-permute-done.7 = f32[256,128]{1,0:T(8,128)S(1)} collective-permute-done((f32[256,128]{1,0:T(8,128)S(1)}, f32[256,128]{1,0:T(8,128)S(1)}, u32[]{:S(2)}, u32[]{:S(2)}) %collective-permute-start.7) | collective-permute-done | bytes 131104 | tf_op jit(solution)/shard_map/ppermute | solution.py:313
  33.2 2.1 %collective-permute-done.6 = f32[256,128]{1,0:T(8,128)S(1)} collective-permute-done((f32[256,128]{1,0:T(8,128)S(1)}, f32[256,128]{1,0:T(8,128)S(1)}, u32[]{:S(2)}, u32[]{:S(2)}) %collective-permute-start.6) | collective-permute-done | bytes 131104 | tf_op jit(solution)/shard_map/ppermute | solution.py:313
  35.3 1.3 %collective-permute-done.5 = f32[256,128]{1,0:T(8,128)S(1)} collective-permute-done((f32[256,128]{1,0:T(8,128)S(1)}, f32[256,128]{1,0:T(8,128)S(1)}, u32[]{:S(2)}, u32[]{:S(2)}) %collective-permute-start.5) | collective-permute-done | bytes 131104 | tf_op jit(solution)/shard_map/ppermute | solution.py:313
  36.6 0.8 %add_add_fusion = (f32[256,128]{1,0:T(8,128)}, f32[256,128]{1,0:T(8,128)}) fusion(f32[256,128]{1,0:T(8,128)S(1)} %collective-permute-done.7, f32[256,128]{1,0:T(8,128)S(1)} %collective-permute-done.6, f32[256,128]{1,0:T(8,128)S(1)} %add_add_fusion.1, f32[256,128]{1,0:T(8,128)S(1)} %collective-permute-done.5, pred[]{:T(512)S(6)} %ge.23, pred[]{:T(512)S(6)} %ge.22, ...), kind=kLoop, calls=%fused_computation.4 | loop fusion | flops 524288 | bytes 1310727 | tf_op jit(solution)/shard_map/add | solution.py:316
  37.4 0.6 copy-done.4
  38.1 11.9 %chemistry.1 = (f32[16,64,128]{2,1,0:T(8,128)}, f32[16,128]{1,0:T(8,128)}, f32[520,128]{1,0:T(8,128)}, f32[520,128]{1,0:T(8,128)}, f32[64,128]{1,0:T(8,128)}) custom-call(f32[2]{0:T(128)} %add_convert_fusion.2.where_ref, f32[6]{0:T(128)} %light_ref.1, s32[4]{0:T(128)} %bitcast.33, f32[16,64,128]{2,1,0:T(8,128)} %get-tuple-element.11.n2_ref, ...), custom_call_target="tpu_custom_call" | custom-call | tf_op jit(solution)/shard_map/chemistry/pallas_call | solution.py:343
  50.0 0.7 %collective-permute-start.10 = (f32[520,128]{1,0:T(8,128)}, f32[520,128]{1,0:T(8,128)S(1)}, u32[]{:S(2)}, u32[]{:S(2)}) collective-permute-start(f32[520,128]{1,0:T(8,128)} %get-tuple-element.16), channel_id=1, source_target_pairs={{0,2},{2,4},{4,6},{6,8},{8,10},{10,12},{12,14},{14,16},{16,18},{18... | collective-permute-start | bytes 798728 | tf_op jit(solution)/shard_map/ppermute | solution.py:365
  50.8 7.1 %collective-permute-start.11 = (f32[520,128]{1,0:T(8,128)}, f32[520,128]{1,0:T(8,128)S(1)}, u32[]{:S(2)}, u32[]{:S(2)}) collective-permute-start(f32[520,128]{1,0:T(8,128)} %get-tuple-element.17), channel_id=1, source_target_pairs={{0,62},{2,0},{4,2},{6,4},{8,6},{10,8},{12,10},{14,12},{16,14},{18,... | collective-permute-start | bytes 798728 | tf_op jit(solution)/shard_map/ppermute | solution.py:366
  57.9 1.8 %collective-permute-start.12 = (f32[64,128]{1,0:T(8,128)}, f32[64,128]{1,0:T(8,128)S(1)}, u32[]{:S(2)}, u32[]{:S(2)}) collective-permute-start(f32[64,128]{1,0:T(8,128)} %get-tuple-element.18), channel_id=1, source_target_pairs={{0,1},{1,0},{2,3},{3,2},{4,5},{5,4},{6,7},{7,6},{8,9},{9,8},{10,11... | collective-permute-start | bytes 98312 | tf_op jit(solution)/shard_map/ppermute | solution.py:368
  59.6 7.3 %collective-permute-done.12.hz_ref = f32[64,128]{1,0:T(8,128)S(1)} collective-permute-done((f32[64,128]{1,0:T(8,128)}, f32[64,128]{1,0:T(8,128)S(1)}, u32[]{:S(2)}, u32[]{:S(2)}) %collective-permute-start.12) | collective-permute-done | bytes 32800 | tf_op jit(solution)/shard_map/ppermute | solution.py:368
  67.8 0.8 %copy-done.1 = f32[16,64,128]{2,1,0:T(8,128)} copy-done((f32[16,64,128]{2,1,0:T(8,128)}, f32[16,64,128]{2,1,0:T(8,128)S(1)}, u32[]{:S(2)}) %copy-start.1) | copy-done | bytes 524312
  68.6 4.8 %transport.1 = f32[1024,128]{1,0:T(8,128)} custom-call(f32[16,64,128]{2,1,0:T(8,128)} %get-tuple-element.15.n_ref, f32[48,128]{1,0:T(8,128)} %bitcast.27, f32[16,64,128]{2,1,0:T(8,128)} %copy-done.1, f32[272,128]{1,0:T(8,128)} %copy-done, f32[520,128]{1,0:T(8,128)} %copy-done.2, f32[520,128]{1,0:T(8,128)} %copy-done.3, f32[64,128]{1,0:T(8,128)} %copy-done.7, ...), custom_call_target="tpu_custom_call" | custom-call | tf_op jit(solution)/shard_map/transport/pallas_call | solution.py:370
  (54 shorter events, 3.1 us)
Async XLA Ops:
  0.6 5.2 %copy-start.6 = (f32[128,64]{0,1:T(8,128)S(1)}, f32[128,64]{0,1:T(8,128)}, u32[]{:S(2)}) copy-start(f32[128,64]{0,1:T(8,128)} %param.14) | copy-start | bytes 98308
  2.8 34.7 %collective-permute-start.8 = (f32[80,128]{1,0:T(8,128)}, f32[80,128]{1,0:T(8,128)S(1)}, u32[]{:S(2)}, u32[]{:S(2)}) collective-permute-start(f32[80,128]{1,0:T(8,128)} %get-tuple-element.14.zown_ref), channel_id=1, source_target_pairs={{0,1},{1,0},{2,3},{3,2},{4,5},{5,4},{6,7},{7,6},{8,9},{9,8},{10,11... | collective-permute-start | bytes 122888 | tf_op jit(solution)/shard_map/ppermute | solution.py:299
  3.2 2.6 %copy-start.8 = (s32[4,256]{1,0:T(4,128)S(1)}, s32[4,256]{1,0:T(4,128)}, u32[]{:S(2)}) copy-start(s32[4,256]{1,0:T(4,128)} %param.20) | copy-start | bytes 12292
  3.2 7.1 %collective-permute-start.1 = (f32[256,128]{1,0:T(8,128)}, f32[256,128]{1,0:T(8,128)S(1)}, u32[]{:S(2)}, u32[]{:S(2)}) collective-permute-start(f32[256,128]{1,0:T(8,128)} %get-tuple-element.13), channel_id=1, source_target_pairs={{0,2},{2,0},{4,6},{6,4},{8,10},{10,8},{12,14},{14,12},{16,18},{18,... | collective-permute-start | bytes 393224 | tf_op jit(solution)/shard_map/ppermute | solution.py:297
  5.7 31.7 %collective-permute-start = (f32[272,128]{1,0:T(8,128)}, f32[272,128]{1,0:T(8,128)S(1)}, u32[]{:S(2)}, u32[]{:S(2)}) collective-permute-start(f32[272,128]{1,0:T(8,128)} %get-tuple-element.12.xown_ref), channel_id=1, source_target_pairs={{0,64},{64,0},{1,65},{65,1},{2,66},{66,2},{3,67},{67,3},{4,68},{68... | collective-permute-start | bytes 417800 | tf_op jit(solution)/shard_map/ppermute | solution.py:298
  5.8 0.7 copy-start.12
  6.5 0.7 copy-start.9
  8.2 2.1 %copy-start.5 = (f32[256,128]{1,0:T(8,128)S(1)}, f32[256,128]{1,0:T(8,128)}, u32[]{:S(2)}) copy-start(f32[256,128]{1,0:T(8,128)} %get-tuple-element.13) | copy-start | bytes 393220
  10.3 4.8 %copy-start.11 = (f32[128]{0:T(128)S(1)}, f32[128]{0:T(128)}, u32[]{:S(2)}) copy-start(f32[128]{0:T(128)} %param.16) | copy-start | bytes 1540
  10.3 9.3 %collective-permute-start.4 = (f32[256,128]{1,0:T(8,128)S(1)}, f32[256,128]{1,0:T(8,128)S(1)}, u32[]{:S(2)}, u32[]{:S(2)}) collective-permute-start(f32[256,128]{1,0:T(8,128)S(1)} %add.73), channel_id=1, source_target_pairs={{0,12},{2,14},{4,0},{6,2},{8,4},{10,6},{12,8},{14,10},{16,28},{18,... | collective-permute-start | bytes 393224 | tf_op jit(solution)/shard_map/ppermute | solution.py:304
  13.5 7.9 %collective-permute-start.3 = (f32[256,128]{1,0:T(8,128)S(1)}, f32[256,128]{1,0:T(8,128)S(1)}, u32[]{:S(2)}, u32[]{:S(2)}) collective-permute-start(f32[256,128]{1,0:T(8,128)S(1)} %add.73), channel_id=1, source_target_pairs={{0,8},{2,10},{4,12},{6,14},{8,0},{10,2},{12,4},{14,6},{16,24},{18,... | collective-permute-start | bytes 393224 | tf_op jit(solution)/shard_map/ppermute | solution.py:304
  14.2 9.2 %collective-permute-start.2 = (f32[256,128]{1,0:T(8,128)S(1)}, f32[256,128]{1,0:T(8,128)S(1)}, u32[]{:S(2)}, u32[]{:S(2)}) collective-permute-start(f32[256,128]{1,0:T(8,128)S(1)} %add.73), channel_id=1, source_target_pairs={{0,4},{2,6},{4,8},{6,10},{8,12},{10,14},{12,0},{14,2},{16,20},{18,... | collective-permute-start | bytes 393224 | tf_op jit(solution)/shard_map/ppermute | solution.py:304
  23.4 9.9 %collective-permute-start.7 = (f32[256,128]{1,0:T(8,128)S(1)}, f32[256,128]{1,0:T(8,128)S(1)}, u32[]{:S(2)}, u32[]{:S(2)}) collective-permute-start(f32[256,128]{1,0:T(8,128)S(1)} %add_add_fusion.1), channel_id=1, source_target_pairs={{0,48},{2,50},{4,52},{6,54},{8,56},{10,58},{12,60},{14,62},{16,0},... | collective-permute-start | bytes 393224 | tf_op jit(solution)/shard_map/ppermute | solution.py:313
  27.5 7.9 %collective-permute-start.6 = (f32[256,128]{1,0:T(8,128)S(1)}, f32[256,128]{1,0:T(8,128)S(1)}, u32[]{:S(2)}, u32[]{:S(2)}) collective-permute-start(f32[256,128]{1,0:T(8,128)S(1)} %add_add_fusion.1), channel_id=1, source_target_pairs={{0,32},{2,34},{4,36},{6,38},{8,40},{10,42},{12,44},{14,46},{16,48}... | collective-permute-start | bytes 393224 | tf_op jit(solution)/shard_map/ppermute | solution.py:313
  27.5 9.2 %collective-permute-start.5 = (f32[256,128]{1,0:T(8,128)S(1)}, f32[256,128]{1,0:T(8,128)S(1)}, u32[]{:S(2)}, u32[]{:S(2)}) collective-permute-start(f32[256,128]{1,0:T(8,128)S(1)} %add_add_fusion.1), channel_id=1, source_target_pairs={{0,16},{2,18},{4,20},{6,22},{8,24},{10,26},{12,28},{14,30},{16,32}... | collective-permute-start | bytes 393224 | tf_op jit(solution)/shard_map/ppermute | solution.py:313
  29.3 0.7 copy-start.10
  37.4 0.6 copy-start.4
  37.4 0.7 copy-start
  49.9 17.1 %collective-permute-start.9 = (f32[16,64,128]{2,1,0:T(8,128)}, f32[16,64,128]{2,1,0:T(8,128)S(1)}, u32[]{:S(2)}, u32[]{:S(2)}) collective-permute-start(f32[16,64,128]{2,1,0:T(8,128)} %get-tuple-element.15.n_ref), channel_id=1, source_target_pairs={{0,64},{64,0},{1,65},{65,1},{2,66},{66,2},{3,67},{67,3},{4,68},{68... | collective-permute-start | bytes 1572872 | tf_op jit(solution)/shard_map/ppermute | solution.py:367
  50.0 16.9 %collective-permute-start.10 = (f32[520,128]{1,0:T(8,128)}, f32[520,128]{1,0:T(8,128)S(1)}, u32[]{:S(2)}, u32[]{:S(2)}) collective-permute-start(f32[520,128]{1,0:T(8,128)} %get-tuple-element.16), channel_id=1, source_target_pairs={{0,2},{2,4},{4,6},{6,8},{8,10},{10,12},{12,14},{14,16},{16,18},{18... | collective-permute-start | bytes 798728 | tf_op jit(solution)/shard_map/ppermute | solution.py:365
  50.8 16.2 %collective-permute-start.11 = (f32[520,128]{1,0:T(8,128)}, f32[520,128]{1,0:T(8,128)S(1)}, u32[]{:S(2)}, u32[]{:S(2)}) collective-permute-start(f32[520,128]{1,0:T(8,128)} %get-tuple-element.17), channel_id=1, source_target_pairs={{0,62},{2,0},{4,2},{6,4},{8,6},{10,8},{12,10},{14,12},{16,14},{18,... | collective-permute-start | bytes 798728 | tf_op jit(solution)/shard_map/ppermute | solution.py:366
  57.9 9.1 %collective-permute-start.12 = (f32[64,128]{1,0:T(8,128)}, f32[64,128]{1,0:T(8,128)S(1)}, u32[]{:S(2)}, u32[]{:S(2)}) collective-permute-start(f32[64,128]{1,0:T(8,128)} %get-tuple-element.18), channel_id=1, source_target_pairs={{0,1},{1,0},{2,3},{3,2},{4,5},{5,4},{6,7},{7,6},{8,9},{9,8},{10,11... | collective-permute-start | bytes 98312 | tf_op jit(solution)/shard_map/ppermute | solution.py:368
  67.0 0.6 copy-start.7
  67.0 0.7 copy-start.2
  67.0 0.8 %copy-start.3 = (f32[520,128]{1,0:T(8,128)}, f32[520,128]{1,0:T(8,128)S(1)}, u32[]{:S(2)}) copy-start(f32[520,128]{1,0:T(8,128)S(1)} %collective-permute-done.11.hi_ref) | copy-start | bytes 798724
  67.8 0.8 %copy-start.1 = (f32[16,64,128]{2,1,0:T(8,128)}, f32[16,64,128]{2,1,0:T(8,128)S(1)}, u32[]{:S(2)}) copy-start(f32[16,64,128]{2,1,0:T(8,128)S(1)} %collective-permute-done.9.hx_ref) | copy-start | bytes 1572868
where the time goes:
time: 73.7 us; the launch traced here: 73.4 us
  starting transfers between devices  22.8 us (31%)
  waiting for transfers between devices  19.4 us (26%)
  Pallas kernels  18.8 us (26%)
  local copies, waits for them, and re-layouts  5.79 us (8%)
  other arithmetic  5.76 us (8%)
  between operations  0.82 us (1%)
    pallas_call x1, Pallas kernels, shards(): pl.pallas_call(chemistry_kernel, out_shape=(sds(TILES, KINDS, LANES), sds...  11.9 us
    ppermute x3, waiting for transfers between devices, shards(): lax.ppermute(total, 'gy', [(a, a // 8 * 8 + (a // 2 + k) % 4 * 2 + a % 2)...  7.46 us
    ppermute x1, waiting for transfers between devices, shards(): hz = lax.ppermute(zs, 'gz', around(gz_size, 1))  7.33 us
    ppermute x1, starting transfers between devices, shards(): high = lax.ppermute(dn, 'gy', around(size, -1))  7.08 us
    ppermute x3, starting transfers between devices, shards(): got = [lax.ppermute(total, 'gy', around(size, 8 * k)) for k in (1, 2, 3)]  5.37 us
    ppermute x3, starting transfers between devices, shards(): lax.ppermute(total, 'gy', [(a, a // 8 * 8 + (a // 2 + k) % 4 * 2 + a % 2)...  4.82 us
    pallas_call x1, Pallas kernels, shards(): pl.pallas_call(transport_kernel, out_shape=sds(KINDS * TILES, LANES), in_...  4.81 us
    ppermute x3, waiting for transfers between devices, shards(): got = [lax.ppermute(total, 'gy', around(size, 8 * k)) for k in (1, 2, 3)]  4.62 us
  transfers between devices with their start and end apart: 13, of which 7 were waited for; matrix products, arithmetic and copies ran while one was open for 10% of the time, Pallas kernels for 0%

commit v1 on v0

v1 whole, which is shorter than its diff:
```python
import functools

import jax
import jax.numpy as jnp
from jax import lax
from jax.experimental import pallas as pl
from jax.experimental.pallas import tpu as pltpu
from jax.sharding import PartitionSpec as P

KINDS = 64
PHOTON = 128
NSUB = 8
TILES = 16
LANES = 128
MAXD = 4
LOG2E = 1.4426950408889634

F32 = jnp.float32
BF16 = jnp.bfloat16


def split(x):
    hi = x.astype(BF16)
    lo = (x - hi.astype(F32)).astype(BF16)
    return hi, lo


def dot(a, b):
    return jnp.dot(a, b, preferred_element_type=F32)


def totals_kernel(n_ref, v_ref, n2_ref, ty_ref, xpay_ref, zpay_ref):
    tiles = []
    for t in range(TILES):
        a = n_ref[pl.ds(t, KINDS, stride=TILES), :]
        n2_ref[t] = a
        tiles.append(a)
    for q in range(4):
        ty_ref[pl.ds(q * KINDS, KINDS), :] = (tiles[4 * q] + tiles[4 * q + 1]) + (
            tiles[4 * q + 2] + tiles[4 * q + 3]
        )
        xpay_ref[pl.ds(q * KINDS, KINDS), :] = (tiles[q] + tiles[q + 4]) + (
            tiles[q + 8] + tiles[q + 12]
        )
    lane = lax.broadcasted_iota(jnp.int32, (KINDS, LANES), 1)
    tz = jnp.zeros((KINDS, LANES), F32)
    for t in range(TILES):
        tz = jnp.where(lane == t, jnp.sum(tiles[t], axis=1, keepdims=True), tz)
    zpay_ref[pl.ds(0, KINDS), :] = tz
    xpay_ref[pl.ds(256, TILES), :] = v_ref[pl.ds(0, TILES), :]
    zpay_ref[pl.ds(KINDS, TILES), :] = v_ref[pl.ds(2 * TILES, TILES), :]


def stacked(x):
    hi, lo = split(x)
    return jnp.concatenate([hi, lo, hi], axis=0)


def local_kernel(
    light_ref, n2_ref, temp_ref, opt_ref, idx_ref, exo_ref, coef_ref, bar_ref, em_ref,
    ost_ref, g2_ref, pg_ref, lt_ref, lp_ref, cb_ref,
    made_ref, lost_ref, heat_ref, den_ref, na_ref, yl_ref, yu_ref, zc_ref,
):
    op_hi, op_lo = split(opt_ref[...])
    op_hi, op_lo = op_hi.astype(F32), op_lo.astype(F32)
    ost = jnp.concatenate([op_hi, op_hi, op_lo], axis=0).T.astype(BF16)
    ost_ref[...] = ost
    a, b = idx_ref[0:1, :], idx_ref[1:2, :]
    c, e = idx_ref[2:3, :], idx_ref[3:4, :]
    taken = wide([a, b[:, PHOTON:]])
    species = lax.broadcasted_iota(jnp.int32, (LANES, 384), 0) % KINDS
    hot = jnp.where(species == taken, 1.0, 0.0).astype(F32)
    g2 = jnp.concatenate([hot[:, q * 128 : (q + 1) * 128].T for q in range(3)], axis=0)
    g2 = g2.astype(BF16)
    g2_ref[...] = g2
    rows = lax.broadcasted_iota(jnp.int32, (80, 256), 0)
    made = jnp.where(rows == c, 1.0, 0.0) + jnp.where(rows == e, 1.0, 0.0)
    exo_hi, exo_lo = split(exo_ref[...])
    made = jnp.where(rows == 64, exo_hi.astype(F32), made)
    made = jnp.where(rows == 65, exo_lo.astype(F32), made)
    pg = wide([made, made]).astype(BF16)
    pg_ref[...] = pg
    rows = lax.broadcasted_iota(jnp.int32, (KINDS, 256), 0)
    lt = jnp.where(rows == wide([a[:, PHOTON:], b[:, PHOTON:]]), 1.0, 0.0)
    lt = wide([lt, lt]).astype(BF16)
    lt_ref[...] = lt
    lp = jnp.where(rows[:, :PHOTON] == a[:, :PHOTON], 1.0, 0.0)
    lp_ref[...] = wide([lp, lp]).astype(BF16)
    coef = jnp.broadcast_to(coef_ref[...], (LANES, LANES)).T
    bar = jnp.broadcast_to(bar_ref[...] * (-LOG2E), (LANES, LANES)).T
    em = jnp.broadcast_to(em_ref[...], (LANES, KINDS)).T
    cb_ref[pl.ds(0, LANES), :] = coef
    cb_ref[pl.ds(LANES, LANES), :] = bar
    cb_ref[pl.ds(2 * LANES, KINDS), :] = em
    k_in = lax.broadcasted_iota(jnp.int32, (2 * LANES, LANES), 0) % LANES
    k_out = lax.broadcasted_iota(jnp.int32, (2 * LANES, LANES), 1)
    uu = jnp.where(k_in < k_out, 1.0, jnp.where(k_in == k_out, 0.5, 0.0)).astype(BF16)
    coef, bar, em = wide([coef, coef]), wide([bar, bar]), wide([em, em])
    pgt = wide([pg[:, 128:256], pg[:, 384:512]])

    def four(i, carry):
        base = i * 4
        blk = n2_ref[pl.ds(base, 4)].reshape(256, LANES)
        zc_ref[pl.ds(i * 256, 256), :] = dot(wide(split(blk)), uu)
        tiles = [n2_ref[base + j] for j in range(4)]
        total = (tiles[0] + tiles[1]) + (tiles[2] + tiles[3])
        run = jnp.zeros_like(total)
        for p in range(2):
            a = base + 2 * p
            cols = []
            for j in (2 * p, 2 * p + 1):
                low = run + 0.5 * tiles[j]
                run = run + tiles[j]
                cols += [low, total - low]
            tau = dot(ost, stacked(wide(cols)))
            for q in range(4):
                part = light_ref[2 + q % 2] * jnp.exp2(
                    tau[:, q * 128 : (q + 1) * 128] * (-LOG2E / 128.0)
                )
                (yl_ref, yu_ref)[q % 2][a + q // 2] = part
            n = wide([tiles[2 * p], tiles[2 * p + 1]])
            temp = wide([temp_ref[pl.ds(a, 1), :], temp_ref[pl.ds(a + 1, 1), :]])
            gat = dot(g2, jnp.concatenate(split(n), axis=0))
            th = coef * jnp.exp2(bar * (1.0 / temp))
            kb = th * gat[256:384]
            ka = th * gat[128:256]
            made = dot(pgt, jnp.concatenate(split(kb * gat[128:256]), axis=0))
            lost = 1.0 + dot(
                lt, jnp.concatenate(split(jnp.concatenate([kb, ka], axis=0)), axis=0)
            )
            heat = made[64:65] + made[65:66]
            den = 1.0 + jnp.sum(em * n, axis=0, keepdims=True)
            for q in range(2):
                cut = slice(q * LANES, (q + 1) * LANES)
                made_ref[a + q] = made[:64, cut]
                lost_ref[a + q] = lost[:, cut]
                na_ref[a + q] = gat[:128, cut]
                heat_ref[pl.ds(a + q, 1), :] = heat[:, cut]
                den_ref[pl.ds(a + q, 1), :] = den[:, cut]
        return carry

    lax.fori_loop(0, 4, four, 0)


def wide(parts):
    return jnp.concatenate(parts, axis=1)


def early_kernel(light_ref, n2_ref, zc_ref, xown_ref, xpay_ref, zown_ref, zpay_ref, ost_ref, pe_ref):
    gx = lax.axis_index("gx").astype(F32)
    gz = lax.axis_index("gz").astype(F32)
    ost = ost_ref[...]
    zsum = zown_ref[pl.ds(0, KINDS), :] + zpay_ref[pl.ds(0, KINDS), :]
    zlow = gz * zpay_ref[pl.ds(0, KINDS), :]
    runx = [gx * xpay_ref[pl.ds(q * KINDS, KINDS), :] for q in range(4)]
    for i in range(4):
        for j in range(4):
            t = i * 4 + j
            n = n2_ref[t]
            xl = runx[j] + 0.5 * n
            runx[j] = runx[j] + n
            zl = zc_ref[pl.ds(t * KINDS, KINDS), :] + zlow[:, t : t + 1]
            xsum = xown_ref[pl.ds(j * KINDS, KINDS), :] + xpay_ref[pl.ds(j * KINDS, KINDS), :]
            tau = dot(ost, stacked(wide([xl, xsum - xl, zl, zsum[:, t : t + 1] - zl])))
            ph = None
            for q in range(4):
                size, d = ((8.0, 0), (8.0, 1), (256.0, 4), (256.0, 5))[q]
                part = light_ref[d] * jnp.exp2(tau[:, q * 128 : (q + 1) * 128] * (-LOG2E / size))
                ph = part if q == 0 else ph + part
            pe_ref[t] = ph


def chemistry_kernel(
    listed_ref,
    n2_ref, temp_ref, v_ref, ty_ref, below_ref, total_ref, last_ref, pe_ref,
    ost_ref, g2_ref, pg_ref, lt_ref, lp_ref, cb_ref,
    made_ref, lost_ref, heat_ref, den_ref, na_ref, yl_ref, yu_ref,
    n_out, temp_out, up_out, dn_out, z_out,
    ph_ref, ll_ref, cur_ref, curt_ref,
):
    upper = jnp.where(lax.axis_index("gy") >= 16, 1.0, 0.0).astype(F32)
    ost = ost_ref[...]
    for i in range(4):
        cut = pl.ds(i * KINDS, KINDS)
        last = last_ref[cut, :]
        below = below_ref[cut, :] + upper * last
        above = (total_ref[cut, :] + last) - below - ty_ref[cut, :]
        far = jnp.exp2(dot(ost, stacked(wide([below, above]))) * (-LOG2E / 128.0))
        for j in range(4):
            t = i * 4 + j
            ph_ref[t] = pe_ref[t] + (yl_ref[t] * far[:, :LANES] + yu_ref[t] * far[:, LANES:])

    lp = lp_ref[...]
    pgp = wide([pg_ref[:, 0:128], pg_ref[:, 256:384]])

    def quiet(c, carry):
        base = c * 4
        for p in range(2):
            a = base + 2 * p
            ph = wide([ph_ref[a], ph_ref[a + 1]])
            ll = dot(lp, jnp.concatenate(split(ph), axis=0))
            na = wide([na_ref[a], na_ref[a + 1]])
            made = dot(pgp, jnp.concatenate(split(ph * na), axis=0))
            heat = made[64:65] + made[65:66]
            for q in range(2):
                cut = slice(q * LANES, (q + 1) * LANES)
                ll_ref[a + q] = ll[:, cut]
                n_out[a + q] = (n2_ref[a + q] + (made_ref[a + q] + made[:64, cut])) / (
                    lost_ref[a + q] + ll[:, cut]
                )
                row = pl.ds(a + q, 1)
                temp_out[row, :] = (temp_ref[row, :] + (heat_ref[row, :] + heat[:, cut])) / (
                    den_ref[row, :]
                )
        return carry

    lax.fori_loop(0, 4, quiet, 0)

    pick = [jnp.minimum(listed_ref[m], TILES - 1) for m in range(MAXD)]
    for m in range(MAXD):
        cur_ref[m] = n2_ref[pick[m]]
        curt_ref[pl.ds(m, 1), :] = temp_ref[pl.ds(pick[m], 1), :]
    g2, pg, lt = g2_ref[...], pg_ref[...], lt_ref[...]
    coef = cb_ref[pl.ds(0, LANES), :]
    bar = cb_ref[pl.ds(LANES, LANES), :]
    em = cb_ref[pl.ds(2 * LANES, KINDS), :]
    coef, bar, em = wide([coef, coef]), wide([bar, bar]), wide([em, em])
    h = 1.0 / NSUB

    def substep(s, carry):
        for p in range(2):
            a, b = 2 * p, 2 * p + 1
            n = wide([cur_ref[a], cur_ref[b]])
            temp = wide([curt_ref[a : a + 1, :], curt_ref[b : b + 1, :]])
            ph = wide([ph_ref[pick[a]], ph_ref[pick[b]]])
            ll = wide([ll_ref[pick[a]], ll_ref[pick[b]]])
            th = coef * jnp.exp2(bar * (1.0 / temp))
            gat = dot(g2, jnp.concatenate(split(n), axis=0))
            kb = th * gat[256:384]
            ka = th * gat[128:256]
            rate = jnp.concatenate([ph * gat[:128], kb * gat[128:256]], axis=0)
            rem = jnp.concatenate([kb, ka], axis=0)
            made = dot(pg, jnp.concatenate(split(rate), axis=0))
            lost = dot(lt, jnp.concatenate(split(rem), axis=0)) + ll
            heat = made[64:65] + made[65:66]
            cool = jnp.sum(em * n, axis=0, keepdims=True)
            nn = (n + h * made[:64]) / (1.0 + h * lost)
            tt = (temp + h * heat) / (1.0 + h * cool)
            cur_ref[a] = nn[:, :LANES]
            cur_ref[b] = nn[:, LANES:]
            curt_ref[a : a + 1, :] = tt[:, :LANES]
            curt_ref[b : b + 1, :] = tt[:, LANES:]
        return carry

    lax.fori_loop(0, NSUB, substep, 0)

    for m in range(MAXD):

        @pl.when(listed_ref[m] < TILES)
        def _():
            n_out[pick[m]] = cur_ref[m]
            temp_out[pl.ds(pick[m], 1), :] = curt_ref[m : m + 1, :]

    lane = lax.broadcasted_iota(jnp.int32, (KINDS, LANES), 1)
    zp = jnp.zeros((KINDS, LANES), F32)
    up_out[pl.ds(512, 8), :] = jnp.zeros((8, LANES), F32)
    dn_out[pl.ds(512, 8), :] = jnp.zeros((8, LANES), F32)
    for i in range(4):
        for j in range(4):
            t = i * 4 + j
            u = n_out[t]
            zp = jnp.where(lane // 8 == t, pltpu.roll(u, (8 * t + 4) % LANES, 1), zp)
            if j < 2:
                dn_out[pl.ds((j * 4 + i) * KINDS, KINDS), :] = u
            else:
                up_out[pl.ds(((j - 2) * 4 + i) * KINDS, KINDS), :] = u
        up_out[pl.ds(512 + i, 1), :] = v_ref[pl.ds(TILES + i * 4 + 3, 1), :]
        dn_out[pl.ds(512 + i, 1), :] = v_ref[pl.ds(TILES + i * 4, 1), :]
    z_out[...] = zp


def flux(face, um1, u, up1, up2):
    state = jnp.where(face > 0, 1.5 * u - 0.5 * um1, 1.5 * up1 - 0.5 * up2)
    return face * state


def inner_kernel(n_ref, v_ref, hx_ref, xpay_ref, acc_ref):
    lane = lax.broadcasted_iota(jnp.int32, (KINDS, LANES), 1)
    edge = jnp.logical_or(lane < 2, lane >= LANES - 2)

    def x_u(i, j):
        if 0 <= i < 4:
            return n_ref[i * 4 + j]
        return hx_ref[(i % 4) * 4 + j]

    def x_v(i, j):
        if 0 <= i < 4:
            return v_ref[i * 4 + j : i * 4 + j + 1, :]
        r = 256 + (i % 4) * 4 + j
        return xpay_ref[r : r + 1, :]

    def x_flux(i, j):
        face = 0.5 * (x_v(i, j) + x_v(i + 1, j))
        return flux(face, x_u(i - 1, j), x_u(i, j), x_u(i + 1, j), x_u(i + 2, j))

    xf = [x_flux(-1, j) for j in range(4)]
    for i in range(4):
        for j in range(4):
            t = i * 4 + j
            u = n_ref[t]
            top = x_flux(i, j)
            change = top - xf[j]
            xf[j] = top
            vz = v_ref[32 + t : 33 + t, :]
            face = 0.5 * (vz + pltpu.roll(vz, LANES - 1, 1))
            fz = flux(
                face,
                pltpu.roll(u, 1, 1),
                u,
                pltpu.roll(u, LANES - 1, 1),
                pltpu.roll(u, LANES - 2, 1),
            )
            change = change + jnp.where(edge, 0.0, fz - pltpu.roll(fz, 1, 1))
            acc_ref[t] = u - 0.25 * change


def outer_kernel(n_ref, acc_ref, v_ref, lo_ref, hi_ref, zs_ref, hz_ref, zpay_ref, out_ref):
    lane = lax.broadcasted_iota(jnp.int32, (KINDS, LANES), 1)
    lane1 = lax.broadcasted_iota(jnp.int32, (1, LANES), 1)
    edge = jnp.logical_or(lane < 2, lane >= LANES - 2)

    vown = jnp.zeros((1, LANES), F32)
    vpart = jnp.zeros((1, LANES), F32)
    for t in range(TILES):
        here = lane1 // 8 == t
        vown = jnp.where(here, pltpu.roll(v_ref[32 + t : 33 + t, :], (8 * t + 4) % LANES, 1), vown)
        vpart = jnp.where(
            here, pltpu.roll(zpay_ref[64 + t : 65 + t, :], (8 * t + 4) % LANES, 1), vpart
        )
    own, part = zs_ref[...], hz_ref[...]
    high = lane % 8 < 4
    high1 = lane1 % 8 < 4
    top, tv = jnp.where(high, own, part), jnp.where(high1, vown, vpart)
    low, lv = jnp.where(high, part, own), jnp.where(high1, vpart, vown)

    def line(u, v):
        face = 0.5 * (v + pltpu.roll(v, LANES - 1, 1))
        f = flux(
            face, pltpu.roll(u, 1, 1), u, pltpu.roll(u, LANES - 1, 1), pltpu.roll(u, LANES - 2, 1)
        )
        return f - pltpu.roll(f, 1, 1)

    packed = jnp.where(high, line(top, tv), line(low, lv))

    def y_u(i, j):
        if j < 0:
            return lo_ref[pl.ds(((j + 2) * 4 + i) * KINDS, KINDS), :]
        if j > 3:
            return hi_ref[pl.ds(((j - 4) * 4 + i) * KINDS, KINDS), :]
        return n_ref[i * 4 + j]

    def y_v(i, j):
        if j < 0:
            return lo_ref[512 + i : 513 + i, :]
        if j > 3:
            return hi_ref[512 + i : 513 + i, :]
        return v_ref[16 + i * 4 + j : 17 + i * 4 + j, :]

    def y_flux(i, j):
        face = 0.5 * (y_v(i, j) + y_v(i, j + 1))
        return flux(face, y_u(i, j - 1), y_u(i, j), y_u(i, j + 1), y_u(i, j + 2))

    for i in range(4):
        yf = y_flux(i, -1)
        for j in range(4):
            t = i * 4 + j
            up = y_flux(i, j)
            zfix = jnp.where(edge, pltpu.roll(packed, (LANES - (8 * t + 4)) % LANES, 1), 0.0)
            out_ref[pl.ds(t, KINDS, stride=TILES), :] = acc_ref[t] - 0.25 * ((up - yf) + zfix)
            yf = up


def hbm(*shape):
    return jax.ShapeDtypeStruct(shape, F32)


def vm(*shape, dtype=F32):
    return pltpu.VMEM(shape, dtype)


VM = pl.BlockSpec(memory_space=pltpu.VMEM)
SM = pl.BlockSpec(memory_space=pltpu.SMEM)


def near(x):
    return pltpu.with_memory_space_constraint(x, pltpu.VMEM)


def call(kernel, name, out_shape, scalars, inputs, scratch=()):
    return pl.pallas_call(
        kernel,
        out_shape=out_shape,
        in_specs=[SM] * len(scalars) + [VM] * len(inputs),
        out_specs=jax.tree.map(lambda _: VM, out_shape),
        scratch_shapes=scratch,
        compiler_params=pltpu.CompilerParams(vmem_limit_bytes=16 * 1024 * 1024),
        name=name,
    )(*scalars, *inputs)


def shards(
    number_densities, kinetic_kelvin, flow_vector, opacity_area, illumination,
    arrhenius_coefficient, arrhenius_barrier, exothermic_energy, emission_loss,
    participant_indices, demanding_patches,
):
    n = number_densities.reshape(KINDS * TILES, LANES)
    v = flow_vector.reshape(3 * TILES, LANES)
    temp = kinetic_kelvin.reshape(TILES, LANES)
    scope = jax.named_scope
    with scope("k_totals"):
        n2, ty, xown, zown = call(
            totals_kernel, "totals",
            (vm(TILES, KINDS, LANES), vm(256, LANES), vm(272, LANES), vm(80, LANES)),
            [], [n, v],
        )

    gy = lax.axis_index("gy")
    size = lax.axis_size("gy")
    around = lambda count, by: [(a, (a + by) % count) for a in range(count)]

    rounds = [
        ("round_x", gy % 2 >= 1, lambda a: a ^ 1),
        ("round_y0", (gy // 2) % 2 >= 1, lambda a: a ^ 2),
        ("round_y1", (gy // 2) % 4 >= 2, lambda a: (a // 8) * 8 + (3 - (a // 2) % 4) * 2 + a % 2),
        ("round_z0", (gy // 8) % 2 >= 1, lambda a: a ^ 8),
        ("round_z1", None, lambda a: (3 - a // 8) * 8 + a % 8),
    ]
    below, total = jnp.zeros_like(ty), ty
    for name, later, to in rounds:
        with scope(name):
            last = lax.ppermute(total, "gy", [(a, to(a)) for a in range(size)])
        if name == "round_x":
            with scope("pay_x"):
                xpay = near(lax.ppermute(xown, "gx", around(lax.axis_size("gx"), 1)))
            with scope("pay_z"):
                zpay = near(lax.ppermute(zown, "gz", around(lax.axis_size("gz"), 1)))
        if later is not None:
            below = below + jnp.where(later, last, 0.0)
            total = total + last
    below, total, last = near(below), near(total), near(last)

    big = (TILES, PHOTON, LANES)
    mid = (TILES, KINDS, LANES)
    with scope("k_local"):
        (ost, g2, pg, lt, lp, cb, made, lost, heat, den, na, yl, yu, zc) = call(
            local_kernel, "local",
            (
                vm(128, 192, dtype=BF16), vm(384, 128, dtype=BF16), vm(80, 512, dtype=BF16),
                vm(64, 512, dtype=BF16), vm(64, 256, dtype=BF16), vm(320, LANES),
                vm(*mid), vm(*mid), vm(TILES, LANES), vm(TILES, LANES), vm(*big), vm(*big),
                vm(*big), vm(TILES * KINDS, LANES),
            ),
            [illumination],
            [
                n2, temp, opacity_area.T, participant_indices, exothermic_energy[None],
                arrhenius_coefficient[None], arrhenius_barrier[None], emission_loss[None],
            ],
        )
    with scope("k_early"):
        pe = call(
            early_kernel, "early", vm(*big), [illumination],
            [n2, zc, xown, xpay, zown, zpay, ost],
        )
    with scope("k_chem"):
        n_new, temp_new, up, dn, zs = call(
            chemistry_kernel, "chemistry",
            (vm(*mid), hbm(TILES, LANES), vm(520, LANES), vm(520, LANES), vm(KINDS, LANES)),
            [demanding_patches.reshape(MAXD)],
            [
                n2, temp, v, ty, below, total, last, pe, ost, g2, pg, lt, lp, cb,
                made, lost, heat, den, na, yl, yu,
            ],
            [
                pltpu.VMEM(big, F32), pltpu.VMEM(mid, F32),
                pltpu.VMEM((MAXD, KINDS, LANES), F32), pltpu.VMEM((8, LANES), F32),
            ],
        )

    with scope("halo_up"):
        low = near(lax.ppermute(up, "gy", around(size, 1)))
    with scope("halo_dn"):
        high = near(lax.ppermute(dn, "gy", around(size, -1)))
    with scope("halo_x"):
        hx = near(lax.ppermute(n_new, "gx", around(lax.axis_size("gx"), 1)))
    with scope("halo_z"):
        hz = near(lax.ppermute(zs, "gz", around(lax.axis_size("gz"), 1)))
    with scope("k_inner"):
        acc = call(inner_kernel, "inner", vm(*mid), [], [n_new, v, hx, xpay])
    with scope("k_outer"):
        out = call(
            outer_kernel, "outer", hbm(KINDS * TILES, LANES), [],
            [n_new, acc, v, low, high, zs, hz, zpay],
        )
    return out.reshape(KINDS, 4, 4, LANES), temp_new.reshape(4, 4, LANES)


def solution(mesh):
    field = P(None, "gx", "gy", "gz")
    return jax.shard_map(
        shards,
        mesh=mesh,
        in_specs=(field, P("gx", "gy", "gz"), field) + (P(),) * 7 + (P("gx", "gy", "gz", None),),
        out_specs=(field, P("gx", "gy", "gz")),
        check_vma=False,
    )
```

time: 73.7 us -> 64.5 us (0.88)
  other arithmetic: 5.76 us -> 0.1 us
  Pallas kernels: 18.8 us -> 15.6 us
  local copies, waits for them, and re-layouts: 5.79 us -> 3.17 us
  waiting for transfers between devices: 19.4 us -> 21 us
    convert_element_type x5 -> x0, other arithmetic: 3.27 us -> none  [the longest x1 0.76 us: shards(): g2 = (taken[:, None] == species[None, :]).astype(BF16)]
    pallas_call x3 -> x6, Pallas kernels: 18.8 us -> 15.6 us  [call(): pl.pallas_call(kernel, out_shape=out_shape, in_specs=[SM] * len(scalars)...]
    ppermute x13 -> x11, waiting for transfers between devices: 19.4 us -> 21 us  [the longest x5 14.2 us: shards(): last = lax.ppermute(total, 'gy', [(a, to(a)) for a in range(size)])]
    concatenate x4 -> x0, other arithmetic: 1.37 us -> none  [the longest x1 0.72 us: shards(): jnp.concatenate([op_hi, op_hi, opacity_area - op_hi], axis=1).astype(BF16)]
    unnamed x27 -> x24, local copies, waits for them, and re-layouts: 4.26 us -> 3.17 us
    ppermute x13 -> x11, starting transfers between devices: 22.8 us -> 22.8 us  [the longest x5 13.1 us: shards(): last = lax.ppermute(total, 'gy', [(a, to(a)) for a in range(size)])]
  transfers between devices with their start and end apart: 13 -> 11, of which waited for: 7 -> 5; matrix products, arithmetic and copies ran while one was open for 10% -> 0% of each run, Pallas kernels for 0% -> 10%
where the time goes in v1:
time: 64.5 us; the launch traced here: 63.5 us
  starting transfers between devices  22.8 us (35%)
  waiting for transfers between devices  21 us (33%)
  Pallas kernels  15.6 us (24%)
  local copies, waits for them, and re-layouts  3.17 us (5%)
  between operations  0.77 us (1%)
    pallas_call x6, Pallas kernels, call(): pl.pallas_call(kernel, out_shape=out_shape, in_specs=[SM] * len(scalars)...  15.6 us
    ppermute x5, waiting for transfers between devices, shards(): last = lax.ppermute(total, 'gy', [(a, to(a)) for a in range(size)])  14.2 us
    ppermute x5, starting transfers between devices, shards(): last = lax.ppermute(total, 'gy', [(a, to(a)) for a in range(size)])  13.1 us
    ppermute x1, waiting for transfers between devices, shards(): hz = near(lax.ppermute(zs, 'gz', around(lax.axis_size('gz'), 1)))  6.77 us
    ppermute x1, starting transfers between devices, shards(): high = near(lax.ppermute(dn, 'gy', around(size, -1)))  5.33 us
    unnamed x24, local copies, waits for them, and re-layouts  3.17 us
    ppermute x1, starting transfers between devices, shards(): low = near(lax.ppermute(up, 'gy', around(size, 1)))  2.42 us
    ppermute x1, starting transfers between devices, shards(): hz = near(lax.ppermute(zs, 'gz', around(lax.axis_size('gz'), 1)))  1.49 us
  transfers between devices with their start and end apart: 11, of which 5 were waited for; matrix products, arithmetic and copies ran while one was open for 0% of the time, Pallas kernels for 10%

profile of v1, /device:TPU:2, one launch (start us, length us, event | category | flops | bytes accessed | tf_op | source)
XLA Modules:
  0.0 63.5 jit_solution(5695613492366214544)
XLA Ops:
  0.6 1.0 %copy-done = f32[64,4,4,128]{3,2,1,0:T(4,128)S(1)} copy-done((f32[64,4,4,128]{3,2,1,0:T(4,128)S(1)}, f32[64,4,4,128]{3,2,1,0:T(4,128)}, u32[]{:S(2)}) %copy-start) | copy-done | bytes 524312
  1.7 0.7 %copy-done.1 = f32[3,4,4,128]{3,2,1,0:T(4,128)S(1)} copy-done((f32[3,4,4,128]{3,2,1,0:T(4,128)S(1)}, f32[3,4,4,128]{3,2,1,0:T(4,128)}, u32[]{:S(2)}) %copy-start.1) | copy-done | bytes 24600
  2.4 0.3 totals.1
  2.7 2.2 %collective-permute-start = (f32[256,128]{1,0:T(8,128)S(1)}, f32[256,128]{1,0:T(8,128)S(1)}, u32[]{:S(2)}, u32[]{:S(2)}) collective-permute-start(f32[256,128]{1,0:T(8,128)S(1)} %get-tuple-element.26.ty_ref), channel_id=1, source_target_pairs={{0,2},{2,0},{4,6},{6,4},{8,10},{10,8},{12,14},{14,12},{16,18},{18,... | collective-permute-start | bytes 393224 | tf_op jit(solution)/shard_map/round_x/ppermute | solution.py:441
  4.9 4.6 %collective-permute-done = f32[256,128]{1,0:T(8,128)S(1)} collective-permute-done((f32[256,128]{1,0:T(8,128)S(1)}, f32[256,128]{1,0:T(8,128)S(1)}, u32[]{:S(2)}, u32[]{:S(2)}) %collective-permute-start) | collective-permute-done | bytes 131104 | tf_op jit(solution)/shard_map/round_x/ppermute | solution.py:441
  9.5 1.7 %collective-permute-start.1 = (f32[256,128]{1,0:T(8,128)S(1)}, f32[256,128]{1,0:T(8,128)S(1)}, u32[]{:S(2)}, u32[]{:S(2)}) collective-permute-start(f32[256,128]{1,0:T(8,128)S(1)} %add.38), channel_id=1, source_target_pairs={{0,4},{2,6},{4,0},{6,2},{8,12},{10,14},{12,8},{14,10},{16,20},{18,... | collective-permute-start | bytes 393224 | tf_op jit(solution)/shard_map/round_y0/ppermute | solution.py:441
  11.2 3.4 %collective-permute-done.1 = f32[256,128]{1,0:T(8,128)S(1)} collective-permute-done((f32[256,128]{1,0:T(8,128)S(1)}, f32[256,128]{1,0:T(8,128)S(1)}, u32[]{:S(2)}, u32[]{:S(2)}) %collective-permute-start.1) | collective-permute-done | bytes 131104 | tf_op jit(solution)/shard_map/round_y0/ppermute | solution.py:441
  14.6 3.1 %collective-permute-start.2 = (f32[256,128]{1,0:T(8,128)S(1)}, f32[256,128]{1,0:T(8,128)S(1)}, u32[]{:S(2)}, u32[]{:S(2)}) collective-permute-start(f32[256,128]{1,0:T(8,128)S(1)} %add.41), channel_id=1, source_target_pairs={{0,12},{2,14},{4,8},{6,10},{8,4},{10,6},{12,0},{14,2},{16,28},{18,... | collective-permute-start | bytes 393224 | tf_op jit(solution)/shard_map/round_y1/ppermute | solution.py:441
  17.7 3.2 %collective-permute-done.2 = f32[256,128]{1,0:T(8,128)S(1)} collective-permute-done((f32[256,128]{1,0:T(8,128)S(1)}, f32[256,128]{1,0:T(8,128)S(1)}, u32[]{:S(2)}, u32[]{:S(2)}) %collective-permute-start.2) | collective-permute-done | bytes 131104 | tf_op jit(solution)/shard_map/round_y1/ppermute | solution.py:441
  20.9 2.0 %collective-permute-start.3 = (f32[256,128]{1,0:T(8,128)S(1)}, f32[256,128]{1,0:T(8,128)S(1)}, u32[]{:S(2)}, u32[]{:S(2)}) collective-permute-start(f32[256,128]{1,0:T(8,128)S(1)} %add.44), channel_id=1, source_target_pairs={{0,16},{2,18},{4,20},{6,22},{8,24},{10,26},{12,28},{14,30},{16,0},... | collective-permute-start | bytes 393224 | tf_op jit(solution)/shard_map/round_z0/ppermute | solution.py:441
  22.9 0.0 collective-permute-start.5
  22.9 3.0 %collective-permute-done.3 = f32[256,128]{1,0:T(8,128)S(1)} collective-permute-done((f32[256,128]{1,0:T(8,128)S(1)}, f32[256,128]{1,0:T(8,128)S(1)}, u32[]{:S(2)}, u32[]{:S(2)}) %collective-permute-start.3) | collective-permute-done | bytes 131104 | tf_op jit(solution)/shard_map/round_z0/ppermute | solution.py:441
  26.0 0.0 copy-start.3
  26.0 4.1 %collective-permute-start.4 = (f32[256,128]{1,0:T(8,128)S(1)}, f32[256,128]{1,0:T(8,128)S(1)}, u32[]{:S(2)}, u32[]{:S(2)}) collective-permute-start(f32[256,128]{1,0:T(8,128)S(1)} %get-tuple-element.48.total_ref), channel_id=1, source_target_pairs={{0,48},{2,50},{4,52},{6,54},{8,56},{10,58},{12,60},{14,62},{16,32}... | collective-permute-start | bytes 393224 | tf_op jit(solution)/shard_map/round_z1/ppermute | solution.py:441
  30.1 0.5 collective-permute-start.6
  30.7 0.6 copy-done.5
  31.3 0.0 copy-done.7
  31.4 3.4 %local.1 = (bf16[128,192]{1,0:T(8,128)(2,1)S(1)}, bf16[384,128]{1,0:T(8,128)(2,1)S(1)}, bf16[80,512]{1,0:T(8,128)(2,1)S(1)}, bf16[64,512]{1,0:T(8,128)(2,1)S(1)}...) custom-call(f32[6]{0:T(128)S(1)} %copy-done.6, ...), custom_call_target="tpu_custom_call" | custom-call | tf_op jit(solution)/shard_map/k_local/local/pallas_call | solution.py:400
  34.8 0.0 collective-permute-done.5.xpay_ref
  34.8 1.6 %early.1.pe_ref = f32[16,128,128]{2,1,0:T(8,128)S(1)} custom-call(f32[6]{0:T(128)S(1)} %copy-done.6, f32[16,64,128]{2,1,0:T(8,128)S(1)} %get-tuple-element.25.n2_ref, f32[1024,128]{1,0:T(8,128)S(1)} %get-tuple-element.27.zc_ref, f32[272,128]{1,0:T(8,128)S(1)} %get-tuple-element.28.xown_ref, f32[272,128]{1,0:T(8,128)S(1)} %collective-permute-done.5.xpay_ref, ...), custom_call_target="tpu_custom_call" | custom-call | tf_op jit(solution)/shard_map/k_early/early/pallas_call | solution.py:400
  36.5 0.0 copy-start.2
  36.5 0.0 collective-permute-done.4.last_ref
  36.5 0.0 copy-start.11
  36.5 0.7 %copy-done.2 = f32[3,4,4,128]{3,2,1,0:T(4,128)S(1)} copy-done((f32[3,4,4,128]{3,2,1,0:T(4,128)S(1)}, f32[3,4,4,128]{3,2,1,0:T(4,128)}, u32[]{:S(2)}) %copy-start.2) | copy-done | bytes 24600
  37.2 7.4 %chemistry.1 = (f32[16,64,128]{2,1,0:T(8,128)S(1)}, f32[16,128]{1,0:T(8,128)}, f32[520,128]{1,0:T(8,128)S(1)}, f32[520,128]{1,0:T(8,128)S(1)}, f32[64,128]{1,0:T(8,128)S(1)}) custom-call(s32[4]{0:T(128)S(1)} %bitcast.23, f32[16,64,128]{2,1,0:T(8,128)S(1)} %get-tuple-element.25.n2_ref, f32[16,128]{1,0:T(8,128)S(1)} %bitcast.17, f32[48,128]{1,0:T(8,128)S(1)} %bitcast.13, ...), custom_call_target="tpu_custom_call" | custom-call | tf_op jit(solution)/shard_map/k_chem/chemistry/pallas_call | solution.py:400
  44.6 0.0 collective-permute-start.7
  44.6 2.4 %collective-permute-start.8 = (f32[520,128]{1,0:T(8,128)S(1)}, f32[520,128]{1,0:T(8,128)S(1)}, u32[]{:S(2)}, u32[]{:S(2)}) collective-permute-start(f32[520,128]{1,0:T(8,128)S(1)} %get-tuple-element.44), channel_id=1, source_target_pairs={{0,2},{2,4},{4,6},{6,8},{8,10},{10,12},{12,14},{14,16},{16,18},{18... | collective-permute-start | bytes 798728 | tf_op jit(solution)/shard_map/halo_up/ppermute | solution.py:490
  47.0 5.3 %collective-permute-start.9 = (f32[520,128]{1,0:T(8,128)S(1)}, f32[520,128]{1,0:T(8,128)S(1)}, u32[]{:S(2)}, u32[]{:S(2)}) collective-permute-start(f32[520,128]{1,0:T(8,128)S(1)} %get-tuple-element.45), channel_id=1, source_target_pairs={{0,62},{2,0},{4,2},{6,4},{8,6},{10,8},{12,10},{14,12},{16,14},{18,... | collective-permute-start | bytes 798728 | tf_op jit(solution)/shard_map/halo_dn/ppermute | solution.py:492
  52.4 1.5 %collective-permute-start.10 = (f32[64,128]{1,0:T(8,128)S(1)}, f32[64,128]{1,0:T(8,128)S(1)}, u32[]{:S(2)}, u32[]{:S(2)}) collective-permute-start(f32[64,128]{1,0:T(8,128)S(1)} %get-tuple-element.46.zs_ref), channel_id=1, source_target_pairs={{0,1},{1,0},{2,3},{3,2},{4,5},{5,4},{6,7},{7,6},{8,9},{9,8},{10,11... | collective-permute-start | bytes 98312 | tf_op jit(solution)/shard_map/halo_z/ppermute | solution.py:496
  53.9 1.4 %inner.1.acc_ref = f32[16,64,128]{2,1,0:T(8,128)S(1)} custom-call(f32[16,64,128]{2,1,0:T(8,128)S(1)} %get-tuple-element.43.n_ref, f32[48,128]{1,0:T(8,128)S(1)} %bitcast.14, f32[16,64,128]{2,1,0:T(8,128)S(1)} %collective-permute-done.7.hx_ref, f32[272,128]{1,0:T(8,128)S(1)} %collective-permute-done.5.xpay_ref), custom_call_target="tpu_custom_call" | custom-call | tf_op jit(solution)/shard_map/k_inner/inner/pallas_call | solution.py:400
  55.3 6.8 %collective-permute-done.10.hz_ref = f32[64,128]{1,0:T(8,128)S(1)} collective-permute-done((f32[64,128]{1,0:T(8,128)S(1)}, f32[64,128]{1,0:T(8,128)S(1)}, u32[]{:S(2)}, u32[]{:S(2)}) %collective-permute-start.10) | collective-permute-done | bytes 32800 | tf_op jit(solution)/shard_map/halo_z/ppermute | solution.py:496
  62.1 1.5 %outer.1 = f32[1024,128]{1,0:T(8,128)} custom-call(f32[16,64,128]{2,1,0:T(8,128)S(1)} %get-tuple-element.43.n_ref, f32[16,64,128]{2,1,0:T(8,128)S(1)} %inner.1.acc_ref, f32[48,128]{1,0:T(8,128)S(1)} %bitcast.15, f32[520,128]{1,0:T(8,128)S(1)} %collective-permute-done.8.lo_ref, f32[520,128]{1,0:T(8,128)S(1)} %collective-permute-done.9.hi_ref, ...), custom_call_target="tpu_custom_call" | custom-call | tf_op jit(solution)/shard_map/k_outer/outer/pallas_call | solution.py:400
  (24 shorter events, 0.1 us)
Async XLA Ops:
  0.6 1.0 %copy-start = (f32[64,4,4,128]{3,2,1,0:T(4,128)S(1)}, f32[64,4,4,128]{3,2,1,0:T(4,128)}, u32[]{:S(2)}) copy-start(f32[64,4,4,128]{3,2,1,0:T(4,128)} %param.11) | copy-start | bytes 1572868
  1.7 0.7 %copy-start.1 = (f32[3,4,4,128]{3,2,1,0:T(4,128)S(1)}, f32[3,4,4,128]{3,2,1,0:T(4,128)}, u32[]{:S(2)}) copy-start(f32[3,4,4,128]{3,2,1,0:T(4,128)} %param.13) | copy-start | bytes 73732
  2.7 6.8 %collective-permute-start = (f32[256,128]{1,0:T(8,128)S(1)}, f32[256,128]{1,0:T(8,128)S(1)}, u32[]{:S(2)}, u32[]{:S(2)}) collective-permute-start(f32[256,128]{1,0:T(8,128)S(1)} %get-tuple-element.26.ty_ref), channel_id=1, source_target_pairs={{0,2},{2,0},{4,6},{6,4},{8,10},{10,8},{12,14},{14,12},{16,18},{18,... | collective-permute-start | bytes 393224 | tf_op jit(solution)/shard_map/round_x/ppermute | solution.py:441
  9.5 5.0 %collective-permute-start.1 = (f32[256,128]{1,0:T(8,128)S(1)}, f32[256,128]{1,0:T(8,128)S(1)}, u32[]{:S(2)}, u32[]{:S(2)}) collective-permute-start(f32[256,128]{1,0:T(8,128)S(1)} %add.38), channel_id=1, source_target_pairs={{0,4},{2,6},{4,0},{6,2},{8,12},{10,14},{12,8},{14,10},{16,20},{18,... | collective-permute-start | bytes 393224 | tf_op jit(solution)/shard_map/round_y0/ppermute | solution.py:441
  14.6 6.3 %collective-permute-start.2 = (f32[256,128]{1,0:T(8,128)S(1)}, f32[256,128]{1,0:T(8,128)S(1)}, u32[]{:S(2)}, u32[]{:S(2)}) collective-permute-start(f32[256,128]{1,0:T(8,128)S(1)} %add.41), channel_id=1, source_target_pairs={{0,12},{2,14},{4,8},{6,10},{8,4},{10,6},{12,0},{14,2},{16,28},{18,... | collective-permute-start | bytes 393224 | tf_op jit(solution)/shard_map/round_y1/ppermute | solution.py:441
  20.9 5.0 %collective-permute-start.3 = (f32[256,128]{1,0:T(8,128)S(1)}, f32[256,128]{1,0:T(8,128)S(1)}, u32[]{:S(2)}, u32[]{:S(2)}) collective-permute-start(f32[256,128]{1,0:T(8,128)S(1)} %add.44), channel_id=1, source_target_pairs={{0,16},{2,18},{4,20},{6,22},{8,24},{10,26},{12,28},{14,30},{16,0},... | collective-permute-start | bytes 393224 | tf_op jit(solution)/shard_map/round_z0/ppermute | solution.py:441
  22.9 11.9 %collective-permute-start.5 = (f32[272,128]{1,0:T(8,128)S(1)}, f32[272,128]{1,0:T(8,128)S(1)}, u32[]{:S(2)}, u32[]{:S(2)}) collective-permute-start(f32[272,128]{1,0:T(8,128)S(1)} %get-tuple-element.28.xown_ref), channel_id=1, source_target_pairs={{0,64},{64,0},{1,65},{65,1},{2,66},{66,2},{3,67},{67,3},{4,68},{68... | collective-permute-start | bytes 417800 | tf_op jit(solution)/shard_map/pay_x/ppermute | solution.py:444
  25.9 4.7 %copy-start.4 = (f32[128,64]{0,1:T(8,128)S(1)}, f32[128,64]{0,1:T(8,128)}, u32[]{:S(2)}) copy-start(f32[128,64]{0,1:T(8,128)} %param.14) | copy-start | bytes 98308
  25.9 4.7 %copy-start.8 = (f32[128]{0:T(128)S(1)}, f32[128]{0:T(128)}, u32[]{:S(2)}) copy-start(f32[128]{0:T(128)} %param.16) | copy-start | bytes 1540
  25.9 4.7 %copy-start.9 = (f32[128]{0:T(128)S(1)}, f32[128]{0:T(128)}, u32[]{:S(2)}) copy-start(f32[128]{0:T(128)} %param.17) | copy-start | bytes 1540
  25.9 4.8 %copy-start.10 = (f32[64]{0:T(128)S(1)}, f32[64]{0:T(128)}, u32[]{:S(2)}) copy-start(f32[64]{0:T(128)} %param.19) | copy-start | bytes 772
  26.0 4.7 %copy-start.3 = (f32[4,4,128]{2,1,0:T(4,128)S(1)}, f32[4,4,128]{2,1,0:T(4,128)}, u32[]{:S(2)}) copy-start(f32[4,4,128]{2,1,0:T(4,128)} %param.12) | copy-start | bytes 24580
  26.0 10.5 %collective-permute-start.4 = (f32[256,128]{1,0:T(8,128)S(1)}, f32[256,128]{1,0:T(8,128)S(1)}, u32[]{:S(2)}, u32[]{:S(2)}) collective-permute-start(f32[256,128]{1,0:T(8,128)S(1)} %get-tuple-element.48.total_ref), channel_id=1, source_target_pairs={{0,48},{2,50},{4,52},{6,54},{8,56},{10,58},{12,60},{14,62},{16,32}... | collective-permute-start | bytes 393224 | tf_op jit(solution)/shard_map/round_z1/ppermute | solution.py:441
  30.1 4.7 %collective-permute-start.6 = (f32[80,128]{1,0:T(8,128)S(1)}, f32[80,128]{1,0:T(8,128)S(1)}, u32[]{:S(2)}, u32[]{:S(2)}) collective-permute-start(f32[80,128]{1,0:T(8,128)S(1)} %get-tuple-element.29.zown_ref), channel_id=1, source_target_pairs={{0,1},{1,0},{2,3},{3,2},{4,5},{5,4},{6,7},{7,6},{8,9},{9,8},{10,11... | collective-permute-start | bytes 122888 | tf_op jit(solution)/shard_map/pay_z/ppermute | solution.py:446
  30.6 0.7 %copy-start.5 = (s32[4,256]{1,0:T(4,128)S(1)}, s32[4,256]{1,0:T(4,128)}, u32[]{:S(2)}) copy-start(s32[4,256]{1,0:T(4,128)} %idx_ref.1) | copy-start | bytes 12292
  30.6 0.7 %copy-start.6 = (f32[6]{0:T(128)S(1)}, f32[6]{0:T(128)}, u32[]{:S(2)}) copy-start(f32[6]{0:T(128)} %light_ref.3) | copy-start | bytes 76
  30.7 0.7 %copy-start.7 = (f32[256]{0:T(256)S(1)}, f32[256]{0:T(256)}, u32[]{:S(2)}) copy-start(f32[256]{0:T(256)} %param.18) | copy-start | bytes 3076
  36.5 0.7 %copy-start.2 = (f32[3,4,4,128]{3,2,1,0:T(4,128)S(1)}, f32[3,4,4,128]{3,2,1,0:T(4,128)}, u32[]{:S(2)}) copy-start(f32[3,4,4,128]{3,2,1,0:T(4,128)} %param.13) | copy-start | bytes 73732
  36.5 0.7 %copy-start.11 = (s32[1,1,1,4]{3,2,1,0:T(1,128)S(1)}, s32[1,1,1,4]{3,2,1,0:T(1,128)}, u32[]{:S(2)}) copy-start(s32[1,1,1,4]{3,2,1,0:T(1,128)} %param.21) | copy-start | bytes 52
  44.6 9.2 %collective-permute-start.7 = (f32[16,64,128]{2,1,0:T(8,128)S(1)}, f32[16,64,128]{2,1,0:T(8,128)S(1)}, u32[]{:S(2)}, u32[]{:S(2)}) collective-permute-start(f32[16,64,128]{2,1,0:T(8,128)S(1)} %get-tuple-element.43.n_ref), channel_id=1, source_target_pairs={{0,64},{64,0},{1,65},{65,1},{2,66},{66,2},{3,67},{67,3},{4,68},{68... | collective-permute-start | bytes 1572872 | tf_op jit(solution)/shard_map/halo_x/ppermute | solution.py:494
  44.6 17.4 %collective-permute-start.8 = (f32[520,128]{1,0:T(8,128)S(1)}, f32[520,128]{1,0:T(8,128)S(1)}, u32[]{:S(2)}, u32[]{:S(2)}) collective-permute-start(f32[520,128]{1,0:T(8,128)S(1)} %get-tuple-element.44), channel_id=1, source_target_pairs={{0,2},{2,4},{4,6},{6,8},{8,10},{10,12},{12,14},{14,16},{16,18},{18... | collective-permute-start | bytes 798728 | tf_op jit(solution)/shard_map/halo_up/ppermute | solution.py:490
  47.0 15.0 %collective-permute-start.9 = (f32[520,128]{1,0:T(8,128)S(1)}, f32[520,128]{1,0:T(8,128)S(1)}, u32[]{:S(2)}, u32[]{:S(2)}) collective-permute-start(f32[520,128]{1,0:T(8,128)S(1)} %get-tuple-element.45), channel_id=1, source_target_pairs={{0,62},{2,0},{4,2},{6,4},{8,6},{10,8},{12,10},{14,12},{16,14},{18,... | collective-permute-start | bytes 798728 | tf_op jit(solution)/shard_map/halo_dn/ppermute | solution.py:492
  52.4 9.7 %collective-permute-start.10 = (f32[64,128]{1,0:T(8,128)S(1)}, f32[64,128]{1,0:T(8,128)S(1)}, u32[]{:S(2)}, u32[]{:S(2)}) collective-permute-start(f32[64,128]{1,0:T(8,128)S(1)} %get-tuple-element.46.zs_ref), channel_id=1, source_target_pairs={{0,1},{1,0},{2,3},{3,2},{4,5},{5,4},{6,7},{7,6},{8,9},{9,8},{10,11... | collective-permute-start | bytes 98312 | tf_op jit(solution)/shard_map/halo_z/ppermute | solution.py:496

commit v2 on v1

--- a/solution.py
+++ b/solution.py
@@ -6,6 +6,7 @@
 from jax.experimental import pallas as pl
 from jax.experimental.pallas import tpu as pltpu
 from jax.sharding import PartitionSpec as P
+
 
 KINDS = 64
 PHOTON = 128
@@ -29,7 +30,7 @@
     return jnp.dot(a, b, preferred_element_type=F32)
 
 
-def totals_kernel(n_ref, v_ref, n2_ref, ty_ref, xpay_ref, zpay_ref):
+def totals_kernel(n_ref, n2_ref, ty_ref, xpay_ref, zpay_ref):
     tiles = []
     for t in range(TILES):
         a = n_ref[pl.ds(t, KINDS, stride=TILES), :]
@@ -46,9 +47,17 @@
     tz = jnp.zeros((KINDS, LANES), F32)
     for t in range(TILES):
         tz = jnp.where(lane == t, jnp.sum(tiles[t], axis=1, keepdims=True), tz)
-    zpay_ref[pl.ds(0, KINDS), :] = tz
-    xpay_ref[pl.ds(256, TILES), :] = v_ref[pl.ds(0, TILES), :]
-    zpay_ref[pl.ds(KINDS, TILES), :] = v_ref[pl.ds(2 * TILES, TILES), :]
+    zpay_ref[...] = tz
+
+
+def combine_kernel(block, count, least, last_ref, total_ref, *refs):
+    below_ref, (below_out, total_out) = refs[:-2], refs[-2:]
+    here = lax.rem(lax.div(lax.axis_index("gy"), block), count)
+    later = jnp.where(here >= least, 1.0, 0.0).astype(F32)
+    last = last_ref[...]
+    total_out[...] = total_ref[...] + last
+    below = later * last
+    below_out[...] = below + below_ref[0][...] if below_ref else below
 
 
 def stacked(x):
@@ -205,7 +214,7 @@
             for q in range(2):
                 cut = slice(q * LANES, (q + 1) * LANES)
                 ll_ref[a + q] = ll[:, cut]
-                n_out[a + q] = (n2_ref[a + q] + (made_ref[a + q] + made[:64, cut])) / (
+                n_out[pl.ds(pl.multiple_of((a + q) * KINDS, KINDS), KINDS), :] = (n2_ref[a + q] + (made_ref[a + q] + made[:64, cut])) / (
                     lost_ref[a + q] + ll[:, cut]
                 )
                 row = pl.ds(a + q, 1)
@@ -258,7 +267,7 @@
 
         @pl.when(listed_ref[m] < TILES)
         def _():
-            n_out[pick[m]] = cur_ref[m]
+            n_out[pl.ds(pl.multiple_of(pick[m] * KINDS, KINDS), KINDS), :] = cur_ref[m]
             temp_out[pl.ds(pick[m], 1), :] = curt_ref[m : m + 1, :]
 
     lane = lax.broadcasted_iota(jnp.int32, (KINDS, LANES), 1)
@@ -268,7 +277,7 @@
     for i in range(4):
         for j in range(4):
             t = i * 4 + j
-            u = n_out[t]
+            u = n_out[pl.ds(t * KINDS, KINDS), :]
             zp = jnp.where(lane // 8 == t, pltpu.roll(u, (8 * t + 4) % LANES, 1), zp)
             if j < 2:
                 dn_out[pl.ds((j * 4 + i) * KINDS, KINDS), :] = u
@@ -276,7 +285,9 @@
                 up_out[pl.ds(((j - 2) * 4 + i) * KINDS, KINDS), :] = u
         up_out[pl.ds(512 + i, 1), :] = v_ref[pl.ds(TILES + i * 4 + 3, 1), :]
         dn_out[pl.ds(512 + i, 1), :] = v_ref[pl.ds(TILES + i * 4, 1), :]
-    z_out[...] = zp
+    z_out[pl.ds(0, KINDS), :] = zp
+    n_out[pl.ds(1024, TILES), :] = v_ref[pl.ds(0, TILES), :]
+    z_out[pl.ds(KINDS, TILES), :] = v_ref[pl.ds(2 * TILES, TILES), :]
 
 
 def flux(face, um1, u, up1, up2):
@@ -284,20 +295,20 @@
     return face * state
 
 
-def inner_kernel(n_ref, v_ref, hx_ref, xpay_ref, acc_ref):
+def inner_kernel(n_ref, v_ref, hx_ref, acc_ref):
     lane = lax.broadcasted_iota(jnp.int32, (KINDS, LANES), 1)
     edge = jnp.logical_or(lane < 2, lane >= LANES - 2)
 
     def x_u(i, j):
         if 0 <= i < 4:
-            return n_ref[i * 4 + j]
-        return hx_ref[(i % 4) * 4 + j]
+            return n_ref[pl.ds((i * 4 + j) * KINDS, KINDS), :]
+        return hx_ref[pl.ds(((i % 4) * 4 + j) * KINDS, KINDS), :]
 
     def x_v(i, j):
         if 0 <= i < 4:
             return v_ref[i * 4 + j : i * 4 + j + 1, :]
-        r = 256 + (i % 4) * 4 + j
-        return xpay_ref[r : r + 1, :]
+        r = 1024 + (i % 4) * 4 + j
+        return hx_ref[r : r + 1, :]
 
     def x_flux(i, j):
         face = 0.5 * (x_v(i, j) + x_v(i + 1, j))
@@ -307,7 +318,7 @@
     for i in range(4):
         for j in range(4):
             t = i * 4 + j
-            u = n_ref[t]
+            u = n_ref[pl.ds(t * KINDS, KINDS), :]
             top = x_flux(i, j)
             change = top - xf[j]
             xf[j] = top
@@ -324,7 +335,7 @@
             acc_ref[t] = u - 0.25 * change
 
 
-def outer_kernel(n_ref, acc_ref, v_ref, lo_ref, hi_ref, zs_ref, hz_ref, zpay_ref, out_ref):
+def outer_kernel(n_ref, acc_ref, v_ref, lo_ref, hi_ref, zs_ref, hz_ref, out_ref):
     lane = lax.broadcasted_iota(jnp.int32, (KINDS, LANES), 1)
     lane1 = lax.broadcasted_iota(jnp.int32, (1, LANES), 1)
     edge = jnp.logical_or(lane < 2, lane >= LANES - 2)
@@ -335,9 +346,9 @@
         here = lane1 // 8 == t
         vown = jnp.where(here, pltpu.roll(v_ref[32 + t : 33 + t, :], (8 * t + 4) % LANES, 1), vown)
         vpart = jnp.where(
-            here, pltpu.roll(zpay_ref[64 + t : 65 + t, :], (8 * t + 4) % LANES, 1), vpart
+            here, pltpu.roll(hz_ref[64 + t : 65 + t, :], (8 * t + 4) % LANES, 1), vpart
         )
-    own, part = zs_ref[...], hz_ref[...]
+    own, part = zs_ref[pl.ds(0, KINDS), :], hz_ref[pl.ds(0, KINDS), :]
     high = lane % 8 < 4
     high1 = lane1 % 8 < 4
     top, tv = jnp.where(high, own, part), jnp.where(high1, vown, vpart)
@@ -357,7 +368,7 @@
             return lo_ref[pl.ds(((j + 2) * 4 + i) * KINDS, KINDS), :]
         if j > 3:
             return hi_ref[pl.ds(((j - 4) * 4 + i) * KINDS, KINDS), :]
-        return n_ref[i * 4 + j]
+        return n_ref[pl.ds((i * 4 + j) * KINDS, KINDS), :]
 
     def y_v(i, j):
         if j < 0:
@@ -396,7 +407,7 @@
     return pltpu.with_memory_space_constraint(x, pltpu.VMEM)
 
 
-def call(kernel, name, out_shape, scalars, inputs, scratch=()):
+def call(kernel, out_shape, scalars, inputs, scratch=()):
     return pl.pallas_call(
         kernel,
         out_shape=out_shape,
@@ -404,7 +415,6 @@
         out_specs=jax.tree.map(lambda _: VM, out_shape),
         scratch_shapes=scratch,
         compiler_params=pltpu.CompilerParams(vmem_limit_bytes=16 * 1024 * 1024),
-        name=name,
     )(*scalars, *inputs)
 
 
@@ -416,91 +426,79 @@
     n = number_densities.reshape(KINDS * TILES, LANES)
     v = flow_vector.reshape(3 * TILES, LANES)
     temp = kinetic_kelvin.reshape(TILES, LANES)
-    scope = jax.named_scope
-    with scope("k_totals"):
-        n2, ty, xown, zown = call(
-            totals_kernel, "totals",
-            (vm(TILES, KINDS, LANES), vm(256, LANES), vm(272, LANES), vm(80, LANES)),
-            [], [n, v],
-        )
-
-    gy = lax.axis_index("gy")
+    n2, ty, xown, zown = call(
+        totals_kernel,
+        (vm(TILES, KINDS, LANES), vm(256, LANES), vm(256, LANES), vm(KINDS, LANES)),
+        [], [n],
+    )
+
     size = lax.axis_size("gy")
     around = lambda count, by: [(a, (a + by) % count) for a in range(count)]
 
     rounds = [
-        ("round_x", gy % 2 >= 1, lambda a: a ^ 1),
-        ("round_y0", (gy // 2) % 2 >= 1, lambda a: a ^ 2),
-        ("round_y1", (gy // 2) % 4 >= 2, lambda a: (a // 8) * 8 + (3 - (a // 2) % 4) * 2 + a % 2),
-        ("round_z0", (gy // 8) % 2 >= 1, lambda a: a ^ 8),
+        ("round_x", (1, 2, 1), lambda a: a ^ 1),
+        ("round_y0", (2, 2, 1), lambda a: a ^ 2),
+        ("round_y1", (2, 4, 2), lambda a: (a // 8) * 8 + (3 - (a // 2) % 4) * 2 + a % 2),
+        ("round_z0", (8, 2, 1), lambda a: a ^ 8),
         ("round_z1", None, lambda a: (3 - a // 8) * 8 + a % 8),
     ]
-    below, total = jnp.zeros_like(ty), ty
+    below, total = None, ty
     for name, later, to in rounds:
-        with scope(name):
-            last = lax.ppermute(total, "gy", [(a, to(a)) for a in range(size)])
+        last = lax.ppermute(total, "gy", [(a, to(a)) for a in range(size)])
         if name == "round_x":
-            with scope("pay_x"):
-                xpay = near(lax.ppermute(xown, "gx", around(lax.axis_size("gx"), 1)))
-            with scope("pay_z"):
-                zpay = near(lax.ppermute(zown, "gz", around(lax.axis_size("gz"), 1)))
+            xpay = near(lax.ppermute(xown, "gx", around(lax.axis_size("gx"), 1)))
+            zpay = near(lax.ppermute(zown, "gz", around(lax.axis_size("gz"), 1)))
+        last = near(last)
         if later is not None:
-            below = below + jnp.where(later, last, 0.0)
-            total = total + last
-    below, total, last = near(below), near(total), near(last)
+            below, total = call(
+                functools.partial(combine_kernel, *later),
+                (vm(256, LANES), vm(256, LANES)),
+                [], [last, total] + ([] if below is None else [below]),
+            )
 
     big = (TILES, PHOTON, LANES)
     mid = (TILES, KINDS, LANES)
-    with scope("k_local"):
-        (ost, g2, pg, lt, lp, cb, made, lost, heat, den, na, yl, yu, zc) = call(
-            local_kernel, "local",
-            (
-                vm(128, 192, dtype=BF16), vm(384, 128, dtype=BF16), vm(80, 512, dtype=BF16),
-                vm(64, 512, dtype=BF16), vm(64, 256, dtype=BF16), vm(320, LANES),
-                vm(*mid), vm(*mid), vm(TILES, LANES), vm(TILES, LANES), vm(*big), vm(*big),
-                vm(*big), vm(TILES * KINDS, LANES),
-            ),
-            [illumination],
-            [
-                n2, temp, opacity_area.T, participant_indices, exothermic_energy[None],
-                arrhenius_coefficient[None], arrhenius_barrier[None], emission_loss[None],
-            ],
-        )
-    with scope("k_early"):
-        pe = call(
-            early_kernel, "early", vm(*big), [illumination],
-            [n2, zc, xown, xpay, zown, zpay, ost],
-        )
-    with scope("k_chem"):
-        n_new, temp_new, up, dn, zs = call(
-            chemistry_kernel, "chemistry",
-            (vm(*mid), hbm(TILES, LANES), vm(520, LANES), vm(520, LANES), vm(KINDS, LANES)),
-            [demanding_patches.reshape(MAXD)],
-            [
-                n2, temp, v, ty, below, total, last, pe, ost, g2, pg, lt, lp, cb,
-                made, lost, heat, den, na, yl, yu,
-            ],
-            [
-                pltpu.VMEM(big, F32), pltpu.VMEM(mid, F32),
-                pltpu.VMEM((MAXD, KINDS, LANES), F32), pltpu.VMEM((8, LANES), F32),
-            ],
-        )
-
-    with scope("halo_up"):
-        low = near(lax.ppermute(up, "gy", around(size, 1)))
-    with scope("halo_dn"):
-        high = near(lax.ppermute(dn, "gy", around(size, -1)))
-    with scope("halo_x"):
-        hx = near(lax.ppermute(n_new, "gx", around(lax.axis_size("gx"), 1)))
-    with scope("halo_z"):
-        hz = near(lax.ppermute(zs, "gz", around(lax.axis_size("gz"), 1)))
-    with scope("k_inner"):
-        acc = call(inner_kernel, "inner", vm(*mid), [], [n_new, v, hx, xpay])
-    with scope("k_outer"):
-        out = call(
-            outer_kernel, "outer", hbm(KINDS * TILES, LANES), [],
-            [n_new, acc, v, low, high, zs, hz, zpay],
-        )
+    (ost, g2, pg, lt, lp, cb, made, lost, heat, den, na, yl, yu, zc) = call(
+        local_kernel,
+        (
+            vm(128, 192, dtype=BF16), vm(384, 128, dtype=BF16), vm(80, 512, dtype=BF16),
+            vm(64, 512, dtype=BF16), vm(64, 256, dtype=BF16), vm(320, LANES),
+            vm(*mid), vm(*mid), vm(TILES, LANES), vm(TILES, LANES), vm(*big), vm(*big),
+            vm(*big), vm(TILES * KINDS, LANES),
+        ),
+        [illumination],
+        [
+            n2, temp, opacity_area.T, participant_indices, exothermic_energy[None],
+            arrhenius_coefficient[None], arrhenius_barrier[None], emission_loss[None],
+        ],
+    )
+    pe = call(
+        early_kernel, vm(*big), [illumination],
+        [n2, zc, xown, xpay, zown, zpay, ost],
+    )
+    n_new, temp_new, up, dn, zs = call(
+        chemistry_kernel,
+        (vm(1040, LANES), hbm(TILES, LANES), vm(520, LANES), vm(520, LANES), vm(80, LANES)),
+        [demanding_patches.reshape(MAXD)],
+        [
+            n2, temp, v, ty, below, total, last, pe, ost, g2, pg, lt, lp, cb,
+            made, lost, heat, den, na, yl, yu,
+        ],
+        [
+            pltpu.VMEM(big, F32), pltpu.VMEM(mid, F32),
+            pltpu.VMEM((MAXD, KINDS, LANES), F32), pltpu.VMEM((8, LANES), F32),
+        ],
+    )
+
+    low = near(lax.ppermute(up, "gy", around(size, 1)))
+    high = near(lax.ppermute(dn, "gy", around(size, -1)))
+    hx = near(lax.ppermute(n_new, "gx", around(lax.axis_size("gx"), 1)))
+    hz = near(lax.ppermute(zs, "gz", around(lax.axis_size("gz"), 1)))
+    acc = call(inner_kernel, vm(*mid), [], [n_new, v, hx])
+    out = call(
+        outer_kernel, hbm(KINDS * TILES, LANES), [],
+        [n_new, acc, v, low, high, zs, hz],
+    )
     return out.reshape(KINDS, 4, 4, LANES), temp_new.reshape(4, 4, LANES)
 
 

time: 64.5 us -> 63.8 us (0.989)
  local copies, waits for them, and re-layouts: 3.17 us -> 2.43 us
    unnamed x24 -> x22, local copies, waits for them, and re-layouts: 3.17 us -> 2.43 us
    pallas_call x6 -> x10, Pallas kernels: 15.6 us -> 15.7 us  [call(): pl.pallas_call(kernel, out_shape=out_shape, in_specs=[SM] * len(scalars)...]
where the time goes in v2:
time: 63.8 us; the launch traced here: 62.9 us
  starting transfers between devices  22.9 us (36%)
  waiting for transfers between devices  21.1 us (33%)
  Pallas kernels  15.7 us (25%)
  local copies, waits for them, and re-layouts  2.43 us (4%)
  between operations  0.78 us (1%)
    pallas_call x10, Pallas kernels, call(): pl.pallas_call(kernel, out_shape=out_shape, in_specs=[SM] * len(scalars)...  15.7 us
    ppermute x5, waiting for transfers between devices, shards(): last = lax.ppermute(total, 'gy', [(a, to(a)) for a in range(size)])  14.2 us
    ppermute x5, starting transfers between devices, shards(): last = lax.ppermute(total, 'gy', [(a, to(a)) for a in range(size)])  13.1 us
    ppermute x1, waiting for transfers between devices, shards(): hz = near(lax.ppermute(zs, 'gz', around(lax.axis_size('gz'), 1)))  6.88 us
    ppermute x1, starting transfers between devices, shards(): high = near(lax.ppermute(dn, 'gy', around(size, -1)))  5.31 us
    ppermute x1, starting transfers between devices, shards(): low = near(lax.ppermute(up, 'gy', around(size, 1)))  2.44 us
    unnamed x22, local copies, waits for them, and re-layouts  2.43 us
    ppermute x1, starting transfers between devices, shards(): hz = near(lax.ppermute(zs, 'gz', around(lax.axis_size('gz'), 1)))  1.51 us
  transfers between devices with their start and end apart: 11, of which 5 were waited for; matrix products, arithmetic and copies ran while one was open for 0% of the time, Pallas kernels for 10%

profile of v2, /device:TPU:2, one launch (start us, length us, event | category | flops | bytes accessed | tf_op | source)
XLA Modules:
  0.0 62.9 jit_solution(18132455590911588046)
XLA Ops:
  0.6 1.0 %copy-done = f32[64,4,4,128]{3,2,1,0:T(4,128)S(1)} copy-done((f32[64,4,4,128]{3,2,1,0:T(4,128)S(1)}, f32[64,4,4,128]{3,2,1,0:T(4,128)}, u32[]{:S(2)}) %copy-start) | copy-done | bytes 524312
  1.7 0.3 shard_map.122
  2.0 2.2 %collective-permute-start = (f32[256,128]{1,0:T(8,128)S(1)}, f32[256,128]{1,0:T(8,128)S(1)}, u32[]{:S(2)}, u32[]{:S(2)}) collective-permute-start(f32[256,128]{1,0:T(8,128)S(1)} %get-tuple-element.34.total_ref.ty_ref), channel_id=1, source_target_pairs={{0,2},{2,0},{4,6},{6,4},{8,10},{10,8},{12,14},{14,12},{16,18},{18,... | collective-permute-start | bytes 393224 | tf_op jit(solution)/shard_map/ppermute | solution.py:447
  4.2 4.6 %collective-permute-done.last_ref = f32[256,128]{1,0:T(8,128)S(1)} collective-permute-done((f32[256,128]{1,0:T(8,128)S(1)}, f32[256,128]{1,0:T(8,128)S(1)}, u32[]{:S(2)}, u32[]{:S(2)}) %collective-permute-start) | collective-permute-done | bytes 131104 | tf_op jit(solution)/shard_map/ppermute | solution.py:447
  8.8 1.7 %collective-permute-start.1 = (f32[256,128]{1,0:T(8,128)S(1)}, f32[256,128]{1,0:T(8,128)S(1)}, u32[]{:S(2)}, u32[]{:S(2)}) collective-permute-start(f32[256,128]{1,0:T(8,128)S(1)} %get-tuple-element.35.total_ref), channel_id=1, source_target_pairs={{0,4},{2,6},{4,0},{6,2},{8,12},{10,14},{12,8},{14,10},{16,20},{18,... | collective-permute-start | bytes 393224 | tf_op jit(solution)/shard_map/ppermute | solution.py:447
  10.5 3.4 %collective-permute-done.1.last_ref = f32[256,128]{1,0:T(8,128)S(1)} collective-permute-done((f32[256,128]{1,0:T(8,128)S(1)}, f32[256,128]{1,0:T(8,128)S(1)}, u32[]{:S(2)}, u32[]{:S(2)}) %collective-permute-start.1) | collective-permute-done | bytes 131104 | tf_op jit(solution)/shard_map/ppermute | solution.py:447
  13.9 3.1 %collective-permute-start.2 = (f32[256,128]{1,0:T(8,128)S(1)}, f32[256,128]{1,0:T(8,128)S(1)}, u32[]{:S(2)}, u32[]{:S(2)}) collective-permute-start(f32[256,128]{1,0:T(8,128)S(1)} %get-tuple-element.37.total_ref), channel_id=1, source_target_pairs={{0,12},{2,14},{4,8},{6,10},{8,4},{10,6},{12,0},{14,2},{16,28},{18,... | collective-permute-start | bytes 393224 | tf_op jit(solution)/shard_map/ppermute | solution.py:447
  17.0 3.2 %collective-permute-done.2.last_ref = f32[256,128]{1,0:T(8,128)S(1)} collective-permute-done((f32[256,128]{1,0:T(8,128)S(1)}, f32[256,128]{1,0:T(8,128)S(1)}, u32[]{:S(2)}, u32[]{:S(2)}) %collective-permute-start.2) | collective-permute-done | bytes 131104 | tf_op jit(solution)/shard_map/ppermute | solution.py:447
  20.2 2.0 %collective-permute-start.3 = (f32[256,128]{1,0:T(8,128)S(1)}, f32[256,128]{1,0:T(8,128)S(1)}, u32[]{:S(2)}, u32[]{:S(2)}) collective-permute-start(f32[256,128]{1,0:T(8,128)S(1)} %get-tuple-element.39.total_ref), channel_id=1, source_target_pairs={{0,16},{2,18},{4,20},{6,22},{8,24},{10,26},{12,28},{14,30},{16,0},... | collective-permute-start | bytes 393224 | tf_op jit(solution)/shard_map/ppermute | solution.py:447
  22.2 0.0 collective-permute-start.5
  22.2 3.0 %collective-permute-done.3.last_ref = f32[256,128]{1,0:T(8,128)S(1)} collective-permute-done((f32[256,128]{1,0:T(8,128)S(1)}, f32[256,128]{1,0:T(8,128)S(1)}, u32[]{:S(2)}, u32[]{:S(2)}) %collective-permute-start.3) | collective-permute-done | bytes 131104 | tf_op jit(solution)/shard_map/ppermute | solution.py:447
  25.3 0.0 copy-start.2
  25.3 4.1 %collective-permute-start.4 = (f32[256,128]{1,0:T(8,128)S(1)}, f32[256,128]{1,0:T(8,128)S(1)}, u32[]{:S(2)}, u32[]{:S(2)}) collective-permute-start(f32[256,128]{1,0:T(8,128)S(1)} %get-tuple-element.42.total_ref), channel_id=1, source_target_pairs={{0,48},{2,50},{4,52},{6,54},{8,56},{10,58},{12,60},{14,62},{16,32}... | collective-permute-start | bytes 393224 | tf_op jit(solution)/shard_map/ppermute | solution.py:447
  29.4 0.5 collective-permute-start.6
  30.0 0.6 %copy-done.4 = s32[4,256]{1,0:T(4,128)S(1)} copy-done((s32[4,256]{1,0:T(4,128)S(1)}, s32[4,256]{1,0:T(4,128)}, u32[]{:S(2)}) %copy-start.4) | copy-done | bytes 4120
  30.6 0.0 copy-done.6
  30.7 3.5 %shard_map.127 = (bf16[128,192]{1,0:T(8,128)(2,1)S(1)}, bf16[384,128]{1,0:T(8,128)(2,1)S(1)}, bf16[80,512]{1,0:T(8,128)(2,1)S(1)}, bf16[64,512]{1,0:T(8,128)(2,1...) custom-call(f32[6]{0:T(128)S(1)} %copy-done.5, ...), custom_call_target="tpu_custom_call" | custom-call | tf_op jit(solution)/shard_map/pallas_call | solution.py:411
  34.1 0.0 collective-permute-done.6.zpay_ref
  34.1 0.0 collective-permute-done.5.xpay_ref
  34.1 1.7 %shard_map.128.pe_ref = f32[16,128,128]{2,1,0:T(8,128)S(1)} custom-call(f32[6]{0:T(128)S(1)} %copy-done.5, f32[16,64,128]{2,1,0:T(8,128)S(1)} %get-tuple-element.33.n2_ref, f32[1024,128]{1,0:T(8,128)S(1)} %get-tuple-element.43.zc_ref, f32[256,128]{1,0:T(8,128)S(1)} %get-tuple-element.44.xown_ref, f32[256,128]{1,0:T(8,128)S(1)} %collective-permute-done.5.xpay_ref, ...), custom_call_target="tpu_custom_call" | custom-call | tf_op jit(solution)/shard_map/pallas_call | solution.py:411
  35.8 0.0 copy-start.1
  35.8 0.0 collective-permute-done.4.last_ref
  35.8 0.0 copy-start.10
  35.8 0.7 %copy-done.1 = f32[3,4,4,128]{3,2,1,0:T(4,128)S(1)} copy-done((f32[3,4,4,128]{3,2,1,0:T(4,128)S(1)}, f32[3,4,4,128]{3,2,1,0:T(4,128)}, u32[]{:S(2)}) %copy-start.1) | copy-done | bytes 24600
  36.6 7.3 %shard_map.129 = (f32[1040,128]{1,0:T(8,128)S(1)}, f32[16,128]{1,0:T(8,128)}, f32[520,128]{1,0:T(8,128)S(1)}, f32[520,128]{1,0:T(8,128)S(1)}, f32[80,128]{1,0:T(8,128)S(1)}) custom-call(s32[4]{0:T(128)S(1)} %bitcast.22, f32[16,64,128]{2,1,0:T(8,128)S(1)} %get-tuple-element.33.n2_ref, f32[16,128]{1,0:T(8,128)S(1)} %bitcast.16, f32[48,128]{1,0:T(8,128)S(1)} %bitcast.12, ...), custom_call_target="tpu_custom_call" | custom-call | tf_op jit(solution)/shard_map/pallas_call | solution.py:411
  43.9 0.0 collective-permute-start.7
  43.9 2.4 %collective-permute-start.8 = (f32[520,128]{1,0:T(8,128)S(1)}, f32[520,128]{1,0:T(8,128)S(1)}, u32[]{:S(2)}, u32[]{:S(2)}) collective-permute-start(f32[520,128]{1,0:T(8,128)S(1)} %get-tuple-element.60), channel_id=1, source_target_pairs={{0,2},{2,4},{4,6},{6,8},{8,10},{10,12},{12,14},{14,16},{16,18},{18... | collective-permute-start | bytes 798728 | tf_op jit(solution)/shard_map/ppermute | solution.py:493
  46.3 5.3 %collective-permute-start.9 = (f32[520,128]{1,0:T(8,128)S(1)}, f32[520,128]{1,0:T(8,128)S(1)}, u32[]{:S(2)}, u32[]{:S(2)}) collective-permute-start(f32[520,128]{1,0:T(8,128)S(1)} %get-tuple-element.61), channel_id=1, source_target_pairs={{0,62},{2,0},{4,2},{6,4},{8,6},{10,8},{12,10},{14,12},{16,14},{18,... | collective-permute-start | bytes 798728 | tf_op jit(solution)/shard_map/ppermute | solution.py:494
  51.6 1.5 %collective-permute-start.10 = (f32[80,128]{1,0:T(8,128)S(1)}, f32[80,128]{1,0:T(8,128)S(1)}, u32[]{:S(2)}, u32[]{:S(2)}) collective-permute-start(f32[80,128]{1,0:T(8,128)S(1)} %get-tuple-element.62.zs_ref), channel_id=1, source_target_pairs={{0,1},{1,0},{2,3},{3,2},{4,5},{5,4},{6,7},{7,6},{8,9},{9,8},{10,11... | collective-permute-start | bytes 122888 | tf_op jit(solution)/shard_map/ppermute | solution.py:496
  53.2 1.4 %shard_map.130.acc_ref = f32[16,64,128]{2,1,0:T(8,128)S(1)} custom-call(f32[1040,128]{1,0:T(8,128)S(1)} %get-tuple-element.59.n_ref, f32[48,128]{1,0:T(8,128)S(1)} %bitcast.13, f32[1040,128]{1,0:T(8,128)S(1)} %collective-permute-done.7.hx_ref), custom_call_target="tpu_custom_call" | custom-call | tf_op jit(solution)/shard_map/pallas_call | solution.py:411
  54.6 6.9 %collective-permute-done.10.hz_ref = f32[80,128]{1,0:T(8,128)S(1)} collective-permute-done((f32[80,128]{1,0:T(8,128)S(1)}, f32[80,128]{1,0:T(8,128)S(1)}, u32[]{:S(2)}, u32[]{:S(2)}) %collective-permute-start.10) | collective-permute-done | bytes 40992 | tf_op jit(solution)/shard_map/ppermute | solution.py:496
  61.5 1.5 %shard_map.131 = f32[1024,128]{1,0:T(8,128)} custom-call(f32[1040,128]{1,0:T(8,128)S(1)} %get-tuple-element.59.n_ref, f32[16,64,128]{2,1,0:T(8,128)S(1)} %shard_map.130.acc_ref, f32[48,128]{1,0:T(8,128)S(1)} %bitcast.14, f32[520,128]{1,0:T(8,128)S(1)} %collective-permute-done.8.lo_ref, f32[520,128]{1,0:T(8,128)S(1)} %collective-permute-done.9.hi_ref, ...), custom_call_target="tpu_custom_call" | custom-call | tf_op jit(solution)/shard_map/pallas_call | solution.py:411
  (22 shorter events, 0.2 us)
Async XLA Ops:
  0.6 1.0 %copy-start = (f32[64,4,4,128]{3,2,1,0:T(4,128)S(1)}, f32[64,4,4,128]{3,2,1,0:T(4,128)}, u32[]{:S(2)}) copy-start(f32[64,4,4,128]{3,2,1,0:T(4,128)} %param.11) | copy-start | bytes 1572868
  2.0 6.8 %collective-permute-start = (f32[256,128]{1,0:T(8,128)S(1)}, f32[256,128]{1,0:T(8,128)S(1)}, u32[]{:S(2)}, u32[]{:S(2)}) collective-permute-start(f32[256,128]{1,0:T(8,128)S(1)} %get-tuple-element.34.total_ref.ty_ref), channel_id=1, source_target_pairs={{0,2},{2,0},{4,6},{6,4},{8,10},{10,8},{12,14},{14,12},{16,18},{18,... | collective-permute-start | bytes 393224 | tf_op jit(solution)/shard_map/ppermute | solution.py:447
  8.8 5.0 %collective-permute-start.1 = (f32[256,128]{1,0:T(8,128)S(1)}, f32[256,128]{1,0:T(8,128)S(1)}, u32[]{:S(2)}, u32[]{:S(2)}) collective-permute-start(f32[256,128]{1,0:T(8,128)S(1)} %get-tuple-element.35.total_ref), channel_id=1, source_target_pairs={{0,4},{2,6},{4,0},{6,2},{8,12},{10,14},{12,8},{14,10},{16,20},{18,... | collective-permute-start | bytes 393224 | tf_op jit(solution)/shard_map/ppermute | solution.py:447
  13.9 6.3 %collective-permute-start.2 = (f32[256,128]{1,0:T(8,128)S(1)}, f32[256,128]{1,0:T(8,128)S(1)}, u32[]{:S(2)}, u32[]{:S(2)}) collective-permute-start(f32[256,128]{1,0:T(8,128)S(1)} %get-tuple-element.37.total_ref), channel_id=1, source_target_pairs={{0,12},{2,14},{4,8},{6,10},{8,4},{10,6},{12,0},{14,2},{16,28},{18,... | collective-permute-start | bytes 393224 | tf_op jit(solution)/shard_map/ppermute | solution.py:447
  20.2 5.0 %collective-permute-start.3 = (f32[256,128]{1,0:T(8,128)S(1)}, f32[256,128]{1,0:T(8,128)S(1)}, u32[]{:S(2)}, u32[]{:S(2)}) collective-permute-start(f32[256,128]{1,0:T(8,128)S(1)} %get-tuple-element.39.total_ref), channel_id=1, source_target_pairs={{0,16},{2,18},{4,20},{6,22},{8,24},{10,26},{12,28},{14,30},{16,0},... | collective-permute-start | bytes 393224 | tf_op jit(solution)/shard_map/ppermute | solution.py:447
  22.2 12.0 %collective-permute-start.5 = (f32[256,128]{1,0:T(8,128)S(1)}, f32[256,128]{1,0:T(8,128)S(1)}, u32[]{:S(2)}, u32[]{:S(2)}) collective-permute-start(f32[256,128]{1,0:T(8,128)S(1)} %get-tuple-element.44.xown_ref), channel_id=1, source_target_pairs={{0,64},{64,0},{1,65},{65,1},{2,66},{66,2},{3,67},{67,3},{4,68},{68... | collective-permute-start | bytes 393224 | tf_op jit(solution)/shard_map/ppermute | solution.py:449
  25.2 4.7 %copy-start.3 = (f32[128,64]{0,1:T(8,128)S(1)}, f32[128,64]{0,1:T(8,128)}, u32[]{:S(2)}) copy-start(f32[128,64]{0,1:T(8,128)} %param.14) | copy-start | bytes 98308
  25.2 4.7 %copy-start.7 = (f32[128]{0:T(128)S(1)}, f32[128]{0:T(128)}, u32[]{:S(2)}) copy-start(f32[128]{0:T(128)} %param.16) | copy-start | bytes 1540
  25.2 4.7 %copy-start.8 = (f32[128]{0:T(128)S(1)}, f32[128]{0:T(128)}, u32[]{:S(2)}) copy-start(f32[128]{0:T(128)} %param.17) | copy-start | bytes 1540
  25.2 4.7 %copy-start.9 = (f32[64]{0:T(128)S(1)}, f32[64]{0:T(128)}, u32[]{:S(2)}) copy-start(f32[64]{0:T(128)} %param.19) | copy-start | bytes 772
  25.3 4.7 %copy-start.2 = (f32[4,4,128]{2,1,0:T(4,128)S(1)}, f32[4,4,128]{2,1,0:T(4,128)}, u32[]{:S(2)}) copy-start(f32[4,4,128]{2,1,0:T(4,128)} %param.12) | copy-start | bytes 24580
  25.3 10.5 %collective-permute-start.4 = (f32[256,128]{1,0:T(8,128)S(1)}, f32[256,128]{1,0:T(8,128)S(1)}, u32[]{:S(2)}, u32[]{:S(2)}) collective-permute-start(f32[256,128]{1,0:T(8,128)S(1)} %get-tuple-element.42.total_ref), channel_id=1, source_target_pairs={{0,48},{2,50},{4,52},{6,54},{8,56},{10,58},{12,60},{14,62},{16,32}... | collective-permute-start | bytes 393224 | tf_op jit(solution)/shard_map/ppermute | solution.py:447
  29.4 4.7 %collective-permute-start.6 = (f32[64,128]{1,0:T(8,128)S(1)}, f32[64,128]{1,0:T(8,128)S(1)}, u32[]{:S(2)}, u32[]{:S(2)}) collective-permute-start(f32[64,128]{1,0:T(8,128)S(1)} %get-tuple-element.45.zown_ref), channel_id=1, source_target_pairs={{0,1},{1,0},{2,3},{3,2},{4,5},{5,4},{6,7},{7,6},{8,9},{9,8},{10,11... | collective-permute-start | bytes 98312 | tf_op jit(solution)/shard_map/ppermute | solution.py:450
  29.9 0.7 %copy-start.4 = (s32[4,256]{1,0:T(4,128)S(1)}, s32[4,256]{1,0:T(4,128)}, u32[]{:S(2)}) copy-start(s32[4,256]{1,0:T(4,128)} %idx_ref.1) | copy-start | bytes 12292
  29.9 0.7 %copy-start.5 = (f32[6]{0:T(128)S(1)}, f32[6]{0:T(128)}, u32[]{:S(2)}) copy-start(f32[6]{0:T(128)} %light_ref.3) | copy-start | bytes 76
  29.9 0.7 %copy-start.6 = (f32[256]{0:T(256)S(1)}, f32[256]{0:T(256)}, u32[]{:S(2)}) copy-start(f32[256]{0:T(256)} %param.18) | copy-start | bytes 3076
  35.8 0.7 %copy-start.1 = (f32[3,4,4,128]{3,2,1,0:T(4,128)S(1)}, f32[3,4,4,128]{3,2,1,0:T(4,128)}, u32[]{:S(2)}) copy-start(f32[3,4,4,128]{3,2,1,0:T(4,128)} %param.13) | copy-start | bytes 73732
  35.8 0.7 %copy-start.10 = (s32[1,1,1,4]{3,2,1,0:T(1,128)S(1)}, s32[1,1,1,4]{3,2,1,0:T(1,128)}, u32[]{:S(2)}) copy-start(s32[1,1,1,4]{3,2,1,0:T(1,128)} %param.21) | copy-start | bytes 52
  43.9 9.3 %collective-permute-start.7 = (f32[1040,128]{1,0:T(8,128)S(1)}, f32[1040,128]{1,0:T(8,128)S(1)}, u32[]{:S(2)}, u32[]{:S(2)}) collective-permute-start(f32[1040,128]{1,0:T(8,128)S(1)} %get-tuple-element.59.n_ref), channel_id=1, source_target_pairs={{0,64},{64,0},{1,65},{65,1},{2,66},{66,2},{3,67},{67,3},{4,68},{68... | collective-permute-start | bytes 1597448 | tf_op jit(solution)/shard_map/ppermute | solution.py:495
  43.9 17.6 %collective-permute-start.8 = (f32[520,128]{1,0:T(8,128)S(1)}, f32[520,128]{1,0:T(8,128)S(1)}, u32[]{:S(2)}, u32[]{:S(2)}) collective-permute-start(f32[520,128]{1,0:T(8,128)S(1)} %get-tuple-element.60), channel_id=1, source_target_pairs={{0,2},{2,4},{4,6},{6,8},{8,10},{10,12},{12,14},{14,16},{16,18},{18... | collective-permute-start | bytes 798728 | tf_op jit(solution)/shard_map/ppermute | solution.py:493
  46.3 15.1 %collective-permute-start.9 = (f32[520,128]{1,0:T(8,128)S(1)}, f32[520,128]{1,0:T(8,128)S(1)}, u32[]{:S(2)}, u32[]{:S(2)}) collective-permute-start(f32[520,128]{1,0:T(8,128)S(1)} %get-tuple-element.61), channel_id=1, source_target_pairs={{0,62},{2,0},{4,2},{6,4},{8,6},{10,8},{12,10},{14,12},{16,14},{18,... | collective-permute-start | bytes 798728 | tf_op jit(solution)/shard_map/ppermute | solution.py:494
  51.6 9.8 %collective-permute-start.10 = (f32[80,128]{1,0:T(8,128)S(1)}, f32[80,128]{1,0:T(8,128)S(1)}, u32[]{:S(2)}, u32[]{:S(2)}) collective-permute-start(f32[80,128]{1,0:T(8,128)S(1)} %get-tuple-element.62.zs_ref), channel_id=1, source_target_pairs={{0,1},{1,0},{2,3},{3,2},{4,5},{5,4},{6,7},{7,6},{8,9},{9,8},{10,11... | collective-permute-start | bytes 122888 | tf_op jit(solution)/shard_map/ppermute | solution.py:496

commit v3 on v2

--- a/solution.py
+++ b/solution.py
@@ -1,5 +1,3 @@
-import functools
-
 import jax
 import jax.numpy as jnp
 from jax import lax
@@ -50,14 +48,22 @@
     zpay_ref[...] = tz
 
 
-def combine_kernel(block, count, least, last_ref, total_ref, *refs):
-    below_ref, (below_out, total_out) = refs[:-2], refs[-2:]
+def later(block, count, least):
     here = lax.rem(lax.div(lax.axis_index("gy"), block), count)
-    later = jnp.where(here >= least, 1.0, 0.0).astype(F32)
-    last = last_ref[...]
-    total_out[...] = total_ref[...] + last
-    below = later * last
-    below_out[...] = below + below_ref[0][...] if below_ref else below
+    return jnp.where(here >= least, 1.0, 0.0).astype(F32)
+
+
+def pair_kernel(own_ref, other_ref, pair_ref):
+    pair_ref[...] = own_ref[...] + other_ref[...]
+
+
+def plane_kernel(other_ref, pair_ref, flip_ref, turn_ref, both_ref, below_ref, plane_ref):
+    flip = flip_ref[...]
+    far = turn_ref[...] + both_ref[...]
+    plane_ref[...] = (pair_ref[...] + flip) + far
+    below_ref[...] = later(1, 2, 1) * other_ref[...] + (
+        later(2, 2, 1) * flip + later(2, 4, 2) * far
+    )
 
 
 def stacked(x):
@@ -155,7 +161,7 @@
     return jnp.concatenate(parts, axis=1)
 
 
-def early_kernel(light_ref, n2_ref, zc_ref, xown_ref, xpay_ref, zown_ref, zpay_ref, ost_ref, pe_ref):
+def early_kernel(light_ref, listed_ref, n2_ref, zc_ref, xown_ref, xpay_ref, zown_ref, zpay_ref, ost_ref, pe_ref):
     gx = lax.axis_index("gx").astype(F32)
     gz = lax.axis_index("gz").astype(F32)
     ost = ost_ref[...]
@@ -181,19 +187,20 @@
 
 def chemistry_kernel(
     listed_ref,
-    n2_ref, temp_ref, v_ref, ty_ref, below_ref, total_ref, last_ref, pe_ref,
+    n2_ref, temp_ref, v_ref, ty_ref, below_ref, plane_ref, flip_ref, turn_ref, both_ref, pe_ref,
     ost_ref, g2_ref, pg_ref, lt_ref, lp_ref, cb_ref,
     made_ref, lost_ref, heat_ref, den_ref, na_ref, yl_ref, yu_ref,
     n_out, temp_out, up_out, dn_out, z_out,
     ph_ref, ll_ref, cur_ref, curt_ref,
 ):
-    upper = jnp.where(lax.axis_index("gy") >= 16, 1.0, 0.0).astype(F32)
+    near_z, far_z = later(8, 2, 1), later(8, 4, 2)
     ost = ost_ref[...]
     for i in range(4):
         cut = pl.ds(i * KINDS, KINDS)
-        last = last_ref[cut, :]
-        below = below_ref[cut, :] + upper * last
-        above = (total_ref[cut, :] + last) - below - ty_ref[cut, :]
+        flip = flip_ref[cut, :]
+        away = turn_ref[cut, :] + both_ref[cut, :]
+        below = below_ref[cut, :] + (near_z * flip + far_z * away)
+        above = ((plane_ref[cut, :] + flip) + away) - below - ty_ref[cut, :]
         far = jnp.exp2(dot(ost, stacked(wide([below, above]))) * (-LOG2E / 128.0))
         for j in range(4):
             t = i * 4 + j
@@ -426,6 +433,7 @@
     n = number_densities.reshape(KINDS * TILES, LANES)
     v = flow_vector.reshape(3 * TILES, LANES)
     temp = kinetic_kelvin.reshape(TILES, LANES)
+    listed = demanding_patches.reshape(MAXD)
     n2, ty, xown, zown = call(
         totals_kernel,
         (vm(TILES, KINDS, LANES), vm(256, LANES), vm(256, LANES), vm(KINDS, LANES)),
@@ -435,26 +443,20 @@
     size = lax.axis_size("gy")
     around = lambda count, by: [(a, (a + by) % count) for a in range(count)]
 
-    rounds = [
-        ("round_x", (1, 2, 1), lambda a: a ^ 1),
-        ("round_y0", (2, 2, 1), lambda a: a ^ 2),
-        ("round_y1", (2, 4, 2), lambda a: (a // 8) * 8 + (3 - (a // 2) % 4) * 2 + a % 2),
-        ("round_z0", (8, 2, 1), lambda a: a ^ 8),
-        ("round_z1", None, lambda a: (3 - a // 8) * 8 + a % 8),
-    ]
-    below, total = None, ty
-    for name, later, to in rounds:
-        last = lax.ppermute(total, "gy", [(a, to(a)) for a in range(size)])
-        if name == "round_x":
-            xpay = near(lax.ppermute(xown, "gx", around(lax.axis_size("gx"), 1)))
-            zpay = near(lax.ppermute(zown, "gz", around(lax.axis_size("gz"), 1)))
-        last = near(last)
-        if later is not None:
-            below, total = call(
-                functools.partial(combine_kernel, *later),
-                (vm(256, LANES), vm(256, LANES)),
-                [], [last, total] + ([] if below is None else [below]),
-            )
+    def send(value, to):
+        return near(lax.ppermute(value, "gy", [(a, to(a)) for a in range(size)]))
+
+    flip_y = lambda a: a ^ 2
+    turn_y = lambda a: (a // 8) * 8 + (3 - (a // 2) % 4) * 2 + a % 2
+    flip_z = lambda a: a ^ 8
+    turn_z = lambda a: (3 - a // 8) * 8 + a % 8
+    other = send(ty, lambda a: a ^ 1)
+    xpay = near(lax.ppermute(xown, "gx", around(lax.axis_size("gx"), 1)))
+    zpay = near(lax.ppermute(zown, "gz", around(lax.axis_size("gz"), 1)))
+    pair = call(pair_kernel, vm(256, LANES), [], [ty, other])
+    y_parts = [send(pair, flip_y), send(pair, turn_y), send(pair, lambda a: turn_y(flip_y(a)))]
+    below, plane = call(plane_kernel, (vm(256, LANES), vm(256, LANES)), [], [other, pair] + y_parts)
+    z_parts = [send(plane, flip_z), send(plane, turn_z), send(plane, lambda a: turn_z(flip_z(a)))]
 
     big = (TILES, PHOTON, LANES)
     mid = (TILES, KINDS, LANES)
@@ -473,15 +475,15 @@
         ],
     )
     pe = call(
-        early_kernel, vm(*big), [illumination],
+        early_kernel, vm(*big), [illumination, listed],
         [n2, zc, xown, xpay, zown, zpay, ost],
     )
     n_new, temp_new, up, dn, zs = call(
         chemistry_kernel,
         (vm(1040, LANES), hbm(TILES, LANES), vm(520, LANES), vm(520, LANES), vm(80, LANES)),
-        [demanding_patches.reshape(MAXD)],
+        [listed],
         [
-            n2, temp, v, ty, below, total, last, pe, ost, g2, pg, lt, lp, cb,
+            n2, temp, v, ty, below, plane, *z_parts, pe, ost, g2, pg, lt, lp, cb,
             made, lost, heat, den, na, yl, yu,
         ],
         [

time: 63.8 us -> 58.6 us (0.918)
  waiting for transfers between devices: 21.1 us -> 16.8 us
  starting transfers between devices: 22.9 us -> 21.3 us
  local copies, waits for them, and re-layouts: 2.43 us -> 3.07 us
    ppermute x5 -> x7, waiting for transfers between devices: 14.2 us -> 9.84 us  [send(): return near(lax.ppermute(value, 'gy', [(a, to(a)) for a in range(size)]))]
    ppermute x5 -> x7, starting transfers between devices: 13.1 us -> 11.5 us  [send(): return near(lax.ppermute(value, 'gy', [(a, to(a)) for a in range(size)]))]
    pallas_call x10 -> x8, Pallas kernels: 15.7 us -> 15.8 us  [call(): pl.pallas_call(kernel, out_shape=out_shape, in_specs=[SM] * len(scalars)...]
  transfers between devices with their start and end apart: 11 -> 13, of which waited for: 5 -> 5; matrix products, arithmetic and copies ran while one was open for 0% -> 0% of each run, Pallas kernels for 10% -> 11%
where the time goes in v3:
time: 58.6 us; the launch traced here: 57.8 us
  starting transfers between devices  21.3 us (36%)
  waiting for transfers between devices  16.8 us (29%)
  Pallas kernels  15.8 us (27%)
  local copies, waits for them, and re-layouts  3.07 us (5%)
  between operations  0.78 us (1%)
    pallas_call x8, Pallas kernels, call(): pl.pallas_call(kernel, out_shape=out_shape, in_specs=[SM] * len(scalars)...  15.8 us
    ppermute x7, starting transfers between devices, send(): return near(lax.ppermute(value, 'gy', [(a, to(a)) for a in range(size)]))  11.5 us
    ppermute x7, waiting for transfers between devices, send(): return near(lax.ppermute(value, 'gy', [(a, to(a)) for a in range(size)]))  9.84 us
    ppermute x1, waiting for transfers between devices, shards(): hz = near(lax.ppermute(zs, 'gz', around(lax.axis_size('gz'), 1)))  6.92 us
    ppermute x1, starting transfers between devices, shards(): high = near(lax.ppermute(dn, 'gy', around(size, -1)))  5.34 us
    unnamed x22, local copies, waits for them, and re-layouts  3.07 us
    ppermute x1, starting transfers between devices, shards(): low = near(lax.ppermute(up, 'gy', around(size, 1)))  2.41 us
    ppermute x1, starting transfers between devices, shards(): hz = near(lax.ppermute(zs, 'gz', around(lax.axis_size('gz'), 1)))  1.48 us
  transfers between devices with their start and end apart: 13, of which 5 were waited for; matrix products, arithmetic and copies ran while one was open for 0% of the time, Pallas kernels for 11%

profile of v3, /device:TPU:2, one launch (start us, length us, event | category | flops | bytes accessed | tf_op | source)
XLA Modules:
  0.0 57.8 jit_solution(8399749499171207616)
XLA Ops:
  0.6 1.0 %copy-done = f32[64,4,4,128]{3,2,1,0:T(4,128)S(1)} copy-done((f32[64,4,4,128]{3,2,1,0:T(4,128)S(1)}, f32[64,4,4,128]{3,2,1,0:T(4,128)}, u32[]{:S(2)}) %copy-start) | copy-done | bytes 524312
  1.7 0.3 shard_map.122
  2.0 2.2 %collective-permute-start = (f32[256,128]{1,0:T(8,128)S(1)}, f32[256,128]{1,0:T(8,128)S(1)}, u32[]{:S(2)}, u32[]{:S(2)}) collective-permute-start(f32[256,128]{1,0:T(8,128)S(1)} %get-tuple-element.28.own_ref.ty_ref), channel_id=1, source_target_pairs={{0,2},{2,0},{4,6},{6,4},{8,10},{10,8},{12,14},{14,12},{16,18},{18,... | collective-permute-start | bytes 393224 | tf_op jit(solution)/shard_map/ppermute | solution.py:447
  4.2 4.6 %collective-permute-done.other_ref = f32[256,128]{1,0:T(8,128)S(1)} collective-permute-done((f32[256,128]{1,0:T(8,128)S(1)}, f32[256,128]{1,0:T(8,128)S(1)}, u32[]{:S(2)}, u32[]{:S(2)}) %collective-permute-start) | collective-permute-done | bytes 131104 | tf_op jit(solution)/shard_map/ppermute | solution.py:447
  8.8 3.3 %collective-permute-start.3 = (f32[256,128]{1,0:T(8,128)S(1)}, f32[256,128]{1,0:T(8,128)S(1)}, u32[]{:S(2)}, u32[]{:S(2)}) collective-permute-start(f32[256,128]{1,0:T(8,128)S(1)} %shard_map.123.pair_ref), channel_id=1, source_target_pairs={{0,8},{2,10},{4,12},{6,14},{8,0},{10,2},{12,4},{14,6},{16,24},{18,... | collective-permute-start | bytes 393224 | tf_op jit(solution)/shard_map/ppermute | solution.py:447
  12.1 1.1 %collective-permute-start.2 = (f32[256,128]{1,0:T(8,128)S(1)}, f32[256,128]{1,0:T(8,128)S(1)}, u32[]{:S(2)}, u32[]{:S(2)}) collective-permute-start(f32[256,128]{1,0:T(8,128)S(1)} %shard_map.123.pair_ref), channel_id=1, source_target_pairs={{0,12},{2,14},{4,8},{6,10},{8,4},{10,6},{12,0},{14,2},{16,28},{18,... | collective-permute-start | bytes 393224 | tf_op jit(solution)/shard_map/ppermute | solution.py:447
  13.1 2.3 %collective-permute-done.3.both_ref = f32[256,128]{1,0:T(8,128)S(1)} collective-permute-done((f32[256,128]{1,0:T(8,128)S(1)}, f32[256,128]{1,0:T(8,128)S(1)}, u32[]{:S(2)}, u32[]{:S(2)}) %collective-permute-start.3) | collective-permute-done | bytes 131104 | tf_op jit(solution)/shard_map/ppermute | solution.py:447
  15.4 2.8 %collective-permute-done.2.turn_ref = f32[256,128]{1,0:T(8,128)S(1)} collective-permute-done((f32[256,128]{1,0:T(8,128)S(1)}, f32[256,128]{1,0:T(8,128)S(1)}, u32[]{:S(2)}, u32[]{:S(2)}) %collective-permute-start.2) | collective-permute-done | bytes 131104 | tf_op jit(solution)/shard_map/ppermute | solution.py:447
  18.2 0.1 collective-permute-done.1.flip_ref
  18.4 0.1 shard_map.124
  18.4 0.0 copy-start.2
  18.4 4.0 %collective-permute-start.6 = (f32[256,128]{1,0:T(8,128)S(1)}, f32[256,128]{1,0:T(8,128)S(1)}, u32[]{:S(2)}, u32[]{:S(2)}) collective-permute-start(f32[256,128]{1,0:T(8,128)S(1)} %get-tuple-element.30.plane_ref), channel_id=1, source_target_pairs={{0,32},{2,34},{4,36},{6,38},{8,40},{10,42},{12,44},{14,46},{16,48}... | collective-permute-start | bytes 393224 | tf_op jit(solution)/shard_map/ppermute | solution.py:447
  22.4 0.7 %collective-permute-start.5 = (f32[256,128]{1,0:T(8,128)S(1)}, f32[256,128]{1,0:T(8,128)S(1)}, u32[]{:S(2)}, u32[]{:S(2)}) collective-permute-start(f32[256,128]{1,0:T(8,128)S(1)} %get-tuple-element.30.plane_ref), channel_id=1, source_target_pairs={{0,48},{2,50},{4,52},{6,54},{8,56},{10,58},{12,60},{14,62},{16,32}... | collective-permute-start | bytes 393224 | tf_op jit(solution)/shard_map/ppermute | solution.py:447
  23.1 0.3 collective-permute-start.4
  23.4 0.5 collective-permute-start.8
  24.0 0.6 %copy-done.4 = s32[4,256]{1,0:T(4,128)S(1)} copy-done((s32[4,256]{1,0:T(4,128)S(1)}, s32[4,256]{1,0:T(4,128)}, u32[]{:S(2)}) %copy-start.4) | copy-done | bytes 4120
  24.6 0.0 copy-done.7
  24.7 3.5 %shard_map.125 = (bf16[128,192]{1,0:T(8,128)(2,1)S(1)}, bf16[384,128]{1,0:T(8,128)(2,1)S(1)}, bf16[80,512]{1,0:T(8,128)(2,1)S(1)}, bf16[64,512]{1,0:T(8,128)(2,1...) custom-call(f32[6]{0:T(128)S(1)} %copy-done.5, ...), custom_call_target="tpu_custom_call" | custom-call | tf_op jit(solution)/shard_map/pallas_call | solution.py:418
  28.1 0.0 collective-permute-done.7.xpay_ref
  28.2 0.0 copy-start.6
  28.2 0.6 %copy-done.6 = s32[1,1,1,4]{3,2,1,0:T(1,128)S(1)} copy-done((s32[1,1,1,4]{3,2,1,0:T(1,128)S(1)}, s32[1,1,1,4]{3,2,1,0:T(1,128)}, u32[]{:S(2)}) %copy-start.6) | copy-done | bytes 40
  28.8 1.7 %shard_map.126.pe_ref = f32[16,128,128]{2,1,0:T(8,128)S(1)} custom-call(f32[6]{0:T(128)S(1)} %copy-done.5, s32[4]{0:T(128)S(1)} %bitcast.18, f32[16,64,128]{2,1,0:T(8,128)S(1)} %get-tuple-element.27.n2_ref, f32[1024,128]{1,0:T(8,128)S(1)} %get-tuple-element.31.zc_ref, f32[256,128]{1,0:T(8,128)S(1)} %get-tuple-element.32.xown_ref, ...), custom_call_target="tpu_custom_call" | custom-call | tf_op jit(solution)/shard_map/pallas_call | solution.py:418
  30.5 0.0 copy-start.1
  30.5 0.0 collective-permute-done.6.both_ref
  30.5 0.7 %copy-done.1 = f32[3,4,4,128]{3,2,1,0:T(4,128)S(1)} copy-done((f32[3,4,4,128]{3,2,1,0:T(4,128)S(1)}, f32[3,4,4,128]{3,2,1,0:T(4,128)}, u32[]{:S(2)}) %copy-start.1) | copy-done | bytes 24600
  31.2 7.5 %shard_map.127 = (f32[1040,128]{1,0:T(8,128)S(1)}, f32[16,128]{1,0:T(8,128)}, f32[520,128]{1,0:T(8,128)S(1)}, f32[520,128]{1,0:T(8,128)S(1)}, f32[80,128]{1,0:T(8,128)S(1)}) custom-call(s32[4]{0:T(128)S(1)} %bitcast.19, f32[16,64,128]{2,1,0:T(8,128)S(1)} %get-tuple-element.27.n2_ref, f32[16,128]{1,0:T(8,128)S(1)} %bitcast.16, f32[48,128]{1,0:T(8,128)S(1)} %bitcast.12, ...), custom_call_target="tpu_custom_call" | custom-call | tf_op jit(solution)/shard_map/pallas_call | solution.py:418
  38.7 2.4 %collective-permute-start.10 = (f32[520,128]{1,0:T(8,128)S(1)}, f32[520,128]{1,0:T(8,128)S(1)}, u32[]{:S(2)}, u32[]{:S(2)}) collective-permute-start(f32[520,128]{1,0:T(8,128)S(1)} %get-tuple-element.48), channel_id=1, source_target_pairs={{0,2},{2,4},{4,6},{6,8},{8,10},{10,12},{12,14},{14,16},{16,18},{18... | collective-permute-start | bytes 798728 | tf_op jit(solution)/shard_map/ppermute | solution.py:495
  41.1 5.3 %collective-permute-start.11 = (f32[520,128]{1,0:T(8,128)S(1)}, f32[520,128]{1,0:T(8,128)S(1)}, u32[]{:S(2)}, u32[]{:S(2)}) collective-permute-start(f32[520,128]{1,0:T(8,128)S(1)} %get-tuple-element.49), channel_id=1, source_target_pairs={{0,62},{2,0},{4,2},{6,4},{8,6},{10,8},{12,10},{14,12},{16,14},{18,... | collective-permute-start | bytes 798728 | tf_op jit(solution)/shard_map/ppermute | solution.py:496
  46.4 1.5 %collective-permute-start.12 = (f32[80,128]{1,0:T(8,128)S(1)}, f32[80,128]{1,0:T(8,128)S(1)}, u32[]{:S(2)}, u32[]{:S(2)}) collective-permute-start(f32[80,128]{1,0:T(8,128)S(1)} %get-tuple-element.50.zs_ref), channel_id=1, source_target_pairs={{0,1},{1,0},{2,3},{3,2},{4,5},{5,4},{6,7},{7,6},{8,9},{9,8},{10,11... | collective-permute-start | bytes 122888 | tf_op jit(solution)/shard_map/ppermute | solution.py:498
  47.9 1.4 %shard_map.128.acc_ref = f32[16,64,128]{2,1,0:T(8,128)S(1)} custom-call(f32[1040,128]{1,0:T(8,128)S(1)} %get-tuple-element.47.n_ref, f32[48,128]{1,0:T(8,128)S(1)} %bitcast.13, f32[1040,128]{1,0:T(8,128)S(1)} %collective-permute-done.9.hx_ref), custom_call_target="tpu_custom_call" | custom-call | tf_op jit(solution)/shard_map/pallas_call | solution.py:418
  49.4 6.9 %collective-permute-done.12.hz_ref = f32[80,128]{1,0:T(8,128)S(1)} collective-permute-done((f32[80,128]{1,0:T(8,128)S(1)}, f32[80,128]{1,0:T(8,128)S(1)}, u32[]{:S(2)}, u32[]{:S(2)}) %collective-permute-start.12) | collective-permute-done | bytes 40992 | tf_op jit(solution)/shard_map/ppermute | solution.py:498
  56.3 1.5 %shard_map.129 = f32[1024,128]{1,0:T(8,128)} custom-call(f32[1040,128]{1,0:T(8,128)S(1)} %get-tuple-element.47.n_ref, f32[16,64,128]{2,1,0:T(8,128)S(1)} %shard_map.128.acc_ref, f32[48,128]{1,0:T(8,128)S(1)} %bitcast.14, f32[520,128]{1,0:T(8,128)S(1)} %collective-permute-done.10.lo_ref, f32[520,128]{1,0:T(8,128)S(1)} %collective-permute-done.11.hi_ref, ...), custom_call_target="tpu_custom_call" | custom-call | tf_op jit(solution)/shard_map/pallas_call | solution.py:418
  (24 shorter events, 0.1 us)
Async XLA Ops:
  0.6 1.0 %copy-start = (f32[64,4,4,128]{3,2,1,0:T(4,128)S(1)}, f32[64,4,4,128]{3,2,1,0:T(4,128)}, u32[]{:S(2)}) copy-start(f32[64,4,4,128]{3,2,1,0:T(4,128)} %param.11) | copy-start | bytes 1572868
  2.0 6.8 %collective-permute-start = (f32[256,128]{1,0:T(8,128)S(1)}, f32[256,128]{1,0:T(8,128)S(1)}, u32[]{:S(2)}, u32[]{:S(2)}) collective-permute-start(f32[256,128]{1,0:T(8,128)S(1)} %get-tuple-element.28.own_ref.ty_ref), channel_id=1, source_target_pairs={{0,2},{2,0},{4,6},{6,4},{8,10},{10,8},{12,14},{14,12},{16,18},{18,... | collective-permute-start | bytes 393224 | tf_op jit(solution)/shard_map/ppermute | solution.py:447
  8.8 6.6 %collective-permute-start.3 = (f32[256,128]{1,0:T(8,128)S(1)}, f32[256,128]{1,0:T(8,128)S(1)}, u32[]{:S(2)}, u32[]{:S(2)}) collective-permute-start(f32[256,128]{1,0:T(8,128)S(1)} %shard_map.123.pair_ref), channel_id=1, source_target_pairs={{0,8},{2,10},{4,12},{6,14},{8,0},{10,2},{12,4},{14,6},{16,24},{18,... | collective-permute-start | bytes 393224 | tf_op jit(solution)/shard_map/ppermute | solution.py:447
  12.1 6.2 %collective-permute-start.2 = (f32[256,128]{1,0:T(8,128)S(1)}, f32[256,128]{1,0:T(8,128)S(1)}, u32[]{:S(2)}, u32[]{:S(2)}) collective-permute-start(f32[256,128]{1,0:T(8,128)S(1)} %shard_map.123.pair_ref), channel_id=1, source_target_pairs={{0,12},{2,14},{4,8},{6,10},{8,4},{10,6},{12,0},{14,2},{16,28},{18,... | collective-permute-start | bytes 393224 | tf_op jit(solution)/shard_map/ppermute | solution.py:447
  13.1 5.2 %collective-permute-start.1 = (f32[256,128]{1,0:T(8,128)S(1)}, f32[256,128]{1,0:T(8,128)S(1)}, u32[]{:S(2)}, u32[]{:S(2)}) collective-permute-start(f32[256,128]{1,0:T(8,128)S(1)} %shard_map.123.pair_ref), channel_id=1, source_target_pairs={{0,4},{2,6},{4,0},{6,2},{8,12},{10,14},{12,8},{14,10},{16,20},{18,... | collective-permute-start | bytes 393224 | tf_op jit(solution)/shard_map/ppermute | solution.py:447
  13.1 15.0 %collective-permute-start.7 = (f32[256,128]{1,0:T(8,128)S(1)}, f32[256,128]{1,0:T(8,128)S(1)}, u32[]{:S(2)}, u32[]{:S(2)}) collective-permute-start(f32[256,128]{1,0:T(8,128)S(1)} %get-tuple-element.32.xown_ref), channel_id=1, source_target_pairs={{0,64},{64,0},{1,65},{65,1},{2,66},{66,2},{3,67},{67,3},{4,68},{68... | collective-permute-start | bytes 393224 | tf_op jit(solution)/shard_map/ppermute | solution.py:454
  18.4 5.6 %copy-start.3 = (f32[128,64]{0,1:T(8,128)S(1)}, f32[128,64]{0,1:T(8,128)}, u32[]{:S(2)}) copy-start(f32[128,64]{0,1:T(8,128)} %param.14) | copy-start | bytes 98308
  18.4 5.6 %copy-start.8 = (f32[128]{0:T(128)S(1)}, f32[128]{0:T(128)}, u32[]{:S(2)}) copy-start(f32[128]{0:T(128)} %param.16) | copy-start | bytes 1540
  18.4 5.6 %copy-start.9 = (f32[128]{0:T(128)S(1)}, f32[128]{0:T(128)}, u32[]{:S(2)}) copy-start(f32[128]{0:T(128)} %param.17) | copy-start | bytes 1540
  18.4 5.6 %copy-start.10 = (f32[64]{0:T(128)S(1)}, f32[64]{0:T(128)}, u32[]{:S(2)}) copy-start(f32[64]{0:T(128)} %param.19) | copy-start | bytes 772
  18.4 5.6 %copy-start.2 = (f32[4,4,128]{2,1,0:T(4,128)S(1)}, f32[4,4,128]{2,1,0:T(4,128)}, u32[]{:S(2)}) copy-start(f32[4,4,128]{2,1,0:T(4,128)} %param.12) | copy-start | bytes 24580
  18.4 12.1 %collective-permute-start.6 = (f32[256,128]{1,0:T(8,128)S(1)}, f32[256,128]{1,0:T(8,128)S(1)}, u32[]{:S(2)}, u32[]{:S(2)}) collective-permute-start(f32[256,128]{1,0:T(8,128)S(1)} %get-tuple-element.30.plane_ref), channel_id=1, source_target_pairs={{0,32},{2,34},{4,36},{6,38},{8,40},{10,42},{12,44},{14,46},{16,48}... | collective-permute-start | bytes 393224 | tf_op jit(solution)/shard_map/ppermute | solution.py:447
  22.4 8.1 %collective-permute-start.5 = (f32[256,128]{1,0:T(8,128)S(1)}, f32[256,128]{1,0:T(8,128)S(1)}, u32[]{:S(2)}, u32[]{:S(2)}) collective-permute-start(f32[256,128]{1,0:T(8,128)S(1)} %get-tuple-element.30.plane_ref), channel_id=1, source_target_pairs={{0,48},{2,50},{4,52},{6,54},{8,56},{10,58},{12,60},{14,62},{16,32}... | collective-permute-start | bytes 393224 | tf_op jit(solution)/shard_map/ppermute | solution.py:447
  23.1 7.4 %collective-permute-start.4 = (f32[256,128]{1,0:T(8,128)S(1)}, f32[256,128]{1,0:T(8,128)S(1)}, u32[]{:S(2)}, u32[]{:S(2)}) collective-permute-start(f32[256,128]{1,0:T(8,128)S(1)} %get-tuple-element.30.plane_ref), channel_id=1, source_target_pairs={{0,16},{2,18},{4,20},{6,22},{8,24},{10,26},{12,28},{14,30},{16,0},... | collective-permute-start | bytes 393224 | tf_op jit(solution)/shard_map/ppermute | solution.py:447
  23.4 4.7 %collective-permute-start.8 = (f32[64,128]{1,0:T(8,128)S(1)}, f32[64,128]{1,0:T(8,128)S(1)}, u32[]{:S(2)}, u32[]{:S(2)}) collective-permute-start(f32[64,128]{1,0:T(8,128)S(1)} %get-tuple-element.33.zown_ref), channel_id=1, source_target_pairs={{0,1},{1,0},{2,3},{3,2},{4,5},{5,4},{6,7},{7,6},{8,9},{9,8},{10,11... | collective-permute-start | bytes 98312 | tf_op jit(solution)/shard_map/ppermute | solution.py:455
  23.9 0.7 %copy-start.4 = (s32[4,256]{1,0:T(4,128)S(1)}, s32[4,256]{1,0:T(4,128)}, u32[]{:S(2)}) copy-start(s32[4,256]{1,0:T(4,128)} %idx_ref.1) | copy-start | bytes 12292
  24.0 0.7 %copy-start.5 = (f32[6]{0:T(128)S(1)}, f32[6]{0:T(128)}, u32[]{:S(2)}) copy-start(f32[6]{0:T(128)} %light_ref.3) | copy-start | bytes 76
  24.0 0.7 %copy-start.7 = (f32[256]{0:T(256)S(1)}, f32[256]{0:T(256)}, u32[]{:S(2)}) copy-start(f32[256]{0:T(256)} %param.18) | copy-start | bytes 3076
  28.2 0.7 %copy-start.6 = (s32[1,1,1,4]{3,2,1,0:T(1,128)S(1)}, s32[1,1,1,4]{3,2,1,0:T(1,128)}, u32[]{:S(2)}) copy-start(s32[1,1,1,4]{3,2,1,0:T(1,128)} %param.21) | copy-start | bytes 52
  30.5 0.7 %copy-start.1 = (f32[3,4,4,128]{3,2,1,0:T(4,128)S(1)}, f32[3,4,4,128]{3,2,1,0:T(4,128)}, u32[]{:S(2)}) copy-start(f32[3,4,4,128]{3,2,1,0:T(4,128)} %param.13) | copy-start | bytes 73732
  38.7 9.2 %collective-permute-start.9 = (f32[1040,128]{1,0:T(8,128)S(1)}, f32[1040,128]{1,0:T(8,128)S(1)}, u32[]{:S(2)}, u32[]{:S(2)}) collective-permute-start(f32[1040,128]{1,0:T(8,128)S(1)} %get-tuple-element.47.n_ref), channel_id=1, source_target_pairs={{0,64},{64,0},{1,65},{65,1},{2,66},{66,2},{3,67},{67,3},{4,68},{68... | collective-permute-start | bytes 1597448 | tf_op jit(solution)/shard_map/ppermute | solution.py:497
  38.7 17.6 %collective-permute-start.10 = (f32[520,128]{1,0:T(8,128)S(1)}, f32[520,128]{1,0:T(8,128)S(1)}, u32[]{:S(2)}, u32[]{:S(2)}) collective-permute-start(f32[520,128]{1,0:T(8,128)S(1)} %get-tuple-element.48), channel_id=1, source_target_pairs={{0,2},{2,4},{4,6},{6,8},{8,10},{10,12},{12,14},{14,16},{16,18},{18... | collective-permute-start | bytes 798728 | tf_op jit(solution)/shard_map/ppermute | solution.py:495
  41.1 15.2 %collective-permute-start.11 = (f32[520,128]{1,0:T(8,128)S(1)}, f32[520,128]{1,0:T(8,128)S(1)}, u32[]{:S(2)}, u32[]{:S(2)}) collective-permute-start(f32[520,128]{1,0:T(8,128)S(1)} %get-tuple-element.49), channel_id=1, source_target_pairs={{0,62},{2,0},{4,2},{6,4},{8,6},{10,8},{12,10},{14,12},{16,14},{18,... | collective-permute-start | bytes 798728 | tf_op jit(solution)/shard_map/ppermute | solution.py:496
  46.4 9.8 %collective-permute-start.12 = (f32[80,128]{1,0:T(8,128)S(1)}, f32[80,128]{1,0:T(8,128)S(1)}, u32[]{:S(2)}, u32[]{:S(2)}) collective-permute-start(f32[80,128]{1,0:T(8,128)S(1)} %get-tuple-element.50.zs_ref), channel_id=1, source_target_pairs={{0,1},{1,0},{2,3},{3,2},{4,5},{5,4},{6,7},{7,6},{8,9},{9,8},{10,11... | collective-permute-start | bytes 122888 | tf_op jit(solution)/shard_map/ppermute | solution.py:498

commit v4 on v3

--- a/solution.py
+++ b/solution.py
@@ -73,7 +73,7 @@
 
 def local_kernel(
     light_ref, n2_ref, temp_ref, opt_ref, idx_ref, exo_ref, coef_ref, bar_ref, em_ref,
-    ost_ref, g2_ref, pg_ref, lt_ref, lp_ref, cb_ref,
+    ost_ref, g2_ref, pg_ref, cb_ref,
     made_ref, lost_ref, heat_ref, den_ref, na_ref, yl_ref, yu_ref, zc_ref,
 ):
     op_hi, op_lo = split(opt_ref[...])
@@ -88,8 +88,11 @@
     g2 = jnp.concatenate([hot[:, q * 128 : (q + 1) * 128].T for q in range(3)], axis=0)
     g2 = g2.astype(BF16)
     g2_ref[...] = g2
-    rows = lax.broadcasted_iota(jnp.int32, (80, 256), 0)
+    rows = lax.broadcasted_iota(jnp.int32, (144, 256), 0)
+    lanes = lax.broadcasted_iota(jnp.int32, (144, 256), 1)
     made = jnp.where(rows == c, 1.0, 0.0) + jnp.where(rows == e, 1.0, 0.0)
+    made = made + jnp.where(rows - 80 == a, 1.0, 0.0)
+    made = made + jnp.where(jnp.logical_and(rows - 80 == b, lanes >= PHOTON), 1.0, 0.0)
     exo_hi, exo_lo = split(exo_ref[...])
     made = jnp.where(rows == 64, exo_hi.astype(F32), made)
     made = jnp.where(rows == 65, exo_lo.astype(F32), made)
@@ -98,9 +101,6 @@
     rows = lax.broadcasted_iota(jnp.int32, (KINDS, 256), 0)
     lt = jnp.where(rows == wide([a[:, PHOTON:], b[:, PHOTON:]]), 1.0, 0.0)
     lt = wide([lt, lt]).astype(BF16)
-    lt_ref[...] = lt
-    lp = jnp.where(rows[:, :PHOTON] == a[:, :PHOTON], 1.0, 0.0)
-    lp_ref[...] = wide([lp, lp]).astype(BF16)
     coef = jnp.broadcast_to(coef_ref[...], (LANES, LANES)).T
     bar = jnp.broadcast_to(bar_ref[...] * (-LOG2E), (LANES, LANES)).T
     em = jnp.broadcast_to(em_ref[...], (LANES, KINDS)).T
@@ -111,7 +111,7 @@
     k_out = lax.broadcasted_iota(jnp.int32, (2 * LANES, LANES), 1)
     uu = jnp.where(k_in < k_out, 1.0, jnp.where(k_in == k_out, 0.5, 0.0)).astype(BF16)
     coef, bar, em = wide([coef, coef]), wide([bar, bar]), wide([em, em])
-    pgt = wide([pg[:, 128:256], pg[:, 384:512]])
+    pgt = wide([pg[:80, 128:256], pg[:80, 384:512]])
 
     def four(i, carry):
         base = i * 4
@@ -161,9 +161,11 @@
     return jnp.concatenate(parts, axis=1)
 
 
-def early_kernel(light_ref, listed_ref, n2_ref, zc_ref, xown_ref, xpay_ref, zown_ref, zpay_ref, ost_ref, pe_ref):
+def early_kernel(light_ref, listed_ref, n2_ref, zc_ref, xown_ref, xpay_ref, zown_ref, zpay_ref, ost_ref, pe_ref, list_out):
     gx = lax.axis_index("gx").astype(F32)
     gz = lax.axis_index("gz").astype(F32)
+    for m in range(MAXD):
+        list_out[m : m + 1, :] = jnp.full((1, LANES), listed_ref[m], jnp.int32)
     ost = ost_ref[...]
     zsum = zown_ref[pl.ds(0, KINDS), :] + zpay_ref[pl.ds(0, KINDS), :]
     zlow = gz * zpay_ref[pl.ds(0, KINDS), :]
@@ -188,10 +190,10 @@
 def chemistry_kernel(
     listed_ref,
     n2_ref, temp_ref, v_ref, ty_ref, below_ref, plane_ref, flip_ref, turn_ref, both_ref, pe_ref,
-    ost_ref, g2_ref, pg_ref, lt_ref, lp_ref, cb_ref,
+    ost_ref, g2_ref, pg_ref, cb_ref,
     made_ref, lost_ref, heat_ref, den_ref, na_ref, yl_ref, yu_ref,
     n_out, temp_out, up_out, dn_out, z_out,
-    ph_ref, ll_ref, cur_ref, curt_ref,
+    ph_ref, cur_ref, curt_ref,
 ):
     near_z, far_z = later(8, 2, 1), later(8, 4, 2)
     ost = ost_ref[...]
@@ -206,7 +208,6 @@
             t = i * 4 + j
             ph_ref[t] = pe_ref[t] + (yl_ref[t] * far[:, :LANES] + yu_ref[t] * far[:, LANES:])
 
-    lp = lp_ref[...]
     pgp = wide([pg_ref[:, 0:128], pg_ref[:, 256:384]])
 
     def quiet(c, carry):
@@ -214,16 +215,15 @@
         for p in range(2):
             a = base + 2 * p
             ph = wide([ph_ref[a], ph_ref[a + 1]])
-            ll = dot(lp, jnp.concatenate(split(ph), axis=0))
             na = wide([na_ref[a], na_ref[a + 1]])
             made = dot(pgp, jnp.concatenate(split(ph * na), axis=0))
             heat = made[64:65] + made[65:66]
             for q in range(2):
                 cut = slice(q * LANES, (q + 1) * LANES)
-                ll_ref[a + q] = ll[:, cut]
-                n_out[pl.ds(pl.multiple_of((a + q) * KINDS, KINDS), KINDS), :] = (n2_ref[a + q] + (made_ref[a + q] + made[:64, cut])) / (
-                    lost_ref[a + q] + ll[:, cut]
-                )
+                n = n2_ref[a + q]
+                n_out[pl.ds(pl.multiple_of((a + q) * KINDS, KINDS), KINDS), :] = (
+                    n * (n + (made_ref[a + q] + made[:64, cut]))
+                ) / (lost_ref[a + q] * n + made[80:, cut])
                 row = pl.ds(a + q, 1)
                 temp_out[row, :] = (temp_ref[row, :] + (heat_ref[row, :] + heat[:, cut])) / (
                     den_ref[row, :]
@@ -232,11 +232,12 @@
 
     lax.fori_loop(0, 4, quiet, 0)
 
-    pick = [jnp.minimum(listed_ref[m], TILES - 1) for m in range(MAXD)]
+    listed = [listed_ref[m, 0] for m in range(MAXD)]
+    pick = [jnp.minimum(listed[m], TILES - 1) for m in range(MAXD)]
     for m in range(MAXD):
         cur_ref[m] = n2_ref[pick[m]]
         curt_ref[pl.ds(m, 1), :] = temp_ref[pl.ds(pick[m], 1), :]
-    g2, pg, lt = g2_ref[...], pg_ref[...], lt_ref[...]
+    g2, pg = g2_ref[...], pg_ref[...]
     coef = cb_ref[pl.ds(0, LANES), :]
     bar = cb_ref[pl.ds(LANES, LANES), :]
     em = cb_ref[pl.ds(2 * LANES, KINDS), :]
@@ -249,18 +250,15 @@
             n = wide([cur_ref[a], cur_ref[b]])
             temp = wide([curt_ref[a : a + 1, :], curt_ref[b : b + 1, :]])
             ph = wide([ph_ref[pick[a]], ph_ref[pick[b]]])
-            ll = wide([ll_ref[pick[a]], ll_ref[pick[b]]])
             th = coef * jnp.exp2(bar * (1.0 / temp))
             gat = dot(g2, jnp.concatenate(split(n), axis=0))
-            kb = th * gat[256:384]
-            ka = th * gat[128:256]
-            rate = jnp.concatenate([ph * gat[:128], kb * gat[128:256]], axis=0)
-            rem = jnp.concatenate([kb, ka], axis=0)
+            rate = jnp.concatenate(
+                [ph * gat[:128], th * gat[128:256] * gat[256:384]], axis=0
+            )
             made = dot(pg, jnp.concatenate(split(rate), axis=0))
-            lost = dot(lt, jnp.concatenate(split(rem), axis=0)) + ll
             heat = made[64:65] + made[65:66]
             cool = jnp.sum(em * n, axis=0, keepdims=True)
-            nn = (n + h * made[:64]) / (1.0 + h * lost)
+            nn = (n * (n + h * made[:64])) / (n + h * made[80:])
             tt = (temp + h * heat) / (1.0 + h * cool)
             cur_ref[a] = nn[:, :LANES]
             cur_ref[b] = nn[:, LANES:]
@@ -272,7 +270,7 @@
 
     for m in range(MAXD):
 
-        @pl.when(listed_ref[m] < TILES)
+        @pl.when(listed[m] < TILES)
         def _():
             n_out[pl.ds(pl.multiple_of(pick[m] * KINDS, KINDS), KINDS), :] = cur_ref[m]
             temp_out[pl.ds(pick[m], 1), :] = curt_ref[m : m + 1, :]
@@ -460,11 +458,11 @@
 
     big = (TILES, PHOTON, LANES)
     mid = (TILES, KINDS, LANES)
-    (ost, g2, pg, lt, lp, cb, made, lost, heat, den, na, yl, yu, zc) = call(
+    (ost, g2, pg, cb, made, lost, heat, den, na, yl, yu, zc) = call(
         local_kernel,
         (
-            vm(128, 192, dtype=BF16), vm(384, 128, dtype=BF16), vm(80, 512, dtype=BF16),
-            vm(64, 512, dtype=BF16), vm(64, 256, dtype=BF16), vm(320, LANES),
+            vm(128, 192, dtype=BF16), vm(384, 128, dtype=BF16), vm(144, 512, dtype=BF16),
+            vm(320, LANES),
             vm(*mid), vm(*mid), vm(TILES, LANES), vm(TILES, LANES), vm(*big), vm(*big),
             vm(*big), vm(TILES * KINDS, LANES),
         ),
@@ -474,20 +472,20 @@
             arrhenius_coefficient[None], arrhenius_barrier[None], emission_loss[None],
         ],
     )
-    pe = call(
-        early_kernel, vm(*big), [illumination, listed],
+    pe, tiles = call(
+        early_kernel, (vm(*big), vm(8, LANES, dtype=jnp.int32)), [illumination, listed],
         [n2, zc, xown, xpay, zown, zpay, ost],
     )
     n_new, temp_new, up, dn, zs = call(
         chemistry_kernel,
-        (vm(1040, LANES), hbm(TILES, LANES), vm(520, LANES), vm(520, LANES), vm(80, LANES)),
-        [listed],
+        (vm(1040, LANES), vm(TILES, LANES), vm(520, LANES), vm(520, LANES), vm(80, LANES)),
+        [],
         [
-            n2, temp, v, ty, below, plane, *z_parts, pe, ost, g2, pg, lt, lp, cb,
+            tiles, n2, temp, v, ty, below, plane, *z_parts, pe, ost, g2, pg, cb,
             made, lost, heat, den, na, yl, yu,
         ],
         [
-            pltpu.VMEM(big, F32), pltpu.VMEM(mid, F32),
+            pltpu.VMEM(big, F32),
             pltpu.VMEM((MAXD, KINDS, LANES), F32), pltpu.VMEM((8, LANES), F32),
         ],
     )

time: 58.6 us -> 58.8 us (level)
  waiting for transfers between devices: 16.8 us -> 16.1 us
  local copies, waits for them, and re-layouts: 3.07 us -> 3.67 us
    ppermute x1, waiting for transfers between devices: 6.92 us -> 6.24 us  [shards(): hz = near(lax.ppermute(zs, 'gz', around(lax.axis_size('gz'), 1)))]
    unnamed x22 -> x23, local copies, waits for them, and re-layouts: 3.07 us -> 3.67 us
  transfers between devices with their start and end apart: 13 -> 13, of which waited for: 5 -> 5; matrix products, arithmetic and copies ran while one was open for 0% -> 1% of each run, Pallas kernels for 11% -> 11%
where the time goes in v4:
time: 58.8 us; the launch traced here: 57.9 us
  starting transfers between devices  21.4 us (36%)
  waiting for transfers between devices  16.1 us (27%)
  Pallas kernels  15.9 us (27%)
  local copies, waits for them, and re-layouts  3.67 us (6%)
  between operations  0.8 us (1%)
    pallas_call x8, Pallas kernels, call(): pl.pallas_call(kernel, out_shape=out_shape, in_specs=[SM] * len(scalars)...  15.9 us
    ppermute x7, starting transfers between devices, send(): return near(lax.ppermute(value, 'gy', [(a, to(a)) for a in range(size)]))  11.5 us
    ppermute x7, waiting for transfers between devices, send(): return near(lax.ppermute(value, 'gy', [(a, to(a)) for a in range(size)]))  9.84 us
    ppermute x1, waiting for transfers between devices, shards(): hz = near(lax.ppermute(zs, 'gz', around(lax.axis_size('gz'), 1)))  6.24 us
    ppermute x1, starting transfers between devices, shards(): high = near(lax.ppermute(dn, 'gy', around(size, -1)))  5.34 us
    unnamed x23, local copies, waits for them, and re-layouts  3.67 us
    ppermute x1, starting transfers between devices, shards(): low = near(lax.ppermute(up, 'gy', around(size, 1)))  2.48 us
    ppermute x1, starting transfers between devices, shards(): hz = near(lax.ppermute(zs, 'gz', around(lax.axis_size('gz'), 1)))  1.49 us
  transfers between devices with their start and end apart: 13, of which 5 were waited for; matrix products, arithmetic and copies ran while one was open for 1% of the time, Pallas kernels for 11%

profile of v4, /device:TPU:2, one launch (start us, length us, event | category | flops | bytes accessed | tf_op | source)
XLA Modules:
  0.0 57.9 jit_solution(17988401883349109689)
XLA Ops:
  0.6 1.0 %copy-done = f32[64,4,4,128]{3,2,1,0:T(4,128)S(1)} copy-done((f32[64,4,4,128]{3,2,1,0:T(4,128)S(1)}, f32[64,4,4,128]{3,2,1,0:T(4,128)}, u32[]{:S(2)}) %copy-start) | copy-done | bytes 524312
  1.7 0.3 shard_map.122
  2.0 2.2 %collective-permute-start.2 = (f32[256,128]{1,0:T(8,128)S(1)}, f32[256,128]{1,0:T(8,128)S(1)}, u32[]{:S(2)}, u32[]{:S(2)}) collective-permute-start(f32[256,128]{1,0:T(8,128)S(1)} %get-tuple-element.33.own_ref.ty_ref), channel_id=1, source_target_pairs={{0,2},{2,0},{4,6},{6,4},{8,10},{10,8},{12,14},{14,12},{16,18},{18,... | collective-permute-start | bytes 393224 | tf_op jit(solution)/shard_map/ppermute | solution.py:445
  4.2 4.6 %collective-permute-done.2.other_ref = f32[256,128]{1,0:T(8,128)S(1)} collective-permute-done((f32[256,128]{1,0:T(8,128)S(1)}, f32[256,128]{1,0:T(8,128)S(1)}, u32[]{:S(2)}, u32[]{:S(2)}) %collective-permute-start.2) | collective-permute-done | bytes 131104 | tf_op jit(solution)/shard_map/ppermute | solution.py:445
  8.8 3.3 %collective-permute-start.5 = (f32[256,128]{1,0:T(8,128)S(1)}, f32[256,128]{1,0:T(8,128)S(1)}, u32[]{:S(2)}, u32[]{:S(2)}) collective-permute-start(f32[256,128]{1,0:T(8,128)S(1)} %shard_map.125.pair_ref), channel_id=1, source_target_pairs={{0,8},{2,10},{4,12},{6,14},{8,0},{10,2},{12,4},{14,6},{16,24},{18,... | collective-permute-start | bytes 393224 | tf_op jit(solution)/shard_map/ppermute | solution.py:445
  12.1 1.1 %collective-permute-start.4 = (f32[256,128]{1,0:T(8,128)S(1)}, f32[256,128]{1,0:T(8,128)S(1)}, u32[]{:S(2)}, u32[]{:S(2)}) collective-permute-start(f32[256,128]{1,0:T(8,128)S(1)} %shard_map.125.pair_ref), channel_id=1, source_target_pairs={{0,12},{2,14},{4,8},{6,10},{8,4},{10,6},{12,0},{14,2},{16,28},{18,... | collective-permute-start | bytes 393224 | tf_op jit(solution)/shard_map/ppermute | solution.py:445
  13.1 2.3 %collective-permute-done.5.both_ref = f32[256,128]{1,0:T(8,128)S(1)} collective-permute-done((f32[256,128]{1,0:T(8,128)S(1)}, f32[256,128]{1,0:T(8,128)S(1)}, u32[]{:S(2)}, u32[]{:S(2)}) %collective-permute-start.5) | collective-permute-done | bytes 131104 | tf_op jit(solution)/shard_map/ppermute | solution.py:445
  15.4 2.8 %collective-permute-done.4.turn_ref = f32[256,128]{1,0:T(8,128)S(1)} collective-permute-done((f32[256,128]{1,0:T(8,128)S(1)}, f32[256,128]{1,0:T(8,128)S(1)}, u32[]{:S(2)}, u32[]{:S(2)}) %collective-permute-start.4) | collective-permute-done | bytes 131104 | tf_op jit(solution)/shard_map/ppermute | solution.py:445
  18.2 0.1 collective-permute-done.3.flip_ref
  18.4 0.1 shard_map.126
  18.4 0.0 copy-start.2
  18.4 4.0 %collective-permute-start.8 = (f32[256,128]{1,0:T(8,128)S(1)}, f32[256,128]{1,0:T(8,128)S(1)}, u32[]{:S(2)}, u32[]{:S(2)}) collective-permute-start(f32[256,128]{1,0:T(8,128)S(1)} %get-tuple-element.35.plane_ref), channel_id=1, source_target_pairs={{0,32},{2,34},{4,36},{6,38},{8,40},{10,42},{12,44},{14,46},{16,48}... | collective-permute-start | bytes 393224 | tf_op jit(solution)/shard_map/ppermute | solution.py:445
  22.4 0.7 %collective-permute-start.7 = (f32[256,128]{1,0:T(8,128)S(1)}, f32[256,128]{1,0:T(8,128)S(1)}, u32[]{:S(2)}, u32[]{:S(2)}) collective-permute-start(f32[256,128]{1,0:T(8,128)S(1)} %get-tuple-element.35.plane_ref), channel_id=1, source_target_pairs={{0,48},{2,50},{4,52},{6,54},{8,56},{10,58},{12,60},{14,62},{16,32}... | collective-permute-start | bytes 393224 | tf_op jit(solution)/shard_map/ppermute | solution.py:445
  23.1 0.3 collective-permute-start.6
  23.4 0.5 collective-permute-start.1
  24.0 0.6 %copy-done.4 = s32[4,256]{1,0:T(4,128)S(1)} copy-done((s32[4,256]{1,0:T(4,128)S(1)}, s32[4,256]{1,0:T(4,128)}, u32[]{:S(2)}) %copy-start.4) | copy-done | bytes 4120
  24.6 0.0 copy-done.6
  24.7 3.5 %shard_map.123 = (bf16[128,192]{1,0:T(8,128)(2,1)S(1)}, bf16[384,128]{1,0:T(8,128)(2,1)S(1)}, bf16[144,512]{1,0:T(8,128)(2,1)S(1)}, f32[320,128]{1,0:T(8,128)S(1...) custom-call(f32[6]{0:T(128)S(1)} %copy-done.5, ...), custom_call_target="tpu_custom_call" | custom-call | tf_op jit(solution)/shard_map/pallas_call | solution.py:416
  28.2 0.0 copy-start.7
  28.2 0.6 %copy-done.7 = s32[1,1,1,4]{3,2,1,0:T(1,128)S(1)} copy-done((s32[1,1,1,4]{3,2,1,0:T(1,128)S(1)}, s32[1,1,1,4]{3,2,1,0:T(1,128)}, u32[]{:S(2)}) %copy-start.7) | copy-done | bytes 40
  28.8 1.7 %shard_map.124 = (f32[16,128,128]{2,1,0:T(8,128)S(1)}, s32[8,128]{1,0:T(8,128)S(1)}) custom-call(f32[6]{0:T(128)S(1)} %copy-done.5, s32[4]{0:T(128)S(1)} %bitcast.20, f32[16,64,128]{2,1,0:T(8,128)S(1)} %get-tuple-element.27.n2_ref, f32[1024,128]{1,0:T(8,128)S(1)} %get-tuple-element.28.zc_ref, f32[256,128]{1,0:T(8,128)S(1)} %get-tuple-element.29.xown_ref, ...), custom_call_target="tpu_custom_call" | custom-call | tf_op jit(solution)/shard_map/pallas_call | solution.py:416
  30.5 0.0 copy-start.1
  30.6 0.7 %copy-done.1 = f32[3,4,4,128]{3,2,1,0:T(4,128)S(1)} copy-done((f32[3,4,4,128]{3,2,1,0:T(4,128)S(1)}, f32[3,4,4,128]{3,2,1,0:T(4,128)}, u32[]{:S(2)}) %copy-start.1) | copy-done | bytes 24600
  31.3 7.5 %shard_map.127 = (f32[1040,128]{1,0:T(8,128)S(1)}, f32[16,128]{1,0:T(8,128)S(1)}, f32[520,128]{1,0:T(8,128)S(1)}, f32[520,128]{1,0:T(8,128)S(1)}, f32[80,128]{1,0:T(8,128)S(1)}) custom-call(s32[8,128]{1,0:T(8,128)S(1)} %get-tuple-element.32.listed_ref, f32[16,64,128]{2,1,0:T(8,128)S(1)} %get-tuple-element.27.n2_ref, f32[16,128]{1,0:T(8,128)S(1)} %bitcast.17, ...), custom_call_target="tpu_custom_call" | custom-call | tf_op jit(solution)/shard_map/pallas_call | solution.py:416
  38.8 0.1 collective-permute-start.9
  38.8 2.5 %collective-permute-start.10 = (f32[520,128]{1,0:T(8,128)S(1)}, f32[520,128]{1,0:T(8,128)S(1)}, u32[]{:S(2)}, u32[]{:S(2)}) collective-permute-start(f32[520,128]{1,0:T(8,128)S(1)} %get-tuple-element.48), channel_id=1, source_target_pairs={{0,2},{2,4},{4,6},{6,8},{8,10},{10,12},{12,14},{14,16},{16,18},{18... | collective-permute-start | bytes 798728 | tf_op jit(solution)/shard_map/ppermute | solution.py:493
  41.3 5.3 %collective-permute-start.11 = (f32[520,128]{1,0:T(8,128)S(1)}, f32[520,128]{1,0:T(8,128)S(1)}, u32[]{:S(2)}, u32[]{:S(2)}) collective-permute-start(f32[520,128]{1,0:T(8,128)S(1)} %get-tuple-element.49), channel_id=1, source_target_pairs={{0,62},{2,0},{4,2},{6,4},{8,6},{10,8},{12,10},{14,12},{16,14},{18,... | collective-permute-start | bytes 798728 | tf_op jit(solution)/shard_map/ppermute | solution.py:494
  46.7 1.5 %collective-permute-start.12 = (f32[80,128]{1,0:T(8,128)S(1)}, f32[80,128]{1,0:T(8,128)S(1)}, u32[]{:S(2)}, u32[]{:S(2)}) collective-permute-start(f32[80,128]{1,0:T(8,128)S(1)} %get-tuple-element.50.zs_ref), channel_id=1, source_target_pairs={{0,1},{1,0},{2,3},{3,2},{4,5},{5,4},{6,7},{7,6},{8,9},{9,8},{10,11... | collective-permute-start | bytes 122888 | tf_op jit(solution)/shard_map/ppermute | solution.py:496
  48.2 0.6 %copy.13 = f32[4,4,128]{2,1,0:T(4,128)} copy(f32[4,4,128]{2,1,0:T(4,128)S(1)} %bitcast.11) | data formatting | bytes 16384
  48.8 1.4 %shard_map.128.acc_ref = f32[16,64,128]{2,1,0:T(8,128)S(1)} custom-call(f32[1040,128]{1,0:T(8,128)S(1)} %get-tuple-element.47.n_ref, f32[48,128]{1,0:T(8,128)S(1)} %bitcast.14, f32[1040,128]{1,0:T(8,128)S(1)} %collective-permute-done.9.hx_ref), custom_call_target="tpu_custom_call" | custom-call | tf_op jit(solution)/shard_map/pallas_call | solution.py:416
  50.2 6.2 %collective-permute-done.12.hz_ref = f32[80,128]{1,0:T(8,128)S(1)} collective-permute-done((f32[80,128]{1,0:T(8,128)S(1)}, f32[80,128]{1,0:T(8,128)S(1)}, u32[]{:S(2)}, u32[]{:S(2)}) %collective-permute-start.12) | collective-permute-done | bytes 40992 | tf_op jit(solution)/shard_map/ppermute | solution.py:496
  56.4 1.5 %shard_map.129 = f32[1024,128]{1,0:T(8,128)} custom-call(f32[1040,128]{1,0:T(8,128)S(1)} %get-tuple-element.47.n_ref, f32[16,64,128]{2,1,0:T(8,128)S(1)} %shard_map.128.acc_ref, f32[48,128]{1,0:T(8,128)S(1)} %bitcast.15, f32[520,128]{1,0:T(8,128)S(1)} %collective-permute-done.10.lo_ref, f32[520,128]{1,0:T(8,128)S(1)} %collective-permute-done.11.hi_ref, ...), custom_call_target="tpu_custom_call" | custom-call | tf_op jit(solution)/shard_map/pallas_call | solution.py:416
  (25 shorter events, 0.1 us)
Async XLA Ops:
  0.6 1.0 %copy-start = (f32[64,4,4,128]{3,2,1,0:T(4,128)S(1)}, f32[64,4,4,128]{3,2,1,0:T(4,128)}, u32[]{:S(2)}) copy-start(f32[64,4,4,128]{3,2,1,0:T(4,128)} %param.11) | copy-start | bytes 1572868
  2.0 6.8 %collective-permute-start.2 = (f32[256,128]{1,0:T(8,128)S(1)}, f32[256,128]{1,0:T(8,128)S(1)}, u32[]{:S(2)}, u32[]{:S(2)}) collective-permute-start(f32[256,128]{1,0:T(8,128)S(1)} %get-tuple-element.33.own_ref.ty_ref), channel_id=1, source_target_pairs={{0,2},{2,0},{4,6},{6,4},{8,10},{10,8},{12,14},{14,12},{16,18},{18,... | collective-permute-start | bytes 393224 | tf_op jit(solution)/shard_map/ppermute | solution.py:445
  8.8 6.6 %collective-permute-start.5 = (f32[256,128]{1,0:T(8,128)S(1)}, f32[256,128]{1,0:T(8,128)S(1)}, u32[]{:S(2)}, u32[]{:S(2)}) collective-permute-start(f32[256,128]{1,0:T(8,128)S(1)} %shard_map.125.pair_ref), channel_id=1, source_target_pairs={{0,8},{2,10},{4,12},{6,14},{8,0},{10,2},{12,4},{14,6},{16,24},{18,... | collective-permute-start | bytes 393224 | tf_op jit(solution)/shard_map/ppermute | solution.py:445
  12.1 6.2 %collective-permute-start.4 = (f32[256,128]{1,0:T(8,128)S(1)}, f32[256,128]{1,0:T(8,128)S(1)}, u32[]{:S(2)}, u32[]{:S(2)}) collective-permute-start(f32[256,128]{1,0:T(8,128)S(1)} %shard_map.125.pair_ref), channel_id=1, source_target_pairs={{0,12},{2,14},{4,8},{6,10},{8,4},{10,6},{12,0},{14,2},{16,28},{18,... | collective-permute-start | bytes 393224 | tf_op jit(solution)/shard_map/ppermute | solution.py:445
  13.1 5.2 %collective-permute-start.3 = (f32[256,128]{1,0:T(8,128)S(1)}, f32[256,128]{1,0:T(8,128)S(1)}, u32[]{:S(2)}, u32[]{:S(2)}) collective-permute-start(f32[256,128]{1,0:T(8,128)S(1)} %shard_map.125.pair_ref), channel_id=1, source_target_pairs={{0,4},{2,6},{4,0},{6,2},{8,12},{10,14},{12,8},{14,10},{16,20},{18,... | collective-permute-start | bytes 393224 | tf_op jit(solution)/shard_map/ppermute | solution.py:445
  13.1 15.0 %collective-permute-start = (f32[256,128]{1,0:T(8,128)S(1)}, f32[256,128]{1,0:T(8,128)S(1)}, u32[]{:S(2)}, u32[]{:S(2)}) collective-permute-start(f32[256,128]{1,0:T(8,128)S(1)} %get-tuple-element.29.xown_ref), channel_id=1, source_target_pairs={{0,64},{64,0},{1,65},{65,1},{2,66},{66,2},{3,67},{67,3},{4,68},{68... | collective-permute-start | bytes 393224 | tf_op jit(solution)/shard_map/ppermute | solution.py:452
  18.4 5.6 %copy-start.3 = (f32[128,64]{0,1:T(8,128)S(1)}, f32[128,64]{0,1:T(8,128)}, u32[]{:S(2)}) copy-start(f32[128,64]{0,1:T(8,128)} %param.14) | copy-start | bytes 98308
  18.4 5.6 %copy-start.8 = (f32[128]{0:T(128)S(1)}, f32[128]{0:T(128)}, u32[]{:S(2)}) copy-start(f32[128]{0:T(128)} %param.16) | copy-start | bytes 1540
  18.4 5.6 %copy-start.9 = (f32[128]{0:T(128)S(1)}, f32[128]{0:T(128)}, u32[]{:S(2)}) copy-start(f32[128]{0:T(128)} %param.17) | copy-start | bytes 1540
  18.4 5.6 %copy-start.10 = (f32[64]{0:T(128)S(1)}, f32[64]{0:T(128)}, u32[]{:S(2)}) copy-start(f32[64]{0:T(128)} %param.19) | copy-start | bytes 772
  18.4 5.6 %copy-start.2 = (f32[4,4,128]{2,1,0:T(4,128)S(1)}, f32[4,4,128]{2,1,0:T(4,128)}, u32[]{:S(2)}) copy-start(f32[4,4,128]{2,1,0:T(4,128)} %param.12) | copy-start | bytes 24580
  18.4 12.1 %collective-permute-start.8 = (f32[256,128]{1,0:T(8,128)S(1)}, f32[256,128]{1,0:T(8,128)S(1)}, u32[]{:S(2)}, u32[]{:S(2)}) collective-permute-start(f32[256,128]{1,0:T(8,128)S(1)} %get-tuple-element.35.plane_ref), channel_id=1, source_target_pairs={{0,32},{2,34},{4,36},{6,38},{8,40},{10,42},{12,44},{14,46},{16,48}... | collective-permute-start | bytes 393224 | tf_op jit(solution)/shard_map/ppermute | solution.py:445
  22.4 8.1 %collective-permute-start.7 = (f32[256,128]{1,0:T(8,128)S(1)}, f32[256,128]{1,0:T(8,128)S(1)}, u32[]{:S(2)}, u32[]{:S(2)}) collective-permute-start(f32[256,128]{1,0:T(8,128)S(1)} %get-tuple-element.35.plane_ref), channel_id=1, source_target_pairs={{0,48},{2,50},{4,52},{6,54},{8,56},{10,58},{12,60},{14,62},{16,32}... | collective-permute-start | bytes 393224 | tf_op jit(solution)/shard_map/ppermute | solution.py:445
  23.1 7.4 %collective-permute-start.6 = (f32[256,128]{1,0:T(8,128)S(1)}, f32[256,128]{1,0:T(8,128)S(1)}, u32[]{:S(2)}, u32[]{:S(2)}) collective-permute-start(f32[256,128]{1,0:T(8,128)S(1)} %get-tuple-element.35.plane_ref), channel_id=1, source_target_pairs={{0,16},{2,18},{4,20},{6,22},{8,24},{10,26},{12,28},{14,30},{16,0},... | collective-permute-start | bytes 393224 | tf_op jit(solution)/shard_map/ppermute | solution.py:445
  23.4 4.7 %collective-permute-start.1 = (f32[64,128]{1,0:T(8,128)S(1)}, f32[64,128]{1,0:T(8,128)S(1)}, u32[]{:S(2)}, u32[]{:S(2)}) collective-permute-start(f32[64,128]{1,0:T(8,128)S(1)} %get-tuple-element.30.zown_ref), channel_id=1, source_target_pairs={{0,1},{1,0},{2,3},{3,2},{4,5},{5,4},{6,7},{7,6},{8,9},{9,8},{10,11... | collective-permute-start | bytes 98312 | tf_op jit(solution)/shard_map/ppermute | solution.py:453
  23.9 0.7 %copy-start.4 = (s32[4,256]{1,0:T(4,128)S(1)}, s32[4,256]{1,0:T(4,128)}, u32[]{:S(2)}) copy-start(s32[4,256]{1,0:T(4,128)} %idx_ref.1) | copy-start | bytes 12292
  24.0 0.7 %copy-start.5 = (f32[6]{0:T(128)S(1)}, f32[6]{0:T(128)}, u32[]{:S(2)}) copy-start(f32[6]{0:T(128)} %light_ref.3) | copy-start | bytes 76
  24.0 0.7 %copy-start.6 = (f32[256]{0:T(256)S(1)}, f32[256]{0:T(256)}, u32[]{:S(2)}) copy-start(f32[256]{0:T(256)} %param.18) | copy-start | bytes 3076
  28.2 0.7 %copy-start.7 = (s32[1,1,1,4]{3,2,1,0:T(1,128)S(1)}, s32[1,1,1,4]{3,2,1,0:T(1,128)}, u32[]{:S(2)}) copy-start(s32[1,1,1,4]{3,2,1,0:T(1,128)} %param.21) | copy-start | bytes 52
  30.5 0.7 %copy-start.1 = (f32[3,4,4,128]{3,2,1,0:T(4,128)S(1)}, f32[3,4,4,128]{3,2,1,0:T(4,128)}, u32[]{:S(2)}) copy-start(f32[3,4,4,128]{3,2,1,0:T(4,128)} %param.13) | copy-start | bytes 73732
  38.8 10.0 %collective-permute-start.9 = (f32[1040,128]{1,0:T(8,128)S(1)}, f32[1040,128]{1,0:T(8,128)S(1)}, u32[]{:S(2)}, u32[]{:S(2)}) collective-permute-start(f32[1040,128]{1,0:T(8,128)S(1)} %get-tuple-element.47.n_ref), channel_id=1, source_target_pairs={{0,64},{64,0},{1,65},{65,1},{2,66},{66,2},{3,67},{67,3},{4,68},{68... | collective-permute-start | bytes 1597448 | tf_op jit(solution)/shard_map/ppermute | solution.py:495
  38.8 17.6 %collective-permute-start.10 = (f32[520,128]{1,0:T(8,128)S(1)}, f32[520,128]{1,0:T(8,128)S(1)}, u32[]{:S(2)}, u32[]{:S(2)}) collective-permute-start(f32[520,128]{1,0:T(8,128)S(1)} %get-tuple-element.48), channel_id=1, source_target_pairs={{0,2},{2,4},{4,6},{6,8},{8,10},{10,12},{12,14},{14,16},{16,18},{18... | collective-permute-start | bytes 798728 | tf_op jit(solution)/shard_map/ppermute | solution.py:493
  41.3 15.1 %collective-permute-start.11 = (f32[520,128]{1,0:T(8,128)S(1)}, f32[520,128]{1,0:T(8,128)S(1)}, u32[]{:S(2)}, u32[]{:S(2)}) collective-permute-start(f32[520,128]{1,0:T(8,128)S(1)} %get-tuple-element.49), channel_id=1, source_target_pairs={{0,62},{2,0},{4,2},{6,4},{8,6},{10,8},{12,10},{14,12},{16,14},{18,... | collective-permute-start | bytes 798728 | tf_op jit(solution)/shard_map/ppermute | solution.py:494
  46.7 9.8 %collective-permute-start.12 = (f32[80,128]{1,0:T(8,128)S(1)}, f32[80,128]{1,0:T(8,128)S(1)}, u32[]{:S(2)}, u32[]{:S(2)}) collective-permute-start(f32[80,128]{1,0:T(8,128)S(1)} %get-tuple-element.50.zs_ref), channel_id=1, source_target_pairs={{0,1},{1,0},{2,3},{3,2},{4,5},{5,4},{6,7},{7,6},{8,9},{9,8},{10,11... | collective-permute-start | bytes 122888 | tf_op jit(solution)/shard_map/ppermute | solution.py:496

commit v5 on v4

--- a/solution.py
+++ b/solution.py
@@ -245,25 +245,28 @@
     h = 1.0 / NSUB
 
     def substep(s, carry):
-        for p in range(2):
-            a, b = 2 * p, 2 * p + 1
-            n = wide([cur_ref[a], cur_ref[b]])
-            temp = wide([curt_ref[a : a + 1, :], curt_ref[b : b + 1, :]])
-            ph = wide([ph_ref[pick[a]], ph_ref[pick[b]]])
-            th = coef * jnp.exp2(bar * (1.0 / temp))
-            gat = dot(g2, jnp.concatenate(split(n), axis=0))
-            rate = jnp.concatenate(
-                [ph * gat[:128], th * gat[128:256] * gat[256:384]], axis=0
-            )
-            made = dot(pg, jnp.concatenate(split(rate), axis=0))
-            heat = made[64:65] + made[65:66]
-            cool = jnp.sum(em * n, axis=0, keepdims=True)
-            nn = (n * (n + h * made[:64])) / (n + h * made[80:])
-            tt = (temp + h * heat) / (1.0 + h * cool)
-            cur_ref[a] = nn[:, :LANES]
-            cur_ref[b] = nn[:, LANES:]
-            curt_ref[a : a + 1, :] = tt[:, :LANES]
-            curt_ref[b : b + 1, :] = tt[:, LANES:]
+        both = [(0, 1), (2, 3)]
+        n = [wide([cur_ref[a], cur_ref[b]]) for a, b in both]
+        temp = [wide([curt_ref[a : a + 1, :], curt_ref[b : b + 1, :]]) for a, b in both]
+        ph = [wide([ph_ref[pick[a]], ph_ref[pick[b]]]) for a, b in both]
+        gat = [dot(g2, jnp.concatenate(split(x), axis=0)) for x in n]
+        th = [coef * jnp.exp2(bar * (1.0 / x)) for x in temp]
+        light = [p * g[:128] for p, g in zip(ph, gat)]
+        dark = [t * g[128:256] * g[256:384] for t, g in zip(th, gat)]
+        made = [
+            dot(pg, jnp.concatenate(split(jnp.concatenate(x, axis=0)), axis=0))
+            for x in zip(light, dark)
+        ]
+        cool = [jnp.sum(em * x, axis=0, keepdims=True) for x in n]
+        new_n = [(x * (x + h * m[:64])) / (x + h * m[80:]) for x, m in zip(n, made)]
+        new_t = [
+            (t + h * (m[64:65] + m[65:66])) / (1.0 + h * c) for t, m, c in zip(temp, made, cool)
+        ]
+        for q, (a, b) in enumerate(both):
+            cur_ref[a] = new_n[q][:, :LANES]
+            cur_ref[b] = new_n[q][:, LANES:]
+            curt_ref[a : a + 1, :] = new_t[q][:, :LANES]
+            curt_ref[b : b + 1, :] = new_t[q][:, LANES:]
         return carry
 
     lax.fori_loop(0, NSUB, substep, 0)

time: 58.8 us -> 56.8 us (0.966)
  Pallas kernels: 15.9 us -> 13.9 us
    pallas_call x8, Pallas kernels: 15.9 us -> 13.9 us  [call(): pl.pallas_call(kernel, out_shape=out_shape, in_specs=[SM] * len(scalars)...]
  transfers between devices with their start and end apart: 13 -> 13, of which waited for: 5 -> 5; matrix products, arithmetic and copies ran while one was open for 1% -> 1% of each run, Pallas kernels for 11% -> 12%
where the time goes in v5:
time: 56.8 us; the launch traced here: 55.9 us
  starting transfers between devices  21.4 us (38%)
  waiting for transfers between devices  16.1 us (28%)
  Pallas kernels  13.9 us (24%)
  local copies, waits for them, and re-layouts  3.67 us (6%)
  between operations  0.8 us (1%)
    pallas_call x8, Pallas kernels, call(): pl.pallas_call(kernel, out_shape=out_shape, in_specs=[SM] * len(scalars)...  13.9 us
    ppermute x7, starting transfers between devices, send(): return near(lax.ppermute(value, 'gy', [(a, to(a)) for a in range(size)]))  11.5 us
    ppermute x7, waiting for transfers between devices, send(): return near(lax.ppermute(value, 'gy', [(a, to(a)) for a in range(size)]))  9.84 us
    ppermute x1, waiting for transfers between devices, shards(): hz = near(lax.ppermute(zs, 'gz', around(lax.axis_size('gz'), 1)))  6.24 us
    ppermute x1, starting transfers between devices, shards(): high = near(lax.ppermute(dn, 'gy', around(size, -1)))  5.33 us
    unnamed x23, local copies, waits for them, and re-layouts  3.67 us
    ppermute x1, starting transfers between devices, shards(): low = near(lax.ppermute(up, 'gy', around(size, 1)))  2.49 us
    ppermute x1, starting transfers between devices, shards(): hz = near(lax.ppermute(zs, 'gz', around(lax.axis_size('gz'), 1)))  1.49 us
  transfers between devices with their start and end apart: 13, of which 5 were waited for; matrix products, arithmetic and copies ran while one was open for 1% of the time, Pallas kernels for 12%

profile of v5, /device:TPU:2, one launch (start us, length us, event | category | flops | bytes accessed | tf_op | source)
XLA Modules:
  0.0 55.9 jit_solution(10501525276242188035)
XLA Ops:
  0.6 1.0 %copy-done = f32[64,4,4,128]{3,2,1,0:T(4,128)S(1)} copy-done((f32[64,4,4,128]{3,2,1,0:T(4,128)S(1)}, f32[64,4,4,128]{3,2,1,0:T(4,128)}, u32[]{:S(2)}) %copy-start) | copy-done | bytes 524312
  1.7 0.3 shard_map.122
  2.0 2.2 %collective-permute-start.2 = (f32[256,128]{1,0:T(8,128)S(1)}, f32[256,128]{1,0:T(8,128)S(1)}, u32[]{:S(2)}, u32[]{:S(2)}) collective-permute-start(f32[256,128]{1,0:T(8,128)S(1)} %get-tuple-element.33.own_ref.ty_ref), channel_id=1, source_target_pairs={{0,2},{2,0},{4,6},{6,4},{8,10},{10,8},{12,14},{14,12},{16,18},{18,... | collective-permute-start | bytes 393224 | tf_op jit(solution)/shard_map/ppermute | solution.py:448
  4.2 4.6 %collective-permute-done.2.other_ref = f32[256,128]{1,0:T(8,128)S(1)} collective-permute-done((f32[256,128]{1,0:T(8,128)S(1)}, f32[256,128]{1,0:T(8,128)S(1)}, u32[]{:S(2)}, u32[]{:S(2)}) %collective-permute-start.2) | collective-permute-done | bytes 131104 | tf_op jit(solution)/shard_map/ppermute | solution.py:448
  8.8 3.3 %collective-permute-start.5 = (f32[256,128]{1,0:T(8,128)S(1)}, f32[256,128]{1,0:T(8,128)S(1)}, u32[]{:S(2)}, u32[]{:S(2)}) collective-permute-start(f32[256,128]{1,0:T(8,128)S(1)} %shard_map.125.pair_ref), channel_id=1, source_target_pairs={{0,8},{2,10},{4,12},{6,14},{8,0},{10,2},{12,4},{14,6},{16,24},{18,... | collective-permute-start | bytes 393224 | tf_op jit(solution)/shard_map/ppermute | solution.py:448
  12.1 1.1 %collective-permute-start.4 = (f32[256,128]{1,0:T(8,128)S(1)}, f32[256,128]{1,0:T(8,128)S(1)}, u32[]{:S(2)}, u32[]{:S(2)}) collective-permute-start(f32[256,128]{1,0:T(8,128)S(1)} %shard_map.125.pair_ref), channel_id=1, source_target_pairs={{0,12},{2,14},{4,8},{6,10},{8,4},{10,6},{12,0},{14,2},{16,28},{18,... | collective-permute-start | bytes 393224 | tf_op jit(solution)/shard_map/ppermute | solution.py:448
  13.1 2.3 %collective-permute-done.5.both_ref = f32[256,128]{1,0:T(8,128)S(1)} collective-permute-done((f32[256,128]{1,0:T(8,128)S(1)}, f32[256,128]{1,0:T(8,128)S(1)}, u32[]{:S(2)}, u32[]{:S(2)}) %collective-permute-start.5) | collective-permute-done | bytes 131104 | tf_op jit(solution)/shard_map/ppermute | solution.py:448
  15.4 2.8 %collective-permute-done.4.turn_ref = f32[256,128]{1,0:T(8,128)S(1)} collective-permute-done((f32[256,128]{1,0:T(8,128)S(1)}, f32[256,128]{1,0:T(8,128)S(1)}, u32[]{:S(2)}, u32[]{:S(2)}) %collective-permute-start.4) | collective-permute-done | bytes 131104 | tf_op jit(solution)/shard_map/ppermute | solution.py:448
  18.2 0.1 collective-permute-done.3.flip_ref
  18.4 0.1 shard_map.126
  18.4 0.0 copy-start.2
  18.4 4.0 %collective-permute-start.8 = (f32[256,128]{1,0:T(8,128)S(1)}, f32[256,128]{1,0:T(8,128)S(1)}, u32[]{:S(2)}, u32[]{:S(2)}) collective-permute-start(f32[256,128]{1,0:T(8,128)S(1)} %get-tuple-element.35.plane_ref), channel_id=1, source_target_pairs={{0,32},{2,34},{4,36},{6,38},{8,40},{10,42},{12,44},{14,46},{16,48}... | collective-permute-start | bytes 393224 | tf_op jit(solution)/shard_map/ppermute | solution.py:448
  22.4 0.7 %collective-permute-start.7 = (f32[256,128]{1,0:T(8,128)S(1)}, f32[256,128]{1,0:T(8,128)S(1)}, u32[]{:S(2)}, u32[]{:S(2)}) collective-permute-start(f32[256,128]{1,0:T(8,128)S(1)} %get-tuple-element.35.plane_ref), channel_id=1, source_target_pairs={{0,48},{2,50},{4,52},{6,54},{8,56},{10,58},{12,60},{14,62},{16,32}... | collective-permute-start | bytes 393224 | tf_op jit(solution)/shard_map/ppermute | solution.py:448
  23.1 0.3 collective-permute-start.6
  23.4 0.5 collective-permute-start.1
  24.0 0.6 %copy-done.4 = s32[4,256]{1,0:T(4,128)S(1)} copy-done((s32[4,256]{1,0:T(4,128)S(1)}, s32[4,256]{1,0:T(4,128)}, u32[]{:S(2)}) %copy-start.4) | copy-done | bytes 4120
  24.6 0.0 copy-done.6
  24.7 3.5 %shard_map.123 = (bf16[128,192]{1,0:T(8,128)(2,1)S(1)}, bf16[384,128]{1,0:T(8,128)(2,1)S(1)}, bf16[144,512]{1,0:T(8,128)(2,1)S(1)}, f32[320,128]{1,0:T(8,128)S(1...) custom-call(f32[6]{0:T(128)S(1)} %copy-done.5, ...), custom_call_target="tpu_custom_call" | custom-call | tf_op jit(solution)/shard_map/pallas_call | solution.py:419
  28.2 0.0 copy-start.7
  28.2 0.6 %copy-done.7 = s32[1,1,1,4]{3,2,1,0:T(1,128)S(1)} copy-done((s32[1,1,1,4]{3,2,1,0:T(1,128)S(1)}, s32[1,1,1,4]{3,2,1,0:T(1,128)}, u32[]{:S(2)}) %copy-start.7) | copy-done | bytes 40
  28.8 1.7 %shard_map.124 = (f32[16,128,128]{2,1,0:T(8,128)S(1)}, s32[8,128]{1,0:T(8,128)S(1)}) custom-call(f32[6]{0:T(128)S(1)} %copy-done.5, s32[4]{0:T(128)S(1)} %bitcast.20, f32[16,64,128]{2,1,0:T(8,128)S(1)} %get-tuple-element.27.n2_ref, f32[1024,128]{1,0:T(8,128)S(1)} %get-tuple-element.28.zc_ref, f32[256,128]{1,0:T(8,128)S(1)} %get-tuple-element.29.xown_ref, ...), custom_call_target="tpu_custom_call" | custom-call | tf_op jit(solution)/shard_map/pallas_call | solution.py:419
  30.5 0.0 copy-start.1
  30.6 0.7 %copy-done.1 = f32[3,4,4,128]{3,2,1,0:T(4,128)S(1)} copy-done((f32[3,4,4,128]{3,2,1,0:T(4,128)S(1)}, f32[3,4,4,128]{3,2,1,0:T(4,128)}, u32[]{:S(2)}) %copy-start.1) | copy-done | bytes 24600
  31.3 5.5 %shard_map.127 = (f32[1040,128]{1,0:T(8,128)S(1)}, f32[16,128]{1,0:T(8,128)S(1)}, f32[520,128]{1,0:T(8,128)S(1)}, f32[520,128]{1,0:T(8,128)S(1)}, f32[80,128]{1,0:T(8,128)S(1)}) custom-call(s32[8,128]{1,0:T(8,128)S(1)} %get-tuple-element.32.listed_ref, f32[16,64,128]{2,1,0:T(8,128)S(1)} %get-tuple-element.27.n2_ref, f32[16,128]{1,0:T(8,128)S(1)} %bitcast.17, ...), custom_call_target="tpu_custom_call" | custom-call | tf_op jit(solution)/shard_map/pallas_call | solution.py:419
  36.7 0.1 collective-permute-start.9
  36.8 2.5 %collective-permute-start.10 = (f32[520,128]{1,0:T(8,128)S(1)}, f32[520,128]{1,0:T(8,128)S(1)}, u32[]{:S(2)}, u32[]{:S(2)}) collective-permute-start(f32[520,128]{1,0:T(8,128)S(1)} %get-tuple-element.48), channel_id=1, source_target_pairs={{0,2},{2,4},{4,6},{6,8},{8,10},{10,12},{12,14},{14,16},{16,18},{18... | collective-permute-start | bytes 798728 | tf_op jit(solution)/shard_map/ppermute | solution.py:496
  39.3 5.3 %collective-permute-start.11 = (f32[520,128]{1,0:T(8,128)S(1)}, f32[520,128]{1,0:T(8,128)S(1)}, u32[]{:S(2)}, u32[]{:S(2)}) collective-permute-start(f32[520,128]{1,0:T(8,128)S(1)} %get-tuple-element.49), channel_id=1, source_target_pairs={{0,62},{2,0},{4,2},{6,4},{8,6},{10,8},{12,10},{14,12},{16,14},{18,... | collective-permute-start | bytes 798728 | tf_op jit(solution)/shard_map/ppermute | solution.py:497
  44.7 1.5 %collective-permute-start.12 = (f32[80,128]{1,0:T(8,128)S(1)}, f32[80,128]{1,0:T(8,128)S(1)}, u32[]{:S(2)}, u32[]{:S(2)}) collective-permute-start(f32[80,128]{1,0:T(8,128)S(1)} %get-tuple-element.50.zs_ref), channel_id=1, source_target_pairs={{0,1},{1,0},{2,3},{3,2},{4,5},{5,4},{6,7},{7,6},{8,9},{9,8},{10,11... | collective-permute-start | bytes 122888 | tf_op jit(solution)/shard_map/ppermute | solution.py:499
  46.1 0.6 %copy.13 = f32[4,4,128]{2,1,0:T(4,128)} copy(f32[4,4,128]{2,1,0:T(4,128)S(1)} %bitcast.11) | data formatting | bytes 16384
  46.7 1.4 %shard_map.128.acc_ref = f32[16,64,128]{2,1,0:T(8,128)S(1)} custom-call(f32[1040,128]{1,0:T(8,128)S(1)} %get-tuple-element.47.n_ref, f32[48,128]{1,0:T(8,128)S(1)} %bitcast.14, f32[1040,128]{1,0:T(8,128)S(1)} %collective-permute-done.9.hx_ref), custom_call_target="tpu_custom_call" | custom-call | tf_op jit(solution)/shard_map/pallas_call | solution.py:419
  48.2 6.2 %collective-permute-done.12.hz_ref = f32[80,128]{1,0:T(8,128)S(1)} collective-permute-done((f32[80,128]{1,0:T(8,128)S(1)}, f32[80,128]{1,0:T(8,128)S(1)}, u32[]{:S(2)}, u32[]{:S(2)}) %collective-permute-start.12) | collective-permute-done | bytes 40992 | tf_op jit(solution)/shard_map/ppermute | solution.py:499
  54.4 1.5 %shard_map.129 = f32[1024,128]{1,0:T(8,128)} custom-call(f32[1040,128]{1,0:T(8,128)S(1)} %get-tuple-element.47.n_ref, f32[16,64,128]{2,1,0:T(8,128)S(1)} %shard_map.128.acc_ref, f32[48,128]{1,0:T(8,128)S(1)} %bitcast.15, f32[520,128]{1,0:T(8,128)S(1)} %collective-permute-done.10.lo_ref, f32[520,128]{1,0:T(8,128)S(1)} %collective-permute-done.11.hi_ref, ...), custom_call_target="tpu_custom_call" | custom-call | tf_op jit(solution)/shard_map/pallas_call | solution.py:419
  (25 shorter events, 0.1 us)
Async XLA Ops:
  0.6 1.0 %copy-start = (f32[64,4,4,128]{3,2,1,0:T(4,128)S(1)}, f32[64,4,4,128]{3,2,1,0:T(4,128)}, u32[]{:S(2)}) copy-start(f32[64,4,4,128]{3,2,1,0:T(4,128)} %param.11) | copy-start | bytes 1572868
  2.0 6.8 %collective-permute-start.2 = (f32[256,128]{1,0:T(8,128)S(1)}, f32[256,128]{1,0:T(8,128)S(1)}, u32[]{:S(2)}, u32[]{:S(2)}) collective-permute-start(f32[256,128]{1,0:T(8,128)S(1)} %get-tuple-element.33.own_ref.ty_ref), channel_id=1, source_target_pairs={{0,2},{2,0},{4,6},{6,4},{8,10},{10,8},{12,14},{14,12},{16,18},{18,... | collective-permute-start | bytes 393224 | tf_op jit(solution)/shard_map/ppermute | solution.py:448
  8.8 6.6 %collective-permute-start.5 = (f32[256,128]{1,0:T(8,128)S(1)}, f32[256,128]{1,0:T(8,128)S(1)}, u32[]{:S(2)}, u32[]{:S(2)}) collective-permute-start(f32[256,128]{1,0:T(8,128)S(1)} %shard_map.125.pair_ref), channel_id=1, source_target_pairs={{0,8},{2,10},{4,12},{6,14},{8,0},{10,2},{12,4},{14,6},{16,24},{18,... | collective-permute-start | bytes 393224 | tf_op jit(solution)/shard_map/ppermute | solution.py:448
  12.1 6.2 %collective-permute-start.4 = (f32[256,128]{1,0:T(8,128)S(1)}, f32[256,128]{1,0:T(8,128)S(1)}, u32[]{:S(2)}, u32[]{:S(2)}) collective-permute-start(f32[256,128]{1,0:T(8,128)S(1)} %shard_map.125.pair_ref), channel_id=1, source_target_pairs={{0,12},{2,14},{4,8},{6,10},{8,4},{10,6},{12,0},{14,2},{16,28},{18,... | collective-permute-start | bytes 393224 | tf_op jit(solution)/shard_map/ppermute | solution.py:448
  13.1 5.2 %collective-permute-start.3 = (f32[256,128]{1,0:T(8,128)S(1)}, f32[256,128]{1,0:T(8,128)S(1)}, u32[]{:S(2)}, u32[]{:S(2)}) collective-permute-start(f32[256,128]{1,0:T(8,128)S(1)} %shard_map.125.pair_ref), channel_id=1, source_target_pairs={{0,4},{2,6},{4,0},{6,2},{8,12},{10,14},{12,8},{14,10},{16,20},{18,... | collective-permute-start | bytes 393224 | tf_op jit(solution)/shard_map/ppermute | solution.py:448
  13.1 15.0 %collective-permute-start = (f32[256,128]{1,0:T(8,128)S(1)}, f32[256,128]{1,0:T(8,128)S(1)}, u32[]{:S(2)}, u32[]{:S(2)}) collective-permute-start(f32[256,128]{1,0:T(8,128)S(1)} %get-tuple-element.29.xown_ref), channel_id=1, source_target_pairs={{0,64},{64,0},{1,65},{65,1},{2,66},{66,2},{3,67},{67,3},{4,68},{68... | collective-permute-start | bytes 393224 | tf_op jit(solution)/shard_map/ppermute | solution.py:455
  18.4 5.6 %copy-start.3 = (f32[128,64]{0,1:T(8,128)S(1)}, f32[128,64]{0,1:T(8,128)}, u32[]{:S(2)}) copy-start(f32[128,64]{0,1:T(8,128)} %param.14) | copy-start | bytes 98308
  18.4 5.6 %copy-start.8 = (f32[128]{0:T(128)S(1)}, f32[128]{0:T(128)}, u32[]{:S(2)}) copy-start(f32[128]{0:T(128)} %param.16) | copy-start | bytes 1540
  18.4 5.6 %copy-start.9 = (f32[128]{0:T(128)S(1)}, f32[128]{0:T(128)}, u32[]{:S(2)}) copy-start(f32[128]{0:T(128)} %param.17) | copy-start | bytes 1540
  18.4 5.6 %copy-start.10 = (f32[64]{0:T(128)S(1)}, f32[64]{0:T(128)}, u32[]{:S(2)}) copy-start(f32[64]{0:T(128)} %param.19) | copy-start | bytes 772
  18.4 5.6 %copy-start.2 = (f32[4,4,128]{2,1,0:T(4,128)S(1)}, f32[4,4,128]{2,1,0:T(4,128)}, u32[]{:S(2)}) copy-start(f32[4,4,128]{2,1,0:T(4,128)} %param.12) | copy-start | bytes 24580
  18.4 12.1 %collective-permute-start.8 = (f32[256,128]{1,0:T(8,128)S(1)}, f32[256,128]{1,0:T(8,128)S(1)}, u32[]{:S(2)}, u32[]{:S(2)}) collective-permute-start(f32[256,128]{1,0:T(8,128)S(1)} %get-tuple-element.35.plane_ref), channel_id=1, source_target_pairs={{0,32},{2,34},{4,36},{6,38},{8,40},{10,42},{12,44},{14,46},{16,48}... | collective-permute-start | bytes 393224 | tf_op jit(solution)/shard_map/ppermute | solution.py:448
  22.4 8.1 %collective-permute-start.7 = (f32[256,128]{1,0:T(8,128)S(1)}, f32[256,128]{1,0:T(8,128)S(1)}, u32[]{:S(2)}, u32[]{:S(2)}) collective-permute-start(f32[256,128]{1,0:T(8,128)S(1)} %get-tuple-element.35.plane_ref), channel_id=1, source_target_pairs={{0,48},{2,50},{4,52},{6,54},{8,56},{10,58},{12,60},{14,62},{16,32}... | collective-permute-start | bytes 393224 | tf_op jit(solution)/shard_map/ppermute | solution.py:448
  23.1 7.4 %collective-permute-start.6 = (f32[256,128]{1,0:T(8,128)S(1)}, f32[256,128]{1,0:T(8,128)S(1)}, u32[]{:S(2)}, u32[]{:S(2)}) collective-permute-start(f32[256,128]{1,0:T(8,128)S(1)} %get-tuple-element.35.plane_ref), channel_id=1, source_target_pairs={{0,16},{2,18},{4,20},{6,22},{8,24},{10,26},{12,28},{14,30},{16,0},... | collective-permute-start | bytes 393224 | tf_op jit(solution)/shard_map/ppermute | solution.py:448
  23.4 4.7 %collective-permute-start.1 = (f32[64,128]{1,0:T(8,128)S(1)}, f32[64,128]{1,0:T(8,128)S(1)}, u32[]{:S(2)}, u32[]{:S(2)}) collective-permute-start(f32[64,128]{1,0:T(8,128)S(1)} %get-tuple-element.30.zown_ref), channel_id=1, source_target_pairs={{0,1},{1,0},{2,3},{3,2},{4,5},{5,4},{6,7},{7,6},{8,9},{9,8},{10,11... | collective-permute-start | bytes 98312 | tf_op jit(solution)/shard_map/ppermute | solution.py:456
  23.9 0.7 %copy-start.4 = (s32[4,256]{1,0:T(4,128)S(1)}, s32[4,256]{1,0:T(4,128)}, u32[]{:S(2)}) copy-start(s32[4,256]{1,0:T(4,128)} %idx_ref.1) | copy-start | bytes 12292
  24.0 0.7 %copy-start.5 = (f32[6]{0:T(128)S(1)}, f32[6]{0:T(128)}, u32[]{:S(2)}) copy-start(f32[6]{0:T(128)} %light_ref.3) | copy-start | bytes 76
  24.0 0.7 %copy-start.6 = (f32[256]{0:T(256)S(1)}, f32[256]{0:T(256)}, u32[]{:S(2)}) copy-start(f32[256]{0:T(256)} %param.18) | copy-start | bytes 3076
  28.2 0.7 %copy-start.7 = (s32[1,1,1,4]{3,2,1,0:T(1,128)S(1)}, s32[1,1,1,4]{3,2,1,0:T(1,128)}, u32[]{:S(2)}) copy-start(s32[1,1,1,4]{3,2,1,0:T(1,128)} %param.21) | copy-start | bytes 52
  30.5 0.7 %copy-start.1 = (f32[3,4,4,128]{3,2,1,0:T(4,128)S(1)}, f32[3,4,4,128]{3,2,1,0:T(4,128)}, u32[]{:S(2)}) copy-start(f32[3,4,4,128]{3,2,1,0:T(4,128)} %param.13) | copy-start | bytes 73732
  36.7 10.0 %collective-permute-start.9 = (f32[1040,128]{1,0:T(8,128)S(1)}, f32[1040,128]{1,0:T(8,128)S(1)}, u32[]{:S(2)}, u32[]{:S(2)}) collective-permute-start(f32[1040,128]{1,0:T(8,128)S(1)} %get-tuple-element.47.n_ref), channel_id=1, source_target_pairs={{0,64},{64,0},{1,65},{65,1},{2,66},{66,2},{3,67},{67,3},{4,68},{68... | collective-permute-start | bytes 1597448 | tf_op jit(solution)/shard_map/ppermute | solution.py:498
  36.8 17.6 %collective-permute-start.10 = (f32[520,128]{1,0:T(8,128)S(1)}, f32[520,128]{1,0:T(8,128)S(1)}, u32[]{:S(2)}, u32[]{:S(2)}) collective-permute-start(f32[520,128]{1,0:T(8,128)S(1)} %get-tuple-element.48), channel_id=1, source_target_pairs={{0,2},{2,4},{4,6},{6,8},{8,10},{10,12},{12,14},{14,16},{16,18},{18... | collective-permute-start | bytes 798728 | tf_op jit(solution)/shard_map/ppermute | solution.py:496
  39.3 15.1 %collective-permute-start.11 = (f32[520,128]{1,0:T(8,128)S(1)}, f32[520,128]{1,0:T(8,128)S(1)}, u32[]{:S(2)}, u32[]{:S(2)}) collective-permute-start(f32[520,128]{1,0:T(8,128)S(1)} %get-tuple-element.49), channel_id=1, source_target_pairs={{0,62},{2,0},{4,2},{6,4},{8,6},{10,8},{12,10},{14,12},{16,14},{18,... | collective-permute-start | bytes 798728 | tf_op jit(solution)/shard_map/ppermute | solution.py:497
  44.7 9.8 %collective-permute-start.12 = (f32[80,128]{1,0:T(8,128)S(1)}, f32[80,128]{1,0:T(8,128)S(1)}, u32[]{:S(2)}, u32[]{:S(2)}) collective-permute-start(f32[80,128]{1,0:T(8,128)S(1)} %get-tuple-element.50.zs_ref), channel_id=1, source_target_pairs={{0,1},{1,0},{2,3},{3,2},{4,5},{5,4},{6,7},{7,6},{8,9},{9,8},{10,11... | collective-permute-start | bytes 122888 | tf_op jit(solution)/shard_map/ppermute | solution.py:499

commit v6 on v5

--- a/solution.py
+++ b/solution.py
@@ -192,8 +192,7 @@
     n2_ref, temp_ref, v_ref, ty_ref, below_ref, plane_ref, flip_ref, turn_ref, both_ref, pe_ref,
     ost_ref, g2_ref, pg_ref, cb_ref,
     made_ref, lost_ref, heat_ref, den_ref, na_ref, yl_ref, yu_ref,
-    n_out, temp_out, up_out, dn_out, z_out,
-    ph_ref, cur_ref, curt_ref,
+    up_out, temp_out, ph_ref, cur_ref, curt_ref,
 ):
     near_z, far_z = later(8, 2, 1), later(8, 4, 2)
     ost = ost_ref[...]
@@ -208,29 +207,7 @@
             t = i * 4 + j
             ph_ref[t] = pe_ref[t] + (yl_ref[t] * far[:, :LANES] + yu_ref[t] * far[:, LANES:])
 
-    pgp = wide([pg_ref[:, 0:128], pg_ref[:, 256:384]])
-
-    def quiet(c, carry):
-        base = c * 4
-        for p in range(2):
-            a = base + 2 * p
-            ph = wide([ph_ref[a], ph_ref[a + 1]])
-            na = wide([na_ref[a], na_ref[a + 1]])
-            made = dot(pgp, jnp.concatenate(split(ph * na), axis=0))
-            heat = made[64:65] + made[65:66]
-            for q in range(2):
-                cut = slice(q * LANES, (q + 1) * LANES)
-                n = n2_ref[a + q]
-                n_out[pl.ds(pl.multiple_of((a + q) * KINDS, KINDS), KINDS), :] = (
-                    n * (n + (made_ref[a + q] + made[:64, cut]))
-                ) / (lost_ref[a + q] * n + made[80:, cut])
-                row = pl.ds(a + q, 1)
-                temp_out[row, :] = (temp_ref[row, :] + (heat_ref[row, :] + heat[:, cut])) / (
-                    den_ref[row, :]
-                )
-        return carry
-
-    lax.fori_loop(0, 4, quiet, 0)
+    quiet_half(2, n2_ref, temp_ref, ph_ref, pg_ref, made_ref, lost_ref, heat_ref, den_ref, na_ref, up_out, temp_out)
 
     listed = [listed_ref[m, 0] for m in range(MAXD)]
     pick = [jnp.minimum(listed[m], TILES - 1) for m in range(MAXD)]
@@ -269,33 +246,84 @@
             curt_ref[b : b + 1, :] = new_t[q][:, LANES:]
         return carry
 
-    lax.fori_loop(0, NSUB, substep, 0)
-
+    lax.fori_loop(0, NSUB, substep, 0, unroll=2)
+
+    place(2, listed, cur_ref, curt_ref, up_out, temp_out)
+    for i in range(4):
+        up_out[pl.ds(512 + i, 1), :] = v_ref[pl.ds(TILES + i * 4 + 3, 1), :]
+    velocities(2, v_ref, up_out)
+
+
+def quiet_half(first, n2_ref, temp_ref, ph_ref, pg_ref, made_ref, lost_ref, heat_ref, den_ref, na_ref, out_ref, temp_out):
+    pgp = wide([pg_ref[:, 0:128], pg_ref[:, 256:384]])
+
+    def two(c, carry):
+        for p in range(2):
+            i = 2 * c + p
+            a = i * 4 + first
+            rate = wide([ph_ref[a] * na_ref[a], ph_ref[a + 1] * na_ref[a + 1]])
+            made = dot(pgp, jnp.concatenate(split(rate), axis=0))
+            heat = made[64:65] + made[65:66]
+            for q in range(2):
+                cut = slice(q * LANES, (q + 1) * LANES)
+                n = n2_ref[a + q]
+                out_ref[pl.ds(pl.multiple_of((q * 4 + i) * KINDS, KINDS), KINDS), :] = (
+                    n * (n + (made_ref[a + q] + made[:64, cut]))
+                ) / (lost_ref[a + q] * n + made[80:, cut])
+                row = pl.ds(a + q, 1)
+                temp_out[row, :] = (temp_ref[row, :] + (heat_ref[row, :] + heat[:, cut])) / (
+                    den_ref[row, :]
+                )
+        return carry
+
+    lax.fori_loop(0, 2, two, 0)
+
+
+def place(first, listed, cur_ref, curt_ref, out_ref, temp_out):
     for m in range(MAXD):
-
-        @pl.when(listed[m] < TILES)
+        column = lax.rem(listed[m], 4)
+        here = jnp.logical_and(column >= first, column < first + 2)
+
+        @pl.when(jnp.logical_and(listed[m] < TILES, here))
         def _():
-            n_out[pl.ds(pl.multiple_of(pick[m] * KINDS, KINDS), KINDS), :] = cur_ref[m]
-            temp_out[pl.ds(pick[m], 1), :] = curt_ref[m : m + 1, :]
-
+            slot = (column - first) * 4 + lax.div(listed[m], 4)
+            out_ref[pl.ds(pl.multiple_of(slot * KINDS, KINDS), KINDS), :] = cur_ref[m]
+            temp_out[pl.ds(listed[m], 1), :] = curt_ref[m : m + 1, :]
+
+
+def velocities(first, v_ref, out_ref):
+    out_ref[pl.ds(516, 4), :] = jnp.zeros((4, LANES), F32)
+    for q in range(2):
+        for i in range(4):
+            t = i * 4 + first + q
+            out_ref[pl.ds(520 + q * 4 + i, 1), :] = v_ref[pl.ds(t, 1), :]
+
+
+def lower_kernel(
+    listed_ref, n2_ref, temp_ref, v_ref, ph_ref, pg_ref,
+    made_ref, lost_ref, heat_ref, den_ref, na_ref, cur_ref, curt_ref, up_ref, half_ref,
+    temp_out, dn_out, z_out,
+):
+    temp_out[...] = half_ref[...]
+    quiet_half(0, n2_ref, temp_ref, ph_ref, pg_ref, made_ref, lost_ref, heat_ref, den_ref, na_ref, dn_out, temp_out)
+    listed = [listed_ref[m, 0] for m in range(MAXD)]
+    place(0, listed, cur_ref, curt_ref, dn_out, temp_out)
+    for i in range(4):
+        dn_out[pl.ds(512 + i, 1), :] = v_ref[pl.ds(TILES + i * 4, 1), :]
+    velocities(0, v_ref, dn_out)
     lane = lax.broadcasted_iota(jnp.int32, (KINDS, LANES), 1)
     zp = jnp.zeros((KINDS, LANES), F32)
-    up_out[pl.ds(512, 8), :] = jnp.zeros((8, LANES), F32)
-    dn_out[pl.ds(512, 8), :] = jnp.zeros((8, LANES), F32)
     for i in range(4):
         for j in range(4):
             t = i * 4 + j
-            u = n_out[pl.ds(t * KINDS, KINDS), :]
+            u = (dn_out, up_ref)[j // 2][pl.ds((j % 2 * 4 + i) * KINDS, KINDS), :]
             zp = jnp.where(lane // 8 == t, pltpu.roll(u, (8 * t + 4) % LANES, 1), zp)
-            if j < 2:
-                dn_out[pl.ds((j * 4 + i) * KINDS, KINDS), :] = u
-            else:
-                up_out[pl.ds(((j - 2) * 4 + i) * KINDS, KINDS), :] = u
-        up_out[pl.ds(512 + i, 1), :] = v_ref[pl.ds(TILES + i * 4 + 3, 1), :]
-        dn_out[pl.ds(512 + i, 1), :] = v_ref[pl.ds(TILES + i * 4, 1), :]
     z_out[pl.ds(0, KINDS), :] = zp
-    n_out[pl.ds(1024, TILES), :] = v_ref[pl.ds(0, TILES), :]
     z_out[pl.ds(KINDS, TILES), :] = v_ref[pl.ds(2 * TILES, TILES), :]
+
+
+def cells(halves, i, j):
+    return halves[j // 2][pl.ds((j % 2 * 4 + i) * KINDS, KINDS), :]
 
 
 def flux(face, um1, u, up1, up2):
@@ -303,20 +331,20 @@
     return face * state
 
 
-def inner_kernel(n_ref, v_ref, hx_ref, acc_ref):
+def inner_kernel(dn_ref, up_ref, v_ref, xdn_ref, xup_ref, acc_ref):
     lane = lax.broadcasted_iota(jnp.int32, (KINDS, LANES), 1)
     edge = jnp.logical_or(lane < 2, lane >= LANES - 2)
 
     def x_u(i, j):
         if 0 <= i < 4:
-            return n_ref[pl.ds((i * 4 + j) * KINDS, KINDS), :]
-        return hx_ref[pl.ds(((i % 4) * 4 + j) * KINDS, KINDS), :]
+            return cells((dn_ref, up_ref), i, j)
+        return cells((xdn_ref, xup_ref), i % 4, j)
 
     def x_v(i, j):
         if 0 <= i < 4:
             return v_ref[i * 4 + j : i * 4 + j + 1, :]
-        r = 1024 + (i % 4) * 4 + j
-        return hx_ref[r : r + 1, :]
+        r = 520 + j % 2 * 4 + i % 4
+        return (xdn_ref, xup_ref)[j // 2][r : r + 1, :]
 
     def x_flux(i, j):
         face = 0.5 * (x_v(i, j) + x_v(i + 1, j))
@@ -326,7 +354,7 @@
     for i in range(4):
         for j in range(4):
             t = i * 4 + j
-            u = n_ref[pl.ds(t * KINDS, KINDS), :]
+            u = cells((dn_ref, up_ref), i, j)
             top = x_flux(i, j)
             change = top - xf[j]
             xf[j] = top
@@ -343,7 +371,7 @@
             acc_ref[t] = u - 0.25 * change
 
 
-def outer_kernel(n_ref, acc_ref, v_ref, lo_ref, hi_ref, zs_ref, hz_ref, out_ref):
+def outer_kernel(dn_ref, up_ref, acc_ref, v_ref, lo_ref, hi_ref, zs_ref, hz_ref, out_ref):
     lane = lax.broadcasted_iota(jnp.int32, (KINDS, LANES), 1)
     lane1 = lax.broadcasted_iota(jnp.int32, (1, LANES), 1)
     edge = jnp.logical_or(lane < 2, lane >= LANES - 2)
@@ -376,7 +404,7 @@
             return lo_ref[pl.ds(((j + 2) * 4 + i) * KINDS, KINDS), :]
         if j > 3:
             return hi_ref[pl.ds(((j - 4) * 4 + i) * KINDS, KINDS), :]
-        return n_ref[pl.ds((i * 4 + j) * KINDS, KINDS), :]
+        return cells((dn_ref, up_ref), i, j)
 
     def y_v(i, j):
         if j < 0:
@@ -479,28 +507,30 @@
         early_kernel, (vm(*big), vm(8, LANES, dtype=jnp.int32)), [illumination, listed],
         [n2, zc, xown, xpay, zown, zpay, ost],
     )
-    n_new, temp_new, up, dn, zs = call(
+    up, half, ph, cur, curt = call(
         chemistry_kernel,
-        (vm(1040, LANES), vm(TILES, LANES), vm(520, LANES), vm(520, LANES), vm(80, LANES)),
+        (vm(528, LANES), vm(TILES, LANES), vm(*big), vm(MAXD, KINDS, LANES), vm(8, LANES)),
         [],
         [
             tiles, n2, temp, v, ty, below, plane, *z_parts, pe, ost, g2, pg, cb,
             made, lost, heat, den, na, yl, yu,
         ],
-        [
-            pltpu.VMEM(big, F32),
-            pltpu.VMEM((MAXD, KINDS, LANES), F32), pltpu.VMEM((8, LANES), F32),
-        ],
-    )
-
+    )
     low = near(lax.ppermute(up, "gy", around(size, 1)))
+    temp_new, dn, zs = call(
+        lower_kernel,
+        (vm(TILES, LANES), vm(528, LANES), vm(80, LANES)),
+        [],
+        [tiles, n2, temp, v, ph, pg, made, lost, heat, den, na, cur, curt, up, half],
+    )
     high = near(lax.ppermute(dn, "gy", around(size, -1)))
-    hx = near(lax.ppermute(n_new, "gx", around(lax.axis_size("gx"), 1)))
     hz = near(lax.ppermute(zs, "gz", around(lax.axis_size("gz"), 1)))
-    acc = call(inner_kernel, vm(*mid), [], [n_new, v, hx])
+    xdn = near(lax.ppermute(dn, "gx", around(lax.axis_size("gx"), 1)))
+    xup = near(lax.ppermute(up, "gx", around(lax.axis_size("gx"), 1)))
+    acc = call(inner_kernel, vm(*mid), [], [dn, up, v, xdn, xup])
     out = call(
         outer_kernel, hbm(KINDS * TILES, LANES), [],
-        [n_new, acc, v, low, high, zs, hz],
+        [dn, up, acc, v, low, high, zs, hz],
     )
     return out.reshape(KINDS, 4, 4, LANES), temp_new.reshape(4, 4, LANES)
 

time: 56.8 us -> 61.1 us (1.076)
  waiting for transfers between devices: 16.1 us -> 20.9 us
  starting transfers between devices: 21.4 us -> 20.6 us
    ppermute x1, waiting for transfers between devices: 6.24 us -> 11.1 us  [shards(): hz = near(lax.ppermute(zs, 'gz', around(lax.axis_size('gz'), 1)))]
    ppermute x1, starting transfers between devices: 2.49 us -> 0.01 us  [shards(): low = near(lax.ppermute(up, 'gy', around(size, 1)))]
    ppermute x1, starting transfers between devices: 5.33 us -> 6.17 us  [shards(): high = near(lax.ppermute(dn, 'gy', around(size, -1)))]
    pallas_call x8 -> x9, Pallas kernels: 13.9 us -> 14 us  [call(): pl.pallas_call(kernel, out_shape=out_shape, in_specs=[SM] * len(scalars)...]
  transfers between devices with their start and end apart: 13 -> 14, of which waited for: 5 -> 5; matrix products, arithmetic and copies ran while one was open for 1% -> 1% of each run, Pallas kernels for 12% -> 11%
where the time goes in v6:
time: 61.1 us; the launch traced here: 60 us
  waiting for transfers between devices  20.9 us (34%)
  starting transfers between devices  20.6 us (34%)
  Pallas kernels  14 us (23%)
  local copies, waits for them, and re-layouts  3.67 us (6%)
  between operations  0.81 us (1%)
    pallas_call x9, Pallas kernels, call(): pl.pallas_call(kernel, out_shape=out_shape, in_specs=[SM] * len(scalars)...  14 us
    ppermute x7, starting transfers between devices, send(): return near(lax.ppermute(value, 'gy', [(a, to(a)) for a in range(size)]))  11.5 us
    ppermute x1, waiting for transfers between devices, shards(): hz = near(lax.ppermute(zs, 'gz', around(lax.axis_size('gz'), 1)))  11.1 us
    ppermute x7, waiting for transfers between devices, send(): return near(lax.ppermute(value, 'gy', [(a, to(a)) for a in range(size)]))  9.84 us
    ppermute x1, starting transfers between devices, shards(): high = near(lax.ppermute(dn, 'gy', around(size, -1)))  6.17 us
    unnamed x23, local copies, waits for them, and re-layouts  3.67 us
    ppermute x1, starting transfers between devices, shards(): hz = near(lax.ppermute(zs, 'gz', around(lax.axis_size('gz'), 1)))  1.8 us
  transfers between devices with their start and end apart: 14, of which 5 were waited for; matrix products, arithmetic and copies ran while one was open for 1% of the time, Pallas kernels for 11%

profile of v6, /device:TPU:2, one launch (start us, length us, event | category | flops | bytes accessed | tf_op | source)
XLA Modules:
  0.0 60.0 jit_solution(1042578523137729214)
XLA Ops:
  0.6 1.0 %copy-done = f32[64,4,4,128]{3,2,1,0:T(4,128)S(1)} copy-done((f32[64,4,4,128]{3,2,1,0:T(4,128)S(1)}, f32[64,4,4,128]{3,2,1,0:T(4,128)}, u32[]{:S(2)}) %copy-start) | copy-done | bytes 524312
  1.7 0.3 shard_map.122
  2.0 2.2 %collective-permute-start.2 = (f32[256,128]{1,0:T(8,128)S(1)}, f32[256,128]{1,0:T(8,128)S(1)}, u32[]{:S(2)}, u32[]{:S(2)}) collective-permute-start(f32[256,128]{1,0:T(8,128)S(1)} %get-tuple-element.36.own_ref.ty_ref), channel_id=1, source_target_pairs={{0,2},{2,0},{4,6},{6,4},{8,10},{10,8},{12,14},{14,12},{16,18},{18,... | collective-permute-start | bytes 393224 | tf_op jit(solution)/shard_map/ppermute | solution.py:476
  4.2 4.6 %collective-permute-done.2.other_ref = f32[256,128]{1,0:T(8,128)S(1)} collective-permute-done((f32[256,128]{1,0:T(8,128)S(1)}, f32[256,128]{1,0:T(8,128)S(1)}, u32[]{:S(2)}, u32[]{:S(2)}) %collective-permute-start.2) | collective-permute-done | bytes 131104 | tf_op jit(solution)/shard_map/ppermute | solution.py:476
  8.8 3.3 %collective-permute-start.5 = (f32[256,128]{1,0:T(8,128)S(1)}, f32[256,128]{1,0:T(8,128)S(1)}, u32[]{:S(2)}, u32[]{:S(2)}) collective-permute-start(f32[256,128]{1,0:T(8,128)S(1)} %shard_map.125.pair_ref), channel_id=1, source_target_pairs={{0,8},{2,10},{4,12},{6,14},{8,0},{10,2},{12,4},{14,6},{16,24},{18,... | collective-permute-start | bytes 393224 | tf_op jit(solution)/shard_map/ppermute | solution.py:476
  12.1 1.1 %collective-permute-start.4 = (f32[256,128]{1,0:T(8,128)S(1)}, f32[256,128]{1,0:T(8,128)S(1)}, u32[]{:S(2)}, u32[]{:S(2)}) collective-permute-start(f32[256,128]{1,0:T(8,128)S(1)} %shard_map.125.pair_ref), channel_id=1, source_target_pairs={{0,12},{2,14},{4,8},{6,10},{8,4},{10,6},{12,0},{14,2},{16,28},{18,... | collective-permute-start | bytes 393224 | tf_op jit(solution)/shard_map/ppermute | solution.py:476
  13.1 2.3 %collective-permute-done.5.both_ref = f32[256,128]{1,0:T(8,128)S(1)} collective-permute-done((f32[256,128]{1,0:T(8,128)S(1)}, f32[256,128]{1,0:T(8,128)S(1)}, u32[]{:S(2)}, u32[]{:S(2)}) %collective-permute-start.5) | collective-permute-done | bytes 131104 | tf_op jit(solution)/shard_map/ppermute | solution.py:476
  15.4 2.8 %collective-permute-done.4.turn_ref = f32[256,128]{1,0:T(8,128)S(1)} collective-permute-done((f32[256,128]{1,0:T(8,128)S(1)}, f32[256,128]{1,0:T(8,128)S(1)}, u32[]{:S(2)}, u32[]{:S(2)}) %collective-permute-start.4) | collective-permute-done | bytes 131104 | tf_op jit(solution)/shard_map/ppermute | solution.py:476
  18.2 0.1 collective-permute-done.3.flip_ref
  18.4 0.1 shard_map.126
  18.4 4.0 %collective-permute-start.8 = (f32[256,128]{1,0:T(8,128)S(1)}, f32[256,128]{1,0:T(8,128)S(1)}, u32[]{:S(2)}, u32[]{:S(2)}) collective-permute-start(f32[256,128]{1,0:T(8,128)S(1)} %get-tuple-element.38.plane_ref), channel_id=1, source_target_pairs={{0,32},{2,34},{4,36},{6,38},{8,40},{10,42},{12,44},{14,46},{16,48}... | collective-permute-start | bytes 393224 | tf_op jit(solution)/shard_map/ppermute | solution.py:476
  22.4 0.7 %collective-permute-start.7 = (f32[256,128]{1,0:T(8,128)S(1)}, f32[256,128]{1,0:T(8,128)S(1)}, u32[]{:S(2)}, u32[]{:S(2)}) collective-permute-start(f32[256,128]{1,0:T(8,128)S(1)} %get-tuple-element.38.plane_ref), channel_id=1, source_target_pairs={{0,48},{2,50},{4,52},{6,54},{8,56},{10,58},{12,60},{14,62},{16,32}... | collective-permute-start | bytes 393224 | tf_op jit(solution)/shard_map/ppermute | solution.py:476
  23.1 0.3 collective-permute-start.6
  23.4 0.5 collective-permute-start.1
  24.0 0.6 %copy-done.4 = s32[4,256]{1,0:T(4,128)S(1)} copy-done((s32[4,256]{1,0:T(4,128)S(1)}, s32[4,256]{1,0:T(4,128)}, u32[]{:S(2)}) %copy-start.4) | copy-done | bytes 4120
  24.6 0.0 copy-done.6
  24.7 3.5 %shard_map.123 = (bf16[128,192]{1,0:T(8,128)(2,1)S(1)}, bf16[384,128]{1,0:T(8,128)(2,1)S(1)}, bf16[144,512]{1,0:T(8,128)(2,1)S(1)}, f32[320,128]{1,0:T(8,128)S(1...) custom-call(f32[6]{0:T(128)S(1)} %copy-done.5, ...), custom_call_target="tpu_custom_call" | custom-call | tf_op jit(solution)/shard_map/pallas_call | solution.py:447
  28.2 0.0 copy-start.7
  28.2 0.6 %copy-done.7 = s32[1,1,1,4]{3,2,1,0:T(1,128)S(1)} copy-done((s32[1,1,1,4]{3,2,1,0:T(1,128)S(1)}, s32[1,1,1,4]{3,2,1,0:T(1,128)}, u32[]{:S(2)}) %copy-start.7) | copy-done | bytes 40
  28.8 1.7 %shard_map.124 = (f32[16,128,128]{2,1,0:T(8,128)S(1)}, s32[8,128]{1,0:T(8,128)S(1)}) custom-call(f32[6]{0:T(128)S(1)} %copy-done.5, s32[4]{0:T(128)S(1)} %bitcast.22, f32[16,64,128]{2,1,0:T(8,128)S(1)} %get-tuple-element.30.n2_ref, f32[1024,128]{1,0:T(8,128)S(1)} %get-tuple-element.31.zc_ref, f32[256,128]{1,0:T(8,128)S(1)} %get-tuple-element.32.xown_ref, ...), custom_call_target="tpu_custom_call" | custom-call | tf_op jit(solution)/shard_map/pallas_call | solution.py:447
  30.5 0.0 copy-start.1
  30.6 0.7 %copy-done.1 = f32[3,4,4,128]{3,2,1,0:T(4,128)S(1)} copy-done((f32[3,4,4,128]{3,2,1,0:T(4,128)S(1)}, f32[3,4,4,128]{3,2,1,0:T(4,128)}, u32[]{:S(2)}) %copy-start.1) | copy-done | bytes 24600
  31.3 4.8 %shard_map.127 = (f32[528,128]{1,0:T(8,128)S(1)}, f32[16,128]{1,0:T(8,128)S(1)}, f32[16,128,128]{2,1,0:T(8,128)S(1)}, f32[4,64,128]{2,1,0:T(8,128)S(1)}, f32[8,128]{1,0:T(8,128)S(1)}) custom-call(s32[8,128]{1,0:T(8,128)S(1)} %get-tuple-element.35.listed_ref, f32[16,64,128]{2,1,0:T(8,128)S(1)} %get-tuple-element.30.n2_ref, f32[16,128]{1,0:T(8,128)S(1)} %bitcast.18, ...), custom_call_target="tpu_custom_call" | custom-call | tf_op jit(solution)/shard_map/pallas_call | solution.py:447
  36.1 0.7 %shard_map.128 = (f32[16,128]{1,0:T(8,128)S(1)}, f32[528,128]{1,0:T(8,128)S(1)}, f32[80,128]{1,0:T(8,128)S(1)}) custom-call(s32[8,128]{1,0:T(8,128)S(1)} %get-tuple-element.35.listed_ref, f32[16,64,128]{2,1,0:T(8,128)S(1)} %get-tuple-element.30.n2_ref, f32[16,128]{1,0:T(8,128)S(1)} %bitcast.19, f32[48,128]{1,0:T(8,128)S(1)} %bitcast.14, ...), custom_call_target="tpu_custom_call" | custom-call | tf_op jit(solution)/shard_map/pallas_call | solution.py:447
  36.8 0.1 collective-permute-start.9
  36.9 0.5 collective-permute-start.10
  37.4 6.2 %collective-permute-start.12 = (f32[528,128]{1,0:T(8,128)S(1)}, f32[528,128]{1,0:T(8,128)S(1)}, u32[]{:S(2)}, u32[]{:S(2)}) collective-permute-start(f32[528,128]{1,0:T(8,128)S(1)} %get-tuple-element.55.dn_ref), channel_id=1, source_target_pairs={{0,62},{2,0},{4,2},{6,4},{8,6},{10,8},{12,10},{14,12},{16,14},{18,... | collective-permute-start | bytes 811016 | tf_op jit(solution)/shard_map/ppermute | solution.py:526
  43.6 1.8 %collective-permute-start.13 = (f32[80,128]{1,0:T(8,128)S(1)}, f32[80,128]{1,0:T(8,128)S(1)}, u32[]{:S(2)}, u32[]{:S(2)}) collective-permute-start(f32[80,128]{1,0:T(8,128)S(1)} %get-tuple-element.56.zs_ref), channel_id=1, source_target_pairs={{0,1},{1,0},{2,3},{3,2},{4,5},{5,4},{6,7},{7,6},{8,9},{9,8},{10,11... | collective-permute-start | bytes 122888 | tf_op jit(solution)/shard_map/ppermute | solution.py:527
  45.4 0.6 copy.13
  46.0 1.4 %shard_map.129.acc_ref = f32[16,64,128]{2,1,0:T(8,128)S(1)} custom-call(f32[528,128]{1,0:T(8,128)S(1)} %get-tuple-element.55.dn_ref, f32[528,128]{1,0:T(8,128)S(1)} %get-tuple-element.53.up_ref, f32[48,128]{1,0:T(8,128)S(1)} %bitcast.15, f32[528,128]{1,0:T(8,128)S(1)} %collective-permute-done.9.xdn_ref, f32[528,128]{1,0:T(8,128)S(1)} %collective-permute-done.10.xup_ref), custom_call_target="tpu_custom_call" | custom-call | tf_op jit(solution)/shard_map/pallas_call | solution.py:447
  47.4 11.1 %collective-permute-done.13.hz_ref = f32[80,128]{1,0:T(8,128)S(1)} collective-permute-done((f32[80,128]{1,0:T(8,128)S(1)}, f32[80,128]{1,0:T(8,128)S(1)}, u32[]{:S(2)}, u32[]{:S(2)}) %collective-permute-start.13) | collective-permute-done | bytes 40992 | tf_op jit(solution)/shard_map/ppermute | solution.py:527
  58.5 1.5 %shard_map.130 = f32[1024,128]{1,0:T(8,128)} custom-call(f32[528,128]{1,0:T(8,128)S(1)} %get-tuple-element.55.dn_ref, f32[528,128]{1,0:T(8,128)S(1)} %get-tuple-element.53.up_ref, f32[16,64,128]{2,1,0:T(8,128)S(1)} %shard_map.129.acc_ref, f32[48,128]{1,0:T(8,128)S(1)} %bitcast.16, f32[528,128]{1,0:T(8,128)S(1)} %collective-permute-done.11.lo_ref, ...), custom_call_target="tpu_custom_call" | custom-call | tf_op jit(solution)/shard_map/pallas_call | solution.py:447
  (28 shorter events, 0.1 us)
Async XLA Ops:
  0.6 1.0 %copy-start = (f32[64,4,4,128]{3,2,1,0:T(4,128)S(1)}, f32[64,4,4,128]{3,2,1,0:T(4,128)}, u32[]{:S(2)}) copy-start(f32[64,4,4,128]{3,2,1,0:T(4,128)} %param.11) | copy-start | bytes 1572868
  2.0 6.8 %collective-permute-start.2 = (f32[256,128]{1,0:T(8,128)S(1)}, f32[256,128]{1,0:T(8,128)S(1)}, u32[]{:S(2)}, u32[]{:S(2)}) collective-permute-start(f32[256,128]{1,0:T(8,128)S(1)} %get-tuple-element.36.own_ref.ty_ref), channel_id=1, source_target_pairs={{0,2},{2,0},{4,6},{6,4},{8,10},{10,8},{12,14},{14,12},{16,18},{18,... | collective-permute-start | bytes 393224 | tf_op jit(solution)/shard_map/ppermute | solution.py:476
  8.8 6.6 %collective-permute-start.5 = (f32[256,128]{1,0:T(8,128)S(1)}, f32[256,128]{1,0:T(8,128)S(1)}, u32[]{:S(2)}, u32[]{:S(2)}) collective-permute-start(f32[256,128]{1,0:T(8,128)S(1)} %shard_map.125.pair_ref), channel_id=1, source_target_pairs={{0,8},{2,10},{4,12},{6,14},{8,0},{10,2},{12,4},{14,6},{16,24},{18,... | collective-permute-start | bytes 393224 | tf_op jit(solution)/shard_map/ppermute | solution.py:476
  12.1 6.2 %collective-permute-start.4 = (f32[256,128]{1,0:T(8,128)S(1)}, f32[256,128]{1,0:T(8,128)S(1)}, u32[]{:S(2)}, u32[]{:S(2)}) collective-permute-start(f32[256,128]{1,0:T(8,128)S(1)} %shard_map.125.pair_ref), channel_id=1, source_target_pairs={{0,12},{2,14},{4,8},{6,10},{8,4},{10,6},{12,0},{14,2},{16,28},{18,... | collective-permute-start | bytes 393224 | tf_op jit(solution)/shard_map/ppermute | solution.py:476
  13.1 5.2 %collective-permute-start.3 = (f32[256,128]{1,0:T(8,128)S(1)}, f32[256,128]{1,0:T(8,128)S(1)}, u32[]{:S(2)}, u32[]{:S(2)}) collective-permute-start(f32[256,128]{1,0:T(8,128)S(1)} %shard_map.125.pair_ref), channel_id=1, source_target_pairs={{0,4},{2,6},{4,0},{6,2},{8,12},{10,14},{12,8},{14,10},{16,20},{18,... | collective-permute-start | bytes 393224 | tf_op jit(solution)/shard_map/ppermute | solution.py:476
  13.1 15.0 %collective-permute-start = (f32[256,128]{1,0:T(8,128)S(1)}, f32[256,128]{1,0:T(8,128)S(1)}, u32[]{:S(2)}, u32[]{:S(2)}) collective-permute-start(f32[256,128]{1,0:T(8,128)S(1)} %get-tuple-element.32.xown_ref), channel_id=1, source_target_pairs={{0,64},{64,0},{1,65},{65,1},{2,66},{66,2},{3,67},{67,3},{4,68},{68... | collective-permute-start | bytes 393224 | tf_op jit(solution)/shard_map/ppermute | solution.py:483
  18.3 5.6 %copy-start.3 = (f32[128,64]{0,1:T(8,128)S(1)}, f32[128,64]{0,1:T(8,128)}, u32[]{:S(2)}) copy-start(f32[128,64]{0,1:T(8,128)} %param.14) | copy-start | bytes 98308
  18.3 5.6 %copy-start.8 = (f32[128]{0:T(128)S(1)}, f32[128]{0:T(128)}, u32[]{:S(2)}) copy-start(f32[128]{0:T(128)} %param.16) | copy-start | bytes 1540
  18.4 5.6 %copy-start.9 = (f32[128]{0:T(128)S(1)}, f32[128]{0:T(128)}, u32[]{:S(2)}) copy-start(f32[128]{0:T(128)} %param.17) | copy-start | bytes 1540
  18.4 5.6 %copy-start.10 = (f32[64]{0:T(128)S(1)}, f32[64]{0:T(128)}, u32[]{:S(2)}) copy-start(f32[64]{0:T(128)} %param.19) | copy-start | bytes 772
  18.4 5.6 %copy-start.2 = (f32[4,4,128]{2,1,0:T(4,128)S(1)}, f32[4,4,128]{2,1,0:T(4,128)}, u32[]{:S(2)}) copy-start(f32[4,4,128]{2,1,0:T(4,128)} %param.12) | copy-start | bytes 24580
  18.4 12.1 %collective-permute-start.8 = (f32[256,128]{1,0:T(8,128)S(1)}, f32[256,128]{1,0:T(8,128)S(1)}, u32[]{:S(2)}, u32[]{:S(2)}) collective-permute-start(f32[256,128]{1,0:T(8,128)S(1)} %get-tuple-element.38.plane_ref), channel_id=1, source_target_pairs={{0,32},{2,34},{4,36},{6,38},{8,40},{10,42},{12,44},{14,46},{16,48}... | collective-permute-start | bytes 393224 | tf_op jit(solution)/shard_map/ppermute | solution.py:476
  22.4 8.1 %collective-permute-start.7 = (f32[256,128]{1,0:T(8,128)S(1)}, f32[256,128]{1,0:T(8,128)S(1)}, u32[]{:S(2)}, u32[]{:S(2)}) collective-permute-start(f32[256,128]{1,0:T(8,128)S(1)} %get-tuple-element.38.plane_ref), channel_id=1, source_target_pairs={{0,48},{2,50},{4,52},{6,54},{8,56},{10,58},{12,60},{14,62},{16,32}... | collective-permute-start | bytes 393224 | tf_op jit(solution)/shard_map/ppermute | solution.py:476
  23.1 7.4 %collective-permute-start.6 = (f32[256,128]{1,0:T(8,128)S(1)}, f32[256,128]{1,0:T(8,128)S(1)}, u32[]{:S(2)}, u32[]{:S(2)}) collective-permute-start(f32[256,128]{1,0:T(8,128)S(1)} %get-tuple-element.38.plane_ref), channel_id=1, source_target_pairs={{0,16},{2,18},{4,20},{6,22},{8,24},{10,26},{12,28},{14,30},{16,0},... | collective-permute-start | bytes 393224 | tf_op jit(solution)/shard_map/ppermute | solution.py:476
  23.4 4.7 %collective-permute-start.1 = (f32[64,128]{1,0:T(8,128)S(1)}, f32[64,128]{1,0:T(8,128)S(1)}, u32[]{:S(2)}, u32[]{:S(2)}) collective-permute-start(f32[64,128]{1,0:T(8,128)S(1)} %get-tuple-element.33.zown_ref), channel_id=1, source_target_pairs={{0,1},{1,0},{2,3},{3,2},{4,5},{5,4},{6,7},{7,6},{8,9},{9,8},{10,11... | collective-permute-start | bytes 98312 | tf_op jit(solution)/shard_map/ppermute | solution.py:484
  23.9 0.7 %copy-start.4 = (s32[4,256]{1,0:T(4,128)S(1)}, s32[4,256]{1,0:T(4,128)}, u32[]{:S(2)}) copy-start(s32[4,256]{1,0:T(4,128)} %idx_ref.1) | copy-start | bytes 12292
  23.9 0.7 %copy-start.5 = (f32[6]{0:T(128)S(1)}, f32[6]{0:T(128)}, u32[]{:S(2)}) copy-start(f32[6]{0:T(128)} %light_ref.3) | copy-start | bytes 76
  23.9 0.7 %copy-start.6 = (f32[256]{0:T(256)S(1)}, f32[256]{0:T(256)}, u32[]{:S(2)}) copy-start(f32[256]{0:T(256)} %param.18) | copy-start | bytes 3076
  28.2 0.7 %copy-start.7 = (s32[1,1,1,4]{3,2,1,0:T(1,128)S(1)}, s32[1,1,1,4]{3,2,1,0:T(1,128)}, u32[]{:S(2)}) copy-start(s32[1,1,1,4]{3,2,1,0:T(1,128)} %param.21) | copy-start | bytes 52
  30.5 0.7 %copy-start.1 = (f32[3,4,4,128]{3,2,1,0:T(4,128)S(1)}, f32[3,4,4,128]{3,2,1,0:T(4,128)}, u32[]{:S(2)}) copy-start(f32[3,4,4,128]{3,2,1,0:T(4,128)} %param.13) | copy-start | bytes 73732
  36.8 9.2 %collective-permute-start.9 = (f32[528,128]{1,0:T(8,128)S(1)}, f32[528,128]{1,0:T(8,128)S(1)}, u32[]{:S(2)}, u32[]{:S(2)}) collective-permute-start(f32[528,128]{1,0:T(8,128)S(1)} %get-tuple-element.55.dn_ref), channel_id=1, source_target_pairs={{0,64},{64,0},{1,65},{65,1},{2,66},{66,2},{3,67},{67,3},{4,68},{68... | collective-permute-start | bytes 811016 | tf_op jit(solution)/shard_map/ppermute | solution.py:528
  36.9 9.1 %collective-permute-start.10 = (f32[528,128]{1,0:T(8,128)S(1)}, f32[528,128]{1,0:T(8,128)S(1)}, u32[]{:S(2)}, u32[]{:S(2)}) collective-permute-start(f32[528,128]{1,0:T(8,128)S(1)} %get-tuple-element.53.up_ref), channel_id=1, source_target_pairs={{0,64},{64,0},{1,65},{65,1},{2,66},{66,2},{3,67},{67,3},{4,68},{68... | collective-permute-start | bytes 811016 | tf_op jit(solution)/shard_map/ppermute | solution.py:529
  37.4 21.1 %collective-permute-start.12 = (f32[528,128]{1,0:T(8,128)S(1)}, f32[528,128]{1,0:T(8,128)S(1)}, u32[]{:S(2)}, u32[]{:S(2)}) collective-permute-start(f32[528,128]{1,0:T(8,128)S(1)} %get-tuple-element.55.dn_ref), channel_id=1, source_target_pairs={{0,62},{2,0},{4,2},{6,4},{8,6},{10,8},{12,10},{14,12},{16,14},{18,... | collective-permute-start | bytes 811016 | tf_op jit(solution)/shard_map/ppermute | solution.py:526
  43.6 14.9 %collective-permute-start.11 = (f32[528,128]{1,0:T(8,128)S(1)}, f32[528,128]{1,0:T(8,128)S(1)}, u32[]{:S(2)}, u32[]{:S(2)}) collective-permute-start(f32[528,128]{1,0:T(8,128)S(1)} %get-tuple-element.53.up_ref), channel_id=1, source_target_pairs={{0,2},{2,4},{4,6},{6,8},{8,10},{10,12},{12,14},{14,16},{16,18},{18... | collective-permute-start | bytes 811016 | tf_op jit(solution)/shard_map/ppermute | solution.py:519
  43.6 14.9 %collective-permute-start.13 = (f32[80,128]{1,0:T(8,128)S(1)}, f32[80,128]{1,0:T(8,128)S(1)}, u32[]{:S(2)}, u32[]{:S(2)}) collective-permute-start(f32[80,128]{1,0:T(8,128)S(1)} %get-tuple-element.56.zs_ref), channel_id=1, source_target_pairs={{0,1},{1,0},{2,3},{3,2},{4,5},{5,4},{6,7},{7,6},{8,9},{9,8},{10,11... | collective-permute-start | bytes 122888 | tf_op jit(solution)/shard_map/ppermute | solution.py:527
